TPU v7x, 256 devices: a whole 4x4x8 slice. The times are simulated.
256 devices in a mesh: group: 16 (over z, core), dp: 16 (over x, y).
Axes of the slice: x: 4, y: 4, z: 8, core: 2. Of those that a mesh axis runs over, the one named last changes fastest.
Arguments:
- resp_q: bfloat16 [16, 4096, 4096], P('group', 'dp'), may hold values from -410 to 410
- resp_k: bfloat16 [16, 4096, 4096], P('group', 'dp'), may hold values from -410 to 410
- resp_v: bfloat16 [16, 4096, 4096], P('group', 'dp'), may hold values from -6 to 6
- prompt_k: bfloat16 [16, 2048, 4096], P('group', 'dp'), may hold values from -410 to 410
- prompt_v: bfloat16 [16, 2048, 4096], P('group', 'dp'), may hold values from -6 to 6
- prompt_len: int32 [16], P('group'), may hold values from 512 to 2048
- resp_len: int32 [16, 16], P('group', 'dp'), may hold values from 1 to 256, as said below
- assign: int32 [16, 32], P('group', 'dp'), may hold values from 0 to 63, as said below
- rewards: float32 [16, 16], P('group', 'dp'), may hold values from -18 to 18
- feat_q: bfloat16 [32, 128, 128], replicated, may hold values from -1 to 1
- feat_k: bfloat16 [32, 128, 128], replicated, may hold values from -1 to 1
Outputs:
- attn_out: bfloat16 [16, 2048, 4096], P('group', 'dp')
- token_adv: float32 [16, 2048], P('group', 'dp')
Inputs may be any that keep to these rules, and one draw needn't show every extreme that they name: Response r of a prompt has ceil(resp_len / 64) live blocks; these counts sum to 2 * 16 over a prompt's responses, and one response of every prompt has 4 blocks. `assign`: entry d * 2 + j names the block r * 4 + c (block c of response r) whose outputs go to slot j of device d of dp. Every live block of the prompt is named exactly once, and the 2 slots of one device name blocks of different responses.
All inputs are finite; a program needn't handle non-finite values.
Results may differ from a plain program's by a relative error of at most 0.0085.
Values may be sent and summed in bfloat16 or wider, within the bound.
No kernel may reach another device: no remote copies, remote signals or barrier semaphores. Data moves between devices by JAX's collectives and lax.ppermute only.
A program may use at most 128 MiB of HBM per device.

v0:
```python
import jax
import jax.numpy as jnp
from jax import lax
from jax.sharding import PartitionSpec as P

BLK = 64


def together(arrays, axis):
    ends = [0]
    for a in arrays:
        ends.append(ends[-1] + a.size)
    subtotal = lax.psum(jnp.concatenate([a.ravel() for a in arrays]), axis)
    return tuple((subtotal[b:e].reshape(a.shape) for a, b, e in zip(arrays, ends, ends[1:])))


def laid_out(tiles, dim):
    shape = list(tiles.shape[1:])
    shape[dim] *= tiles.shape[0]
    return jnp.moveaxis(tiles, 0, dim).reshape(shape)


def gather_together(arrays, axis, dims):
    ravelled = jnp.concatenate([a.reshape(-1) for a in arrays])
    lines, at, finished = (lax.all_gather(ravelled, axis), 0, [])
    for a, dim in zip(arrays, dims):
        tiles = lines[:, at : at + a.size].reshape(-1, *a.shape)
        finished.append(laid_out(tiles, dim))
        at += a.size
    return tuple(finished)


def features(rows, weights):
    logits = jnp.einsum("thd,hdf->thf", rows, weights, preferred_element_type=jnp.float32)
    return jnp.concatenate(
        [jax.nn.softmax(logits, axis=-1), jax.nn.softmax(-logits, axis=-1)], axis=-1
    ).astype(jnp.bfloat16)


def state_terms(query_feat, state_rounded, total_rounded):
    numerator = jnp.einsum(
        "thf,hfe->the", query_feat, state_rounded, preferred_element_type=jnp.float32
    )
    denominator = jnp.einsum(
        "thf,hf->th", query_feat, total_rounded, preferred_element_type=jnp.float32
    )
    return (numerator.astype(jnp.bfloat16), denominator.astype(jnp.bfloat16))


def body(
    resp_q,
    resp_k,
    resp_v,
    prompt_k,
    prompt_v,
    prompt_len,
    resp_len,
    assign,
    rewards,
    feat_q,
    feat_k,
):
    dp_count = lax.axis_size("dp")
    my_index = lax.axis_index("dp")
    head_count = feat_q.shape[0]
    head_width = feat_q.shape[1]
    length = resp_q.shape[1]
    prompt_rows = prompt_k.shape[1]
    queries = resp_q[0].reshape(length, head_count, head_width)
    key_rows = resp_k[0].reshape(length, head_count, head_width)
    values = resp_v[0].reshape(length, head_count, head_width)
    prompt_keys = prompt_k[0].reshape(prompt_rows, head_count, head_width)
    prompt_values = prompt_v[0].reshape(prompt_rows, head_count, head_width)
    keep = my_index * prompt_rows + jnp.arange(prompt_rows) < prompt_len[0]
    prompt_feat = jnp.where(
        keep[:, None, None], features(prompt_keys, feat_k), jnp.zeros((), jnp.bfloat16)
    )
    part_state = jnp.einsum(
        "shf,she->hfe", prompt_feat, prompt_values, preferred_element_type=jnp.float32
    )
    part_total = jnp.sum(prompt_feat.astype(jnp.float32), axis=0)
    query_feat = features(queries, feat_q)
    key_feat = features(key_rows, feat_k)
    kv_state, key_total = together((part_state, part_total), "dp")
    prompt_num, prompt_den = state_terms(
        query_feat, kv_state.astype(jnp.bfloat16), key_total.astype(jnp.bfloat16)
    )
    causal = jnp.arange(length)[:, None] >= jnp.arange(length)[None, :]
    scores = jnp.einsum("thf,shf->hts", query_feat, key_feat, preferred_element_type=jnp.float32)
    scores = jnp.where(causal[None], scores, jnp.float32(0.0))
    intra_den = jnp.sum(scores, axis=-1)
    intra_num = jnp.einsum(
        "hts,she->the", scores.astype(jnp.bfloat16), values, preferred_element_type=jnp.float32
    )
    combined = (prompt_num.astype(jnp.float32) + intra_num) / (
        prompt_den.astype(jnp.float32) + intra_den.T
    )[:, :, None]
    live_rows = jnp.arange(length) < resp_len[0, 0]
    combined = jnp.where(live_rows[:, None, None], combined, jnp.float32(0.0))
    result = combined.astype(jnp.bfloat16).reshape(-1, BLK, head_count * head_width)
    pieces = result.shape[0]
    slot_width = assign.shape[1]
    table, lengths = gather_together((assign, resp_len), "dp", (1, 1))
    slot_ids = table[0].reshape(dp_count, slot_width)
    own_ids = assign[0]
    source = own_ids // pieces
    stretch_index = own_ids % pieces
    picker = source[:, None] == jnp.arange(dp_count)[None, :]
    flat_rows = result.reshape(pieces * BLK, head_count * head_width)
    columns = lax.all_to_all(flat_rows, "dp", split_axis=1, concat_axis=0, tiled=True)
    narrow = columns.shape[1]
    every_block = columns.reshape(dp_count * pieces, BLK * narrow)
    chooser = slot_ids.reshape(-1)[:, None] == jnp.arange(dp_count * pieces)[None, :]
    routed = jnp.dot(
        chooser.astype(jnp.bfloat16), every_block, preferred_element_type=jnp.float32
    ).astype(jnp.bfloat16)
    routed = routed.reshape(dp_count, slot_width * BLK, narrow)
    arrived = lax.all_to_all(routed, "dp", split_axis=0, concat_axis=2, tiled=True)
    reward_all = lax.all_gather(rewards, "dp", axis=1, tiled=True)[0]
    centred = reward_all - jnp.sum(reward_all) / dp_count
    spread = lax.psum(jnp.sum(centred * centred), "group")
    advantage = centred / jnp.sqrt(spread / (lax.axis_size("group") * dp_count) + 1e-06)
    slot_adv = jnp.sum(jnp.where(picker, advantage[None, :], jnp.float32(0.0)), axis=1)
    slot_len = jnp.sum(jnp.where(picker, lengths[0][None, :], 0), axis=1)
    positions = stretch_index[:, None] * BLK + jnp.arange(BLK)[None, :]
    token_adv = jnp.where(positions < slot_len[:, None], slot_adv[:, None], jnp.float32(0.0))
    return (arrived, token_adv.reshape(1, slot_width * BLK))


def solution(mesh):
    return jax.shard_map(
        body,
        mesh=mesh,
        in_specs=(
            P("group", "dp", None),
            P("group", "dp", None),
            P("group", "dp", None),
            P("group", "dp", None),
            P("group", "dp", None),
            P("group"),
            P("group", "dp"),
            P("group", "dp"),
            P("group", "dp"),
            P(),
            P(),
        ),
        out_specs=(P("group", "dp", None), P("group", "dp")),
        check_vma=False,
    )
```

profile of v0, /device:TPU:8, one launch (start us, length us, event | category | flops | bytes accessed | tf_op | source)
XLA Modules:
  0.0 253.0 jit_solution(6353449763170602200)
XLA Ops:
  0.6 0.0 copy-start
  0.7 2.1 copy.72
  2.8 0.0 copy-done
  2.8 1.3 fusion.28
  4.2 3.0 %fusion.53 = (f32[256,32]{0,1:T(8,128)S(1)}, f32[256,32,128]{0,2,1:T(8,128)}) fusion(f32[32,128,256]{2,1,0:T(8,128)S(1)} %fusion.28), kind=kOutput, calls=%fused_computation.89 | output fusion | flops 4194431 | bytes 8421376 | tf_op jit(solution)/shard_map/sub | solution.py:36
  7.1 2.7 %fusion.54 = (f32[256,32]{0,1:T(8,128)S(1)}, f32[256,32,128]{0,2,1:T(8,128)}) fusion(f32[32,128,256]{2,1,0:T(8,128)S(1)} %fusion.28), kind=kOutput, calls=%fused_computation.90 | output fusion | flops 2097279 | bytes 8421376 | tf_op jit(solution)/shard_map/sub | solution.py:36
  9.8 0.0 copy-done.4
  9.8 0.5 copy.71
  10.3 0.7 copy-done.10
  11.1 1.4 fusion.30
  12.5 2.9 %fusion.55 = (f32[256,32]{0,1:T(8,128)S(1)}, f32[256,32,128]{0,2,1:T(8,128)}) fusion(f32[32,128,256]{2,1,0:T(8,128)S(1)} %fusion.30), kind=kOutput, calls=%fused_computation.91 | output fusion | flops 4194431 | bytes 8421376 | tf_op jit(solution)/shard_map/sub | solution.py:36
  15.4 2.7 %fusion.56 = (f32[256,32]{0,1:T(8,128)S(1)}, f32[256,32,128]{0,2,1:T(8,128)}) fusion(f32[32,128,256]{2,1,0:T(8,128)S(1)} %fusion.30), kind=kOutput, calls=%fused_computation.92 | output fusion | flops 2097279 | bytes 8421376 | tf_op jit(solution)/shard_map/sub | solution.py:36
  18.1 0.2 copy.68
  18.3 2.5 fusion.57
  20.8 0.9 fusion.38
  21.7 1.9 fusion.60
  24.3 0.0 copy-start.12
  24.3 2.2 divide_convert_fusion.4
  26.5 0.6 convert_reduce_fusion
  27.2 0.0 copy-done.12
  27.2 0.2 copy.69
  27.4 0.8 fusion.36
  28.2 0.0 copy-start.14
  28.2 2.7 %pad_maximum_fusion = f32[1056768]{0:T(1024)} fusion(f32[8192]{0:T(1024)S(1)} %bitcast.141, f32[1048576]{0:T(1024)S(1)} %bitcast.129), kind=kLoop, calls=%fused_computation.9 | loop fusion | flops 1056768 | bytes 8454144 | tf_op jit(solution)/shard_map/concatenate | solution.py:13
  31.6 0.6 dynamic-slice
  32.2 0.9 bitcast_dynamic-update-slice_fusion
  33.0 114.3 %all-reduce.4 = (bf16[1056768]{0:T(1024)(128)(2,1)S(1)}, f32[16]{0:T(128)S(1)}) all-reduce(f32[1056768]{0:T(1024)} %pad_maximum_fusion, f32[16]{0:T(128)S(1)} %bitcast_dynamic-update-slice_fusion), channel_id=1, replica_groups=mesh['group'=16,'dp'=16] {'dp'}, use_global_device_ids=true, to_apply=%region_5.6 | all-reduce | flops 1056784 | bytes 6340736 | tf_op jit(solution)/shard_map/psum | solution.py:13
  147.3 1.5 slice.27
  148.8 3.3 %copy.66 = bf16[1,256,4096]{1,2,0:T(8,128)(2,1)S(1)} copy(bf16[1,256,4096]{2,1,0:T(8,128)(2,1)} %param.13) | data formatting | bytes 4194304 | tf_op jit(solution)/shard_map/reshape;squeeze | solution.py:71
  152.8 4.8 %divide_convert_fusion.2 = (bf16[256,32,128]{0,2,1:T(8,128)(2,1)S(1)}, bf16[256,32,128]{0,2,1:T(8,128)(2,1)S(1)}) fusion(f32[256,32,128]{0,2,1:T(8,128)} %get-tuple-element.11, f32[256,32]{0,1:T(8,128)S(1)} %get-tuple-element.10, f32[256,32,128]{0,2,1:T(8,128)} %get-tuple-element.13, f32[256,32]{0,1:T(8,128)S(1)} %get-tuple-element.12), kind=kLoop, calls=%fused_computation.34 | loop fusion | flops 4194304 | bytes 12648448 | tf_op jit(solution)/shard_map/convert.5
  157.7 0.7 fusion.35
  158.3 0.0 copy-done.3
  158.3 3.0 %copy-done.2 = f32[256,32,128]{0,2,1:T(8,128)S(1)} copy-done((f32[256,32,128]{0,2,1:T(8,128)S(1)}, f32[256,32,128]{0,2,1:T(8,128)}, u32[]{:S(2)}) %copy-start.2) | copy-done | bytes 4194328
  161.4 3.2 %divide_convert_fusion = (bf16[256,32,128]{0,2,1:T(8,128)(2,1)}, bf16[256,32,128]{0,2,1:T(8,128)(2,1)}) fusion(f32[256,32,128]{0,2,1:T(8,128)S(1)} %copy-done.2, f32[256,32]{0,1:T(8,128)S(1)} %get-tuple-element.6, f32[256,32,128]{0,2,1:T(8,128)S(1)} %copy-done.3, f32[256,32]{0,1:T(8,128)S(1)} %get-tuple-element.8), kind=kLoop, calls=%fused_computation.31 | loop fusion | flops 4194304 | bytes 12648448 | tf_op jit(solution)/shard_map/convert.3
  164.5 5.3 %select_reduce_fusion = (f32[32,256]{1,0:T(8,128)S(1)}, bf16[32,256,256]{1,2,0:T(8,128)(2,1)S(1)}) fusion(pred[256,256]{0,1:T(8,128)(4,1)S(1)} %iota_compare_fusion, bf16[256,32,128]{0,2,1:T(8,128)(2,1)} %get-tuple-element.20, bf16[256,32,128]{0,2,1:T(8,128)(2,1)} %get-tuple-element.21, bf16[256,32,128]{0,2,1:T(8,128)(2,1)} %copy-done.6, ...), kind=kOutput, calls=%fused_computation.7 | convolution fusion | flops 1096802304 | bytes 12681216 | tf_op jit(solution)/shard_map/thf,shf->hts/dot_general | solution.py:89
  169.9 0.8 fusion.6
  170.6 0.8 copy-done.5
  171.4 0.6 copy-done.7
  172.1 0.6 copy-done.9
  172.7 1.2 fusion.13
  173.9 0.0 copy-start.13
  173.9 2.4 copy.54
  176.3 6.6 %all-to-all-start = ((bf16[256,16,256]{2,0,1:T(8,128)(2,1)}), bf16[256,16,256]{2,0,1:T(8,128)(2,1)S(1)}, u32[]{:S(2)}, u32[]{:S(2)}) async-start(bf16[256,16,256]{2,0,1:T(8,128)(2,1)} %copy.54), calls=%async_computation | async-start | bytes 4194304 | tf_op jit(solution)/shard_map/all_to_all | solution.py:110
  182.9 0.6 reduce_sum.117
  184.1 0.6 multiply_reduce_fusion
  184.7 27.0 %psum.15 = f32[]{:T(128)} all-reduce(f32[]{:T(128)} %multiply_reduce_fusion), channel_id=1, replica_groups=mesh['group'=16,'dp'=16] {'group'}, use_global_device_ids=true, to_apply=%region_18.19 | all-reduce | flops 1 | bytes 8 | tf_op jit(solution)/shard_map/psum | solution.py:121
  212.3 0.0 copy-done.13
  212.3 0.2 add_dynamic-update-slice_fusion
  212.5 15.0 %all-reduce = s32[48]{0:T(128)S(1)} all-reduce(s32[48]{0:T(128)S(1)} %add_dynamic-update-slice_fusion), channel_id=2, replica_groups=mesh['group'=16,'dp'=16] {'dp'}, use_global_device_ids=true, to_apply=%add | all-reduce | flops 48 | bytes 384
  227.5 0.1 reshape.187
  227.6 0.1 eq.30
  228.4 0.0 all-to-all-done
  228.4 0.0 copy-start.1
  228.4 2.4 reshape.185
  230.8 2.1 convolution_convert_fusion
  232.9 1.3 reshape.186
  234.2 4.9 %all-to-all-start.1 = ((bf16[16,128,256]{2,1,0:T(8,128)(2,1)}), bf16[16,128,256]{2,1,0:T(8,128)(2,1)S(1)}, u32[]{:S(2)}, u32[]{:S(2)}) async-start(bf16[16,128,256]{2,1,0:T(8,128)(2,1)} %reshape.186), calls=%async_computation.1 | async-start | bytes 2097152 | tf_op jit(solution)/shard_map/all_to_all | solution.py:118
  239.1 0.2 slice_reduce_fusion
  239.3 0.2 select_reduce_fusion.1
  239.5 0.2 select_reduce_fusion.2
  239.7 0.1 compare_select_fusion
  239.7 0.6 select_n.62
  240.3 11.6 %all-to-all-done.1 = bf16[16,128,256]{2,1,0:T(8,128)(2,1)S(1)} async-done(((bf16[16,128,256]{2,1,0:T(8,128)(2,1)}), bf16[16,128,256]{2,1,0:T(8,128)(2,1)S(1)}, u32[]{:S(2)}, u32[]{:S(2)}) %all-to-all-start.1) | async-done | bytes 1048608 | tf_op jit(solution)/shard_map/all_to_all | solution.py:118
  251.9 1.1 copy.67
  (26 shorter events, 0.1 us)
Async XLA Ops:
  0.6 2.2 copy-start
  7.1 2.7 %copy-start.4 = (bf16[1,256,4096]{2,1,0:T(8,128)(2,1)S(1)}, bf16[1,256,4096]{2,1,0:T(8,128)(2,1)}, u32[]{:S(2)}) copy-start(bf16[1,256,4096]{2,1,0:T(8,128)(2,1)} %param.11) | copy-start | bytes 6291460
  9.8 1.2 copy-start.10
  15.4 2.7 %copy-start.11 = (bf16[1,128,4096]{2,1,0:T(8,128)(2,1)S(1)}, bf16[1,128,4096]{2,1,0:T(8,128)(2,1)}, u32[]{:S(2)}) copy-start(bf16[1,128,4096]{2,1,0:T(8,128)(2,1)} %param.14) | copy-start | bytes 3145732
  24.3 2.9 %copy-start.12 = (bf16[1,128,4096]{2,1,0:T(8,128)(2,1)S(1)}, bf16[1,128,4096]{2,1,0:T(8,128)(2,1)}, u32[]{:S(2)}) copy-start(bf16[1,128,4096]{2,1,0:T(8,128)(2,1)} %param.15) | copy-start | bytes 3145732
  28.2 3.4 %copy-start.14 = (u32[256]{0:T(256)S(1)}, u32[256]{0:T(256)}, u32[]{:S(2)}) copy-start(u32[256]{0:T(256)} %constant.64) | copy-start | bytes 3076
  152.8 5.5 %copy-start.3 = (f32[256,32,128]{0,2,1:T(8,128)S(1)}, f32[256,32,128]{0,2,1:T(8,128)}, u32[]{:S(2)}) copy-start(f32[256,32,128]{0,2,1:T(8,128)} %get-tuple-element.9) | copy-start | bytes 12582916
  157.6 6.9 %copy-start.6 = (bf16[256,32,128]{0,2,1:T(8,128)(2,1)}, bf16[256,32,128]{0,2,1:T(8,128)(2,1)S(1)}, u32[]{:S(2)}) copy-start(bf16[256,32,128]{0,2,1:T(8,128)(2,1)S(1)} %get-tuple-element.22) | copy-start | bytes 6291460
  157.6 6.9 %copy-start.8 = (bf16[256,32,128]{0,2,1:T(8,128)(2,1)}, bf16[256,32,128]{0,2,1:T(8,128)(2,1)S(1)}, u32[]{:S(2)}) copy-start(bf16[256,32,128]{0,2,1:T(8,128)(2,1)S(1)} %get-tuple-element.23) | copy-start | bytes 6291460
  157.7 3.7 %copy-start.2 = (f32[256,32,128]{0,2,1:T(8,128)S(1)}, f32[256,32,128]{0,2,1:T(8,128)}, u32[]{:S(2)}) copy-start(f32[256,32,128]{0,2,1:T(8,128)} %get-tuple-element.7) | copy-start | bytes 12582916
  169.8 1.6 copy-start.5
  169.8 2.2 copy-start.7
  169.9 2.8 %copy-start.9 = (bf16[256,32,128]{0,2,1:T(8,128)(2,1)S(1)}, bf16[256,32,128]{0,2,1:T(8,128)(2,1)}, u32[]{:S(2)}) copy-start(bf16[256,32,128]{0,2,1:T(8,128)(2,1)} %copy-done.8) | copy-start | bytes 6291460
  173.9 38.4 %copy-start.13 = (s32[1,2]{1,0:T(1,128)S(1)}, s32[1,2]{1,0:T(1,128)}, u32[]{:S(2)}) copy-start(s32[1,2]{1,0:T(1,128)} %param.18) | copy-start | bytes 28
  176.3 52.1 %all-to-all-start = ((bf16[256,16,256]{2,0,1:T(8,128)(2,1)}), bf16[256,16,256]{2,0,1:T(8,128)(2,1)S(1)}, u32[]{:S(2)}, u32[]{:S(2)}) async-start(bf16[256,16,256]{2,0,1:T(8,128)(2,1)} %copy.54), calls=%async_computation | async-start | bytes 4194304 | tf_op jit(solution)/shard_map/all_to_all | solution.py:110
  228.4 24.6 %copy-start.1 = (bf16[32,128,128]{2,1,0:T(8,128)(2,1)S(1)}, bf16[32,128,128]{2,1,0:T(8,128)(2,1)}, u32[]{:S(2)}) copy-start(bf16[32,128,128]{2,1,0:T(8,128)(2,1)} %param.21) | copy-start | bytes 3145732
  234.2 17.7 %all-to-all-start.1 = ((bf16[16,128,256]{2,1,0:T(8,128)(2,1)}), bf16[16,128,256]{2,1,0:T(8,128)(2,1)S(1)}, u32[]{:S(2)}, u32[]{:S(2)}) async-start(bf16[16,128,256]{2,1,0:T(8,128)(2,1)} %reshape.186), calls=%async_computation.1 | async-start | bytes 2097152 | tf_op jit(solution)/shard_map/all_to_all | solution.py:118
where the time goes:
time: 254 us; the launch traced here: 253 us
  blocking collectives  156 us (61%)
  other arithmetic  28.6 us (11%)
  local copies, waits for them, and re-layouts  23.4 us (9%)
  matrix products  16.8 us (7%)
  waiting for transfers between devices  11.6 us (5%)
  starting transfers between devices  11.5 us (5%)
  between operations  4.87 us (2%)
    psum x1, blocking collectives, together(): subtotal = lax.psum(jnp.concatenate([a.ravel() for a in arrays]), axis)  114 us
    psum x1, blocking collectives, body(): spread = lax.psum(jnp.sum(centred * centred), 'group')  27 us
    unnamed x1, blocking collectives  15 us
    all_to_all x1, waiting for transfers between devices, body(): lax.all_to_all(routed, 'dp', split_axis=0, concat_axis=2, tiled=True)  11.6 us
    unnamed x39, local copies, waits for them, and re-layouts  10.5 us
    another operation x3, other arithmetic  10.2 us
    sub x3, other arithmetic, features(): jax.nn.softmax(logits, axis=-1)  7.28 us
    all_to_all x1, starting transfers between devices, body(): lax.all_to_all(flat_rows, 'dp', split_axis=1, concat_axis=0, tiled=True)  6.58 us
  transfers between devices with their start and end apart: 2, of which 1 were waited for; matrix products, arithmetic and copies ran while one was open for 1% of the time, Pallas kernels for 0%

commit v1 on v0

v1 whole, which is shorter than its diff:
```python
import jax
import jax.numpy as jnp
from jax import lax
from jax.experimental import pallas as pl
from jax.experimental.pallas import tpu as pltpu
from jax.sharding import PartitionSpec as P

BLK = 64
F32 = jnp.float32
BF16 = jnp.bfloat16
NT = (((1,), (1,)), ((), ()))
TN = (((0,), (0,)), ((), ()))
NN = (((1,), (0,)), ((), ()))


def mm(a, b, dims=NN):
    return lax.dot_general(a, b, dims, preferred_element_type=F32)


def feats(x, w):
    u = mm(x, w)
    ep = jnp.exp(u - jnp.max(u, axis=-1, keepdims=True))
    en = jnp.exp(jnp.min(u, axis=-1, keepdims=True) - u)
    rp = 1.0 / jnp.sum(ep, axis=-1, keepdims=True)
    rn = 1.0 / jnp.sum(en, axis=-1, keepdims=True)
    return jnp.concatenate([ep * rp, en * rn], axis=-1)


def state_kernel(n_ref, k_ref, v_ref, w_ref, o_ref):
    rows, width = k_ref.shape[0], w_ref.shape[1]
    full = 2 * w_ref.shape[2]
    keep = lax.broadcasted_iota(jnp.int32, (rows, 1), 0) < n_ref[0]
    rid = lax.broadcasted_iota(jnp.int32, (16, rows), 0)
    tot = jnp.zeros((16, full // 2), F32)
    for h in range(2):
        cols = slice(h * width, (h + 1) * width)
        phi = jnp.where(keep, feats(k_ref[:, cols], w_ref[h]), 0.0).astype(BF16)
        o_ref[0, h * full : (h + 1) * full, :] = mm(phi, v_ref[:, cols], TN).astype(BF16)
        for s in range(2):
            pick = (rid == 2 * h + s).astype(BF16)
            tot = tot + mm(pick, phi[:, s * full // 2 : (s + 1) * full // 2])
    o_ref[0, 2 * full : 2 * full + 16, :] = tot.astype(BF16)


def intra_kernel(q_ref, k_ref, v_ref, wq_ref, wk_ref, o_ref):
    length = q_ref.shape[0]
    pieces = length // BLK
    pq = feats(q_ref[...], wq_ref[0]).astype(BF16)
    pk = feats(k_ref[...], wk_ref[0]).astype(BF16)
    score = mm(pq, pk, NT)
    t = lax.broadcasted_iota(jnp.int32, score.shape, 0)
    s = lax.broadcasted_iota(jnp.int32, score.shape, 1)
    score = jnp.where(s <= t, score, 0.0)
    hi = score.astype(BF16)
    lo = (score - hi.astype(F32)).astype(BF16)
    o_ref[0, :length, :] = mm(hi, v_ref[...]).astype(BF16)
    rid = lax.broadcasted_iota(jnp.int32, (16, length), 0)
    den = jnp.zeros((16, BLK), F32)
    for c in range(pieces):
        pick = (rid // 2 == c).astype(BF16)
        rows = slice(c * BLK, (c + 1) * BLK)
        den = den + mm(pick, hi[rows], NT) + mm(pick, lo[rows], NT)
    dhi = den.astype(BF16).astype(F32)
    odd = lax.broadcasted_iota(jnp.int32, den.shape, 0) % 2 == 1
    den = jnp.where(odd, den - dhi, dhi).astype(BF16)
    o_ref[0, length:, :] = jnp.concatenate([den, jnp.zeros_like(den)], axis=1)


def prompt_kernel(ids_ref, q_ref, part_ref, w_ref, num_ref, den_ref, s_ref, t_ref):
    i = pl.program_id(0)
    width = w_ref.shape[1]
    full = 2 * w_ref.shape[2]
    many = num_ref.shape[1]

    @pl.when(i == 0)
    def _():
        acc = part_ref[0].astype(F32)
        for d in range(1, part_ref.shape[0]):
            acc = acc + part_ref[d].astype(F32)
        acc = acc.astype(BF16)
        s_ref[...] = acc[: 2 * full]
        tail = acc[2 * full :].astype(F32)
        for h in range(2):
            row = jnp.concatenate([tail[2 * h : 2 * h + 1], tail[2 * h + 1 : 2 * h + 2]], axis=1)
            t_ref[h] = jnp.broadcast_to(row, t_ref.shape[1:]).astype(BF16)

    rows = []
    for j in range(many):
        b = ids_ref[i * many + j]
        pieces = q_ref.shape[1] // BLK
        rows.append(q_ref[b // pieces, pl.ds(pl.multiple_of(b % pieces * BLK, BLK), BLK), :])
    x = jnp.concatenate(rows, axis=0)
    for h in range(2):
        phi = feats(x[:, h * width : (h + 1) * width], w_ref[h]).astype(BF16)
        num = mm(phi, s_ref[h * full : (h + 1) * full, :]).astype(BF16)
        den = mm(phi, t_ref[h], NT).astype(BF16)
        num_ref[h] = num.reshape(many, BLK, width)
        den_ref[h] = den.reshape(many, BLK, width)


def combine_kernel(ids_ref, len_ref, part_ref, num_ref, den_ref, o_ref):
    length = part_ref.shape[1] - 16
    pieces = length // BLK
    many = num_ref.shape[1]
    rid = lax.broadcasted_iota(jnp.int32, (16, part_ref.shape[2]), 0)
    row = lax.broadcasted_iota(jnp.int32, (BLK, 1), 0)
    for j in range(many):
        b = ids_ref[j]
        r, c = b // pieces, b % pieces
        num = part_ref[r, pl.ds(pl.multiple_of(c * BLK, BLK), BLK), :].astype(F32)
        pick = (rid // 2 == c).astype(BF16)
        den = mm(part_ref[r, length:, :BLK], pick, TN)
        num = num_ref[0, j].astype(F32) + num
        den = den_ref[0, j].astype(F32) + den
        out = jnp.where(row < len_ref[r] - c * BLK, num / den, 0.0)
        o_ref[j * BLK : (j + 1) * BLK, :] = out.astype(BF16)


def place_kernel(a_ref, b_ref, o_ref):
    width = a_ref.shape[2]
    for o in range(a_ref.shape[0]):
        o_ref[:, 2 * o * width : (2 * o + 1) * width] = a_ref[o]
        o_ref[:, (2 * o + 1) * width : (2 * o + 2) * width] = b_ref[o]


def body(
    resp_q,
    resp_k,
    resp_v,
    prompt_k,
    prompt_v,
    prompt_len,
    resp_len,
    assign,
    rewards,
    feat_q,
    feat_k,
):
    dp = lax.axis_size("dp")
    groups = lax.axis_size("group")
    me = lax.axis_index("dp")
    heads, width, feat = feat_q.shape
    length = resp_q.shape[1]
    pieces = length // BLK
    prompt_rows = prompt_k.shape[1]
    slots = assign.shape[1]
    two = 2 * width
    q, k, v, pk, pv = resp_q[0], resp_k[0], resp_v[0], prompt_k[0], prompt_v[0]

    tiny = jnp.concatenate(
        [assign[0].astype(F32), resp_len[0].astype(F32), rewards[0]]
    )
    tiny = lax.all_to_all(
        jnp.broadcast_to(tiny[None], (dp, slots + 2)), "dp", 0, 0, tiled=True
    )
    ids = tiny[:, :slots].astype(jnp.int32).reshape(-1)
    lens = tiny[:, slots].astype(jnp.int32)
    reward_all = tiny[:, slots + 1]

    q_all = lax.all_to_all(q, "dp", split_axis=1, concat_axis=0, tiled=True).reshape(
        dp, length, two
    )

    keep = jnp.clip(prompt_len[0] - me * prompt_rows, 0, prompt_rows).astype(jnp.int32)
    state_rows = 4 * feat + 16
    part = pl.pallas_call(
        state_kernel,
        grid=(dp,),
        in_specs=[
            pl.BlockSpec(memory_space=pltpu.SMEM),
            pl.BlockSpec((prompt_rows, two), lambda o: (0, o)),
            pl.BlockSpec((prompt_rows, two), lambda o: (0, o)),
            pl.BlockSpec((2, width, feat), lambda o: (o, 0, 0)),
        ],
        out_specs=pl.BlockSpec((1, state_rows, width), lambda o: (o, 0, 0)),
        out_shape=jax.ShapeDtypeStruct((dp, state_rows, width), BF16),
        name="state",
    )(keep.reshape(1), pk, pv, feat_k)
    part = lax.all_to_all(part, "dp", 0, 0, tiled=True)

    inner = []
    for p in range(2):
        piece = pl.pallas_call(
            intra_kernel,
            grid=(dp,),
            in_specs=[
                pl.BlockSpec((length, width), lambda o, p=p: (0, 2 * o + p)),
                pl.BlockSpec((length, width), lambda o, p=p: (0, 2 * o + p)),
                pl.BlockSpec((length, width), lambda o, p=p: (0, 2 * o + p)),
                pl.BlockSpec((1, width, feat), lambda o, p=p: (2 * o + p, 0, 0)),
                pl.BlockSpec((1, width, feat), lambda o, p=p: (2 * o + p, 0, 0)),
            ],
            out_specs=pl.BlockSpec((1, length + 16, width), lambda o: (o, 0, 0)),
            out_shape=jax.ShapeDtypeStruct((dp, length + 16, width), BF16),
            name="intra",
        )(q, k, v, feat_q, feat_k)
        inner.append(lax.all_to_all(piece, "dp", 0, 0, tiled=True))

    total = dp * slots
    many = 4
    own_w = lax.dynamic_slice_in_dim(feat_q, 2 * me, 2, 0)
    num, den = pl.pallas_call(
        prompt_kernel,
        grid=(total // many,),
        in_specs=[
            pl.BlockSpec(memory_space=pltpu.SMEM),
            pl.BlockSpec((dp, length, two), lambda i: (0, 0, 0)),
            pl.BlockSpec((dp, state_rows, width), lambda i: (0, 0, 0)),
            pl.BlockSpec((2, width, feat), lambda i: (0, 0, 0)),
        ],
        out_specs=[
            pl.BlockSpec((2, many, BLK, width), lambda i: (0, i, 0, 0)),
            pl.BlockSpec((2, many, BLK, width), lambda i: (0, i, 0, 0)),
        ],
        out_shape=[
            jax.ShapeDtypeStruct((2, total, BLK, width), BF16),
            jax.ShapeDtypeStruct((2, total, BLK, width), BF16),
        ],
        scratch_shapes=[
            pltpu.VMEM((4 * feat, width), BF16),
            pltpu.VMEM((2, width, 2 * feat), BF16),
        ],
        name="prompt",
    )(ids, q_all, part, own_w)

    outs = []
    for p in range(2):
        piece = pl.pallas_call(
            combine_kernel,
            in_specs=[
                pl.BlockSpec(memory_space=pltpu.SMEM),
                pl.BlockSpec(memory_space=pltpu.SMEM),
                pl.BlockSpec((dp, length + 16, width), lambda i: (0, 0, 0)),
                pl.BlockSpec((1, total, BLK, width), lambda i, p=p: (p, 0, 0, 0)),
                pl.BlockSpec((1, total, BLK, width), lambda i, p=p: (p, 0, 0, 0)),
            ],
            grid=(1,),
            out_specs=pl.BlockSpec((total * BLK, width), lambda i: (0, 0)),
            out_shape=jax.ShapeDtypeStruct((total * BLK, width), BF16),
            name="combine",
        )(ids, lens, inner[p], num, den)
        outs.append(
            lax.all_to_all(piece.reshape(dp, slots * BLK, width), "dp", 0, 0, tiled=True)
        )
    attn = pl.pallas_call(
        place_kernel,
        out_shape=jax.ShapeDtypeStruct((slots * BLK, heads * width), BF16),
        name="place",
    )(*outs)

    centred = reward_all - jnp.sum(reward_all) / dp
    squares = jnp.sum(centred * centred)
    spread = jnp.sum(
        lax.all_to_all(jnp.broadcast_to(squares, (groups, 1)), "group", 0, 0, tiled=True)
    )
    advantage = centred / jnp.sqrt(spread / (groups * dp) + 1e-06)
    own = assign[0]
    picker = (own // pieces)[:, None] == jnp.arange(dp)[None, :]
    slot_adv = jnp.sum(jnp.where(picker, advantage[None, :], 0.0), axis=1)
    slot_len = jnp.sum(jnp.where(picker, lens[None, :], 0), axis=1)
    positions = (own % pieces)[:, None] * BLK + jnp.arange(BLK)[None, :]
    token_adv = jnp.where(positions < slot_len[:, None], slot_adv[:, None], F32(0.0))
    return (attn[None], token_adv.reshape(1, slots * BLK))


def solution(mesh):
    return jax.shard_map(
        body,
        mesh=mesh,
        in_specs=(
            P("group", "dp", None),
            P("group", "dp", None),
            P("group", "dp", None),
            P("group", "dp", None),
            P("group", "dp", None),
            P("group"),
            P("group", "dp"),
            P("group", "dp"),
            P("group", "dp"),
            P(),
            P(),
        ),
        out_specs=(P("group", "dp", None), P("group", "dp")),
        check_vma=False,
    )
```

time: 254 us -> 195 us (0.77); the launches traced: 253 us -> 191 us
  blocking collectives: 156 us -> 13.4 us
  Pallas kernels: 0 us -> 68.3 us
  waiting for transfers between devices: 11.6 us -> 47.7 us
  starting transfers between devices: 11.5 us -> 41.5 us
  other arithmetic: 28.6 us -> 3.61 us
  matrix products: 16.8 us -> 0 us
  local copies, waits for them, and re-layouts: 23.4 us -> 12.6 us
    psum x2 -> x0, blocking collectives: 141 us -> none  [the longest x1 114 us: together(): subtotal = lax.psum(jnp.concatenate([a.ravel() for a in arrays]), axis)]
    pallas_call x0 -> x7, Pallas kernels: none -> 68.3 us  [the longest x2 32.8 us: body(): pl.pallas_call(intra_kernel, grid=(dp,), in_specs=[pl.BlockSpec((length,...]
    all_to_all x2 -> x7, waiting for transfers between devices: 11.6 us -> 47.7 us  [the longest x2 13.5 us: body(): lax.all_to_all(piece.reshape(dp, slots * BLK, width), 'dp', 0, 0, tiled=T...]
    all_to_all x2 -> x7, starting transfers between devices: 11.5 us -> 41.5 us  [the longest x2 12.1 us: body(): lax.all_to_all(piece.reshape(dp, slots * BLK, width), 'dp', 0, 0, tiled=T...]
    unnamed x1 -> x0, blocking collectives: 15 us -> none
    dot_general x9 -> x0, matrix products: 14.3 us -> none  [the longest x1 5.31 us: body(): jnp.einsum('thf,shf->hts', query_feat, key_feat, preferred_element_type=j...]
    all_to_all x0 -> x1, blocking collectives: none -> 13.4 us  [body(): lax.all_to_all(jnp.broadcast_to(tiny[None], (dp, slots + 2)), 'dp', 0, 0,...]
    sub x5 -> x0, other arithmetic: 13.2 us -> none  [the longest x3 7.28 us: features(): jax.nn.softmax(logits, axis=-1)]
  transfers between devices with their start and end apart: 2 -> 7, of which waited for: 1 -> 5; matrix products, arithmetic and copies ran while one was open for 1% -> 6% of each run, Pallas kernels for 0% -> 34%
where the time goes in v1:
time: 195 us; the launch traced here: 191 us
  Pallas kernels  68.3 us (35%)
  waiting for transfers between devices  47.7 us (24%)
  starting transfers between devices  41.5 us (21%)
  blocking collectives  13.4 us (7%)
  local copies, waits for them, and re-layouts  12.6 us (6%)
  between operations  4 us (2%)
  other arithmetic  3.61 us (2%)
    pallas_call x2, Pallas kernels, body(): pl.pallas_call(intra_kernel, grid=(dp,), in_specs=[pl.BlockSpec((length,...  32.8 us
    pallas_call x1, Pallas kernels, body(): pl.pallas_call(state_kernel, grid=(dp,), in_specs=[pl.BlockSpec(memory_sp...  16.4 us
    all_to_all x2, waiting for transfers between devices, body(): lax.all_to_all(piece.reshape(dp, slots * BLK, width), 'dp', 0, 0, tiled=T...  13.5 us
    all_to_all x1, blocking collectives, body(): lax.all_to_all(jnp.broadcast_to(tiny[None], (dp, slots + 2)), 'dp', 0, 0,...  13.4 us
    all_to_all x2, starting transfers between devices, body(): lax.all_to_all(piece.reshape(dp, slots * BLK, width), 'dp', 0, 0, tiled=T...  12.1 us
    all_to_all x2, waiting for transfers between devices, body(): inner.append(lax.all_to_all(piece, 'dp', 0, 0, tiled=True))  11.9 us
    all_to_all x1, waiting for transfers between devices, body(): lax.all_to_all(q, 'dp', split_axis=1, concat_axis=0, tiled=True)  11.5 us
    pallas_call x1, Pallas kernels, body(): pl.pallas_call(prompt_kernel, grid=(total // many,), in_specs=[pl.BlockSp...  10.9 us
  transfers between devices with their start and end apart: 7, of which 5 were waited for; matrix products, arithmetic and copies ran while one was open for 6% of the time, Pallas kernels for 34%

profile of v1, /device:TPU:8, one launch (start us, length us, event | category | flops | bytes accessed | tf_op | source)
XLA Modules:
  0.0 191.1 jit_solution(4756981594469267)
XLA Ops:
  1.9 0.7 bitcast_convert_fusion
  2.6 0.1 pad_maximum_fusion
  2.7 13.4 %all_to_all.56 = f32[16,1,4]{2,1,0:T(1,128)S(1)} all-to-all(f32[16,1,4]{2,1,0:T(1,128)S(1)} %broadcast_in_dim.56), channel_id=1, replica_groups=mesh['group'=16,'dp'=16] {'dp'}, dimensions={0} | all-to-all | bytes 512 | tf_op jit(solution)/shard_map/all_to_all | solution.py:153
  16.1 0.1 copy.25
  16.2 0.6 slice_reduce_fusion
  17.4 0.6 multiply_reduce_fusion
  18.0 1.2 broadcast_in_dim.60
  19.3 8.6 %all-to-all-start.7 = ((f32[16,1,1]{2,1,0:T(1,128)}), f32[16,1,1]{2,1,0:T(1,128)S(1)}, u32[]{:S(2)}, u32[]{:S(2)}) async-start(f32[16,1,1]{2,1,0:T(1,128)} %broadcast_in_dim.60), calls=%async_computation.7 | async-start | bytes 16384 | tf_op jit(solution)/shard_map/all_to_all | solution.py:254
  27.8 16.4 %intra.3 = bf16[16,272,128]{2,1,0:T(8,128)(2,1)} custom-call(bf16[256,4096]{1,0:T(8,128)(2,1)} %bitcast.37, bf16[256,4096]{1,0:T(8,128)(2,1)} %bitcast.41, bf16[256,4096]{1,0:T(8,128)(2,1)} %bitcast.43, bf16[32,128,128]{2,1,0:T(8,128)(2,1)} %wq_ref.3, bf16[32,128,128]{2,1,0:T(8,128)(2,1)} %wk_ref.3), custom_call_target="tpu_custom_call" | custom-call | tf_op jit(solution)/shard_map/intra/pallas_call | solution.py:183
  44.2 0.0 copy-start
  44.2 0.0 all-to-all-done.7
  44.2 5.1 %all-to-all-start.5 = ((bf16[16,272,128]{2,1,0:T(8,128)(2,1)}), bf16[16,272,128]{2,1,0:T(8,128)(2,1)S(1)}, u32[]{:S(2)}, u32[]{:S(2)}) async-start(bf16[16,272,128]{2,1,0:T(8,128)(2,1)} %intra.3), calls=%async_computation.5 | async-start | bytes 2228224 | tf_op jit(solution)/shard_map/all_to_all | solution.py:197
  49.3 0.0 copy-done
  49.3 2.5 %copy.27 = bf16[1,256,4096]{1,2,0:T(8,128)(2,1)} copy(bf16[1,256,4096]{2,1,0:T(8,128)(2,1)S(1)} %copy-done) | data formatting | bytes 4194304 | tf_op args[0]
  51.8 3.9 %copy.28 = bf16[256,16,256]{2,0,1:T(8,128)(2,1)} copy(bf16[256,16,256]{0,2,1:T(8,128)(2,1)} %bitcast.40) | data formatting | bytes 4194304 | tf_op jit(solution)/shard_map/all_to_all | solution.py:160
  55.7 11.9 %all-to-all-done.5.part_ref = bf16[16,272,128]{2,1,0:T(8,128)(2,1)S(1)} async-done(((bf16[16,272,128]{2,1,0:T(8,128)(2,1)}), bf16[16,272,128]{2,1,0:T(8,128)(2,1)S(1)}, u32[]{:S(2)}, u32[]{:S(2)}) %all-to-all-start.5) | async-done | bytes 1114144 | tf_op jit(solution)/shard_map/all_to_all | solution.py:197
  67.6 0.0 copy-start.3
  67.6 5.0 %all-to-all-start.2 = ((bf16[256,16,256]{2,0,1:T(8,128)(2,1)}), bf16[256,16,256]{2,0,1:T(8,128)(2,1)S(1)}, u32[]{:S(2)}, u32[]{:S(2)}) async-start(bf16[256,16,256]{2,0,1:T(8,128)(2,1)} %copy.28), calls=%async_computation.2 | async-start | bytes 4194304 | tf_op jit(solution)/shard_map/all_to_all | solution.py:160
  72.5 0.0 copy-done.3
  73.2 16.4 %state.1 = bf16[16,528,128]{2,1,0:T(8,128)(2,1)} custom-call(s32[1]{0:T(128)} %bitcast.11.n_ref, bf16[128,4096]{1,0:T(8,128)(2,1)} %bitcast.48, bf16[128,4096]{1,0:T(8,128)(2,1)} %bitcast.49, bf16[32,128,128]{2,1,0:T(8,128)(2,1)} %wk_ref.3), custom_call_target="tpu_custom_call" | custom-call | tf_op jit(solution)/shard_map/state/pallas_call | solution.py:166
  89.6 11.5 %all-to-all-done.2 = bf16[256,16,256]{2,0,1:T(8,128)(2,1)S(1)} async-done(((bf16[256,16,256]{2,0,1:T(8,128)(2,1)}), bf16[256,16,256]{2,0,1:T(8,128)(2,1)S(1)}, u32[]{:S(2)}, u32[]{:S(2)}) %all-to-all-start.2) | async-done | bytes 2097184 | tf_op jit(solution)/shard_map/all_to_all | solution.py:160
  101.1 0.0 copy-start.2
  101.1 1.3 copy-done.2
  102.4 5.2 %all-to-all-start.3 = ((bf16[16,528,128]{2,1,0:T(8,128)(2,1)}), bf16[16,528,128]{2,1,0:T(8,128)(2,1)S(1)}, u32[]{:S(2)}, u32[]{:S(2)}) async-start(bf16[16,528,128]{2,1,0:T(8,128)(2,1)} %state.1), calls=%async_computation.3 | async-start | bytes 4325376 | tf_op jit(solution)/shard_map/all_to_all | solution.py:179
  107.6 16.4 %intra.2 = bf16[16,272,128]{2,1,0:T(8,128)(2,1)} custom-call(bf16[256,4096]{1,0:T(8,128)(2,1)} %bitcast.38, bf16[256,4096]{1,0:T(8,128)(2,1)} %bitcast.42, bf16[256,4096]{1,0:T(8,128)(2,1)} %bitcast.44, bf16[32,128,128]{2,1,0:T(8,128)(2,1)} %wq_ref.3, bf16[32,128,128]{2,1,0:T(8,128)(2,1)} %wk_ref.3), custom_call_target="tpu_custom_call" | custom-call | tf_op jit(solution)/shard_map/intra/pallas_call | solution.py:183
  124.0 10.7 %all-to-all-done.3.part_ref = bf16[16,528,128]{2,1,0:T(8,128)(2,1)S(1)} async-done(((bf16[16,528,128]{2,1,0:T(8,128)(2,1)}), bf16[16,528,128]{2,1,0:T(8,128)(2,1)S(1)}, u32[]{:S(2)}, u32[]{:S(2)}) %all-to-all-start.3) | async-done | bytes 2162720 | tf_op jit(solution)/shard_map/all_to_all | solution.py:179
  134.7 0.0 copy-start.1
  134.7 5.7 %all-to-all-start.1 = ((bf16[16,272,128]{2,1,0:T(8,128)(2,1)}), bf16[16,272,128]{2,1,0:T(8,128)(2,1)S(1)}, u32[]{:S(2)}, u32[]{:S(2)}) async-start(bf16[16,272,128]{2,1,0:T(8,128)(2,1)} %intra.2), calls=%async_computation.1 | async-start | bytes 2228224 | tf_op jit(solution)/shard_map/all_to_all | solution.py:197
  140.4 1.5 constant_dynamic-slice_fusion.w_ref
  141.8 0.1 copy.26
  141.9 0.6 reshape.152.ids_ref
  142.5 0.6 reduce_sum.48
  143.8 0.6 divide_bitcast_fusion
  144.4 0.0 copy-done.1
  144.4 10.9 %prompt.1 = (bf16[2,32,64,128]{3,2,1,0:T(8,128)(2,1)}, bf16[2,32,64,128]{3,2,1,0:T(8,128)(2,1)}) custom-call(s32[32]{0:T(128)} %reshape.152.ids_ref, bf16[16,256,256]{2,1,0:T(8,128)(2,1)} %bitcast.39, bf16[16,528,128]{2,1,0:T(8,128)(2,1)} %copy-done.1, bf16[2,128,128]{2,1,0:T(8,128)(2,1)} %constant_dynamic-slice_fusion.w_ref), custom_call_target="tpu_custom_call" | custom-call | tf_op jit(solution)/shard_map/prompt/pallas_call | solution.py:202
  155.3 2.9 %combine.3 = bf16[2048,128]{1,0:T(8,128)(2,1)} custom-call(s32[32]{0:T(128)} %reshape.152.ids_ref, s32[16]{0:T(128)} %get-tuple-element.7.len_ref, bf16[16,272,128]{2,1,0:T(8,128)(2,1)} %copy-done.3, bf16[2,32,64,128]{3,2,1,0:T(8,128)(2,1)} %get-tuple-element.4.num_ref, bf16[2,32,64,128]{3,2,1,0:T(8,128)(2,1)} %get-tuple-element.5.den_ref), custom_call_target="tpu_custom_call" | custom-call | tf_op jit(solution)/shard_map/combine/pallas_call | solution.py:228
  158.3 0.0 all-to-all-done.1.part_ref
  158.3 0.0 copy-start.4
  158.3 7.2 %all-to-all-start.6 = ((bf16[16,128,128]{2,1,0:T(8,128)(2,1)}), bf16[16,128,128]{2,1,0:T(8,128)(2,1)S(1)}, u32[]{:S(2)}, u32[]{:S(2)}) async-start(bf16[16,128,128]{2,1,0:T(8,128)(2,1)} %bitcast.46), calls=%async_computation.6 | async-start | bytes 1048576 | tf_op jit(solution)/shard_map/all_to_all | solution.py:243
  165.5 0.0 copy-done.4
  165.5 0.0 copy-start.8
  165.5 0.0 copy-start.7
  165.5 2.9 %combine.2 = bf16[2048,128]{1,0:T(8,128)(2,1)} custom-call(s32[32]{0:T(128)} %reshape.152.ids_ref, s32[16]{0:T(128)} %get-tuple-element.7.len_ref, bf16[16,272,128]{2,1,0:T(8,128)(2,1)} %copy-done.4, bf16[2,32,64,128]{3,2,1,0:T(8,128)(2,1)} %get-tuple-element.4.num_ref, bf16[2,32,64,128]{3,2,1,0:T(8,128)(2,1)} %get-tuple-element.5.den_ref), custom_call_target="tpu_custom_call" | custom-call | tf_op jit(solution)/shard_map/combine/pallas_call | solution.py:228
  168.4 5.8 %all-to-all-done.6.b_ref = bf16[16,128,128]{2,1,0:T(8,128)(2,1)S(1)} async-done(((bf16[16,128,128]{2,1,0:T(8,128)(2,1)}), bf16[16,128,128]{2,1,0:T(8,128)(2,1)S(1)}, u32[]{:S(2)}, u32[]{:S(2)}) %all-to-all-start.6) | async-done | bytes 524320 | tf_op jit(solution)/shard_map/all_to_all | solution.py:243
  174.2 0.0 copy-start.5
  174.2 4.8 %all-to-all-start.4 = ((bf16[16,128,128]{2,1,0:T(8,128)(2,1)}), bf16[16,128,128]{2,1,0:T(8,128)(2,1)S(1)}, u32[]{:S(2)}, u32[]{:S(2)}) async-start(bf16[16,128,128]{2,1,0:T(8,128)(2,1)} %bitcast.45), calls=%async_computation.4 | async-start | bytes 1048576 | tf_op jit(solution)/shard_map/all_to_all | solution.py:243
  179.0 0.0 copy-done.8
  179.1 0.0 copy-done.7
  179.1 0.2 select_reduce_fusion.1
  179.3 0.2 select_reduce_fusion
  179.4 0.1 compare_select_fusion
  179.5 0.6 select_n.51
  180.1 7.7 %all-to-all-done.4.a_ref = bf16[16,128,128]{2,1,0:T(8,128)(2,1)S(1)} async-done(((bf16[16,128,128]{2,1,0:T(8,128)(2,1)}), bf16[16,128,128]{2,1,0:T(8,128)(2,1)S(1)}, u32[]{:S(2)}, u32[]{:S(2)}) %all-to-all-start.4) | async-done | bytes 524320 | tf_op jit(solution)/shard_map/all_to_all | solution.py:243
  187.9 0.0 copy-done.5
  187.9 0.0 copy-start.6
  187.9 0.8 copy-done.6
  188.7 2.4 %place.1 = bf16[128,4096]{1,0:T(8,128)(2,1)} custom-call(bf16[16,128,128]{2,1,0:T(8,128)(2,1)} %copy-done.6, bf16[16,128,128]{2,1,0:T(8,128)(2,1)} %copy-done.5), custom_call_target="tpu_custom_call" | custom-call | tf_op jit(solution)/shard_map/place/pallas_call | solution.py:245
  (3 shorter events, 0.0 us)
Async XLA Ops:
  19.3 25.0 %all-to-all-start.7 = ((f32[16,1,1]{2,1,0:T(1,128)}), f32[16,1,1]{2,1,0:T(1,128)S(1)}, u32[]{:S(2)}, u32[]{:S(2)}) async-start(f32[16,1,1]{2,1,0:T(1,128)} %broadcast_in_dim.60), calls=%async_computation.7 | async-start | bytes 16384 | tf_op jit(solution)/shard_map/all_to_all | solution.py:254
  44.2 5.1 %copy-start = (bf16[1,256,4096]{2,1,0:T(8,128)(2,1)S(1)}, bf16[1,256,4096]{2,1,0:T(8,128)(2,1)}, u32[]{:S(2)}) copy-start(bf16[1,256,4096]{2,1,0:T(8,128)(2,1)} %param.11) | copy-start | bytes 6291460
  44.2 23.4 %all-to-all-start.5 = ((bf16[16,272,128]{2,1,0:T(8,128)(2,1)}), bf16[16,272,128]{2,1,0:T(8,128)(2,1)S(1)}, u32[]{:S(2)}, u32[]{:S(2)}) async-start(bf16[16,272,128]{2,1,0:T(8,128)(2,1)} %intra.3), calls=%async_computation.5 | async-start | bytes 2228224 | tf_op jit(solution)/shard_map/all_to_all | solution.py:197
  67.6 5.0 %copy-start.3 = (bf16[16,272,128]{2,1,0:T(8,128)(2,1)}, bf16[16,272,128]{2,1,0:T(8,128)(2,1)S(1)}, u32[]{:S(2)}) copy-start(bf16[16,272,128]{2,1,0:T(8,128)(2,1)S(1)} %all-to-all-done.5.part_ref) | copy-start | bytes 3342340
  67.6 33.5 %all-to-all-start.2 = ((bf16[256,16,256]{2,0,1:T(8,128)(2,1)}), bf16[256,16,256]{2,0,1:T(8,128)(2,1)S(1)}, u32[]{:S(2)}, u32[]{:S(2)}) async-start(bf16[256,16,256]{2,0,1:T(8,128)(2,1)} %copy.28), calls=%async_computation.2 | async-start | bytes 4194304 | tf_op jit(solution)/shard_map/all_to_all | solution.py:160
  101.1 1.3 copy-start.2
  102.4 32.3 %all-to-all-start.3 = ((bf16[16,528,128]{2,1,0:T(8,128)(2,1)}), bf16[16,528,128]{2,1,0:T(8,128)(2,1)S(1)}, u32[]{:S(2)}, u32[]{:S(2)}) async-start(bf16[16,528,128]{2,1,0:T(8,128)(2,1)} %state.1), calls=%async_computation.3 | async-start | bytes 4325376 | tf_op jit(solution)/shard_map/all_to_all | solution.py:179
  134.7 9.7 %copy-start.1 = (bf16[16,528,128]{2,1,0:T(8,128)(2,1)}, bf16[16,528,128]{2,1,0:T(8,128)(2,1)S(1)}, u32[]{:S(2)}) copy-start(bf16[16,528,128]{2,1,0:T(8,128)(2,1)S(1)} %all-to-all-done.3.part_ref) | copy-start | bytes 6488068
  134.7 23.5 %all-to-all-start.1 = ((bf16[16,272,128]{2,1,0:T(8,128)(2,1)}), bf16[16,272,128]{2,1,0:T(8,128)(2,1)S(1)}, u32[]{:S(2)}, u32[]{:S(2)}) async-start(bf16[16,272,128]{2,1,0:T(8,128)(2,1)} %intra.2), calls=%async_computation.1 | async-start | bytes 2228224 | tf_op jit(solution)/shard_map/all_to_all | solution.py:197
  158.3 7.2 %copy-start.4 = (bf16[16,272,128]{2,1,0:T(8,128)(2,1)}, bf16[16,272,128]{2,1,0:T(8,128)(2,1)S(1)}, u32[]{:S(2)}) copy-start(bf16[16,272,128]{2,1,0:T(8,128)(2,1)S(1)} %all-to-all-done.1.part_ref) | copy-start | bytes 3342340
  158.3 16.0 %all-to-all-start.6 = ((bf16[16,128,128]{2,1,0:T(8,128)(2,1)}), bf16[16,128,128]{2,1,0:T(8,128)(2,1)S(1)}, u32[]{:S(2)}, u32[]{:S(2)}) async-start(bf16[16,128,128]{2,1,0:T(8,128)(2,1)} %bitcast.46), calls=%async_computation.6 | async-start | bytes 1048576 | tf_op jit(solution)/shard_map/all_to_all | solution.py:243
  165.5 13.6 %copy-start.8 = (s32[1,2]{1,0:T(1,128)S(1)}, s32[1,2]{1,0:T(1,128)}, u32[]{:S(2)}) copy-start(s32[1,2]{1,0:T(1,128)} %param.18) | copy-start | bytes 28
  165.5 13.6 %copy-start.7 = (s32[16]{0:T(128)S(1)}, s32[16]{0:T(128)}, u32[]{:S(2)}) copy-start(s32[16]{0:T(128)} %get-tuple-element.7.len_ref) | copy-start | bytes 196
  174.2 13.6 %copy-start.5 = (bf16[16,128,128]{2,1,0:T(8,128)(2,1)}, bf16[16,128,128]{2,1,0:T(8,128)(2,1)S(1)}, u32[]{:S(2)}) copy-start(bf16[16,128,128]{2,1,0:T(8,128)(2,1)S(1)} %all-to-all-done.6.b_ref) | copy-start | bytes 1572868
  174.2 13.6 %all-to-all-start.4 = ((bf16[16,128,128]{2,1,0:T(8,128)(2,1)}), bf16[16,128,128]{2,1,0:T(8,128)(2,1)S(1)}, u32[]{:S(2)}, u32[]{:S(2)}) async-start(bf16[16,128,128]{2,1,0:T(8,128)(2,1)} %bitcast.45), calls=%async_computation.4 | async-start | bytes 1048576 | tf_op jit(solution)/shard_map/all_to_all | solution.py:243
  187.9 0.8 copy-start.6

commit v2 on v1

v2 whole, which is shorter than its diff:
```python
import jax
import jax.numpy as jnp
from jax import lax
from jax.experimental import pallas as pl
from jax.experimental.pallas import tpu as pltpu
from jax.sharding import PartitionSpec as P


BLK = 64
SIDE = 4
EXTRA = 8
F32 = jnp.float32
BF16 = jnp.bfloat16
NT = (((1,), (1,)), ((), ()))
TN = (((0,), (0,)), ((), ()))
NN = (((1,), (0,)), ((), ()))


def mm(a, b, dims=NN):
    return lax.dot_general(a, b, dims, preferred_element_type=F32)


def feats(x, w):
    u = mm(w.T, x, NT)
    ep = jnp.exp(u - jnp.max(u, axis=0, keepdims=True))
    en = jnp.exp(jnp.min(u, axis=0, keepdims=True) - u)
    rp = 1.0 / jnp.sum(ep, axis=0, keepdims=True)
    rn = 1.0 / jnp.sum(en, axis=0, keepdims=True)
    return jnp.concatenate([ep * rp, en * rn], axis=0)


def spread_kernel(tab_ref, q_ref, o_ref):
    length, width = q_ref.shape[0], o_ref.shape[2]
    part = width // 8
    r = jnp.broadcast_to(tab_ref[...], (EXTRA, width))
    col = lax.broadcasted_iota(jnp.int32, r.shape, 1)
    r1 = r.astype(BF16).astype(F32)
    r2 = (r - r1).astype(BF16).astype(F32)
    r3 = r - r1 - r2
    tabs = jnp.where(col < 2 * part, r1, jnp.where(col < 3 * part, r2, r3)).astype(BF16)
    for o in range(o_ref.shape[0]):
        o_ref[o, :length, :] = q_ref[:, o * width : (o + 1) * width]
        o_ref[o, length:, :] = tabs


def state_kernel(at_ref, *refs):
    ins, outs = refs[:6], refs[6:]
    rows, width = ins[0].shape
    keep = lax.broadcasted_iota(jnp.int32, (1, rows), 1) < at_ref[2]
    rid = lax.broadcasted_iota(jnp.int32, (EXTRA, rows), 0)
    shift = pl.program_id(0)
    for p in range(2):
        k_ref, v_ref, w_ref = ins[3 * p : 3 * p + 3]
        phi = jnp.where(keep, feats(k_ref[...], w_ref[0]), 0.0).astype(BF16)
        half = phi.shape[0] // 2
        state = mm(phi, v_ref[...]).astype(BF16)
        tail = jnp.zeros((EXTRA, width), F32)
        for i in range(2):
            pick = (rid == i).astype(BF16)
            tail = tail + mm(pick, phi[i * half : (i + 1) * half], NT)
        tail = tail.astype(BF16)
        for s in range(SIDE):

            @pl.when(shift == s)
            def _(o_ref=outs[SIDE * p + s], state=state, tail=tail):
                o_ref[0, : 2 * half, :] = state
                o_ref[0, 2 * half :, :] = tail


def add_kernel(at_ref, *refs):
    ins, outs = refs[: 2 * SIDE], refs[2 * SIDE :]
    for p in range(2):
        for s in range(SIDE):
            j = (at_ref[1 - p] + s) % SIDE
            acc = ins[SIDE * p][j].astype(F32)
            for i in range(1, SIDE):
                acc = acc + ins[SIDE * p + i][j].astype(F32)
            outs[SIDE * p + s][...] = acc.astype(BF16)


def intra_kernel(q_ref, k_ref, v_ref, wq_ref, wk_ref, *rest):
    o_ref = rest[-1]
    length = q_ref.shape[0]
    half = length // 2
    pq = feats(q_ref[...], wq_ref[0]).astype(BF16).T
    pk = feats(k_ref[...], wk_ref[0]).astype(BF16)
    score = mm(pq, pk)
    t = lax.broadcasted_iota(jnp.int32, score.shape, 0)
    s = lax.broadcasted_iota(jnp.int32, score.shape, 1)
    score = jnp.where(s <= t, score, 0.0)
    o_ref[0, :length, :] = mm(score.astype(BF16), v_ref[...]).astype(BF16)
    fold = score[:, :half] + score[:, half:]
    hi = fold.astype(BF16)
    lo = (fold - hi.astype(F32)).astype(BF16)
    ones = jnp.ones((EXTRA, length), BF16)
    den = mm(ones, jnp.concatenate([hi, lo], axis=1), NT)
    rid = lax.broadcasted_iota(jnp.int32, (EXTRA, half), 0)
    den = jnp.where(rid < 2, den[:, :half], den[:, half:])
    dhi = den.astype(BF16).astype(F32)
    den = jnp.where(rid % 2 == 1, den - dhi, dhi)
    o_ref[0, length:, :] = den.astype(BF16)


def prompt_kernel(ids_ref, q_ref, w_ref, *refs):
    parts = refs[: 2 * SIDE]
    num_ref, den_ref, s_ref, t_ref = refs[2 * SIDE :]
    i = pl.program_id(0)
    width = w_ref.shape[1]
    full = 2 * w_ref.shape[2]
    many = num_ref.shape[0]

    @pl.when(i == 0)
    def _():
        for h in range(2):
            acc = parts[SIDE * h][...].astype(F32)
            for d in range(1, SIDE):
                acc = acc + parts[SIDE * h + d][...].astype(F32)
            s_ref[h] = acc[:full].astype(BF16)
            row = jnp.concatenate([acc[full : full + 1], acc[full + 1 : full + 2]], axis=1)
            t_ref[h] = jnp.broadcast_to(row, t_ref.shape[1:]).astype(BF16)

    rows = []
    pieces = q_ref.shape[1] // BLK
    for j in range(many):
        b = ids_ref[i * many + j]
        rows.append(q_ref[b // pieces, pl.ds(pl.multiple_of(b % pieces * BLK, BLK), BLK), :])
    x = jnp.concatenate(rows, axis=0)
    for h in range(2):
        cols = slice(h * width, (h + 1) * width)
        phi = feats(x[:, cols], w_ref[h]).astype(BF16).T
        num = mm(phi, s_ref[h]).astype(BF16)
        den = mm(phi, t_ref[h], NT).astype(BF16)
        num_ref[:, :, cols] = num.reshape(many, BLK, width)
        den_ref[:, :, cols] = den.reshape(many, BLK, width)


def combine_kernel(ids_ref, len_ref, part_ref, num_ref, den_ref, o_ref):
    length = part_ref.shape[1] - EXTRA
    width = part_ref.shape[2] // 2
    pieces = length // BLK
    many = num_ref.shape[0]
    i = pl.program_id(0)
    rid = lax.broadcasted_iota(jnp.int32, (EXTRA, width), 0)
    row = lax.broadcasted_iota(jnp.int32, (BLK, 1), 0)
    for j in range(many):
        b = ids_ref[i * many + j]
        r, c = b // pieces, b % pieces
        pick = (rid // 2 == c // 2).astype(BF16)
        for h in range(2):
            cols = slice(h * width, (h + 1) * width)
            num = part_ref[r, pl.ds(pl.multiple_of(c * BLK, BLK), BLK), cols].astype(F32)
            den = mm(part_ref[r, length:, cols], pick, TN)
            den = jnp.where(c % 2 == 0, den[:BLK], den[BLK:])
            num = num_ref[j, :, cols].astype(F32) + num
            den = den_ref[j, :, cols].astype(F32) + den
            out = jnp.where(row < len_ref[r] - c * BLK, num / den, 0.0)
            o_ref[j * BLK : (j + 1) * BLK, cols] = out.astype(BF16)


def place_kernel(a_ref, o_ref):
    width = a_ref.shape[2]
    for o in range(a_ref.shape[0]):
        o_ref[:, o * width : (o + 1) * width] = a_ref[o]


def hop(dx, dy):
    return [
        (x * SIDE + y, (x + dx) % SIDE * SIDE + (y + dy) % SIDE)
        for x in range(SIDE)
        for y in range(SIDE)
    ]


def body(
    resp_q,
    resp_k,
    resp_v,
    prompt_k,
    prompt_v,
    prompt_len,
    resp_len,
    assign,
    rewards,
    feat_q,
    feat_k,
):
    dp = lax.axis_size("dp")
    groups = lax.axis_size("group")
    me = lax.axis_index("dp")
    heads, width, feat = feat_q.shape
    length = resp_q.shape[1]
    pieces = length // BLK
    prompt_rows = prompt_k.shape[1]
    slots = assign.shape[1]
    two = 2 * width
    tall = length + EXTRA
    q, k, v, pk, pv = resp_q[0], resp_k[0], resp_v[0], prompt_k[0], prompt_v[0]

    part = two // 8
    table = jnp.concatenate(
        [
            assign[0].astype(F32),
            resp_len[0].astype(F32),
            jnp.zeros((part - slots - 1,), F32),
            jnp.broadcast_to(rewards[0], (two - part,)),
        ]
    ).reshape(1, two)
    q_all = pl.pallas_call(
        spread_kernel,
        grid=(4,),
        in_specs=[
            pl.BlockSpec((1, two), lambda o: (0, 0)),
            pl.BlockSpec((length, heads * width // 4), lambda o: (0, o)),
        ],
        out_specs=pl.BlockSpec((dp // 4, tall, two), lambda o: (o, 0, 0)),
        out_shape=jax.ShapeDtypeStruct((dp, tall, two), BF16),
        name="spread",
    )(table, q)
    q_all = lax.all_to_all(q_all, "dp", 0, 0, tiled=True)
    tabs = q_all[:, length, :].astype(F32)
    ids = tabs[:, :slots].astype(jnp.int32).reshape(-1)
    lens = tabs[:, slots].astype(jnp.int32)
    reward_all = tabs[:, part] + tabs[:, 2 * part] + tabs[:, 3 * part]

    keep = jnp.clip(prompt_len[0] - me * prompt_rows, 0, prompt_rows)
    at = jnp.stack([me // SIDE, me % SIDE, keep]).astype(jnp.int32)

    def head(p, s, j, at_ref):
        if p == 0:
            return 2 * ((at_ref[0] + s) % SIDE * SIDE + j)
        return 2 * (j * SIDE + (at_ref[1] + s) % SIDE) + 1

    srows = 2 * feat + EXTRA
    in_specs, out_specs = [], []
    for p in range(2):
        for _ in range(2):
            in_specs.append(
                pl.BlockSpec((prompt_rows, width), lambda s, j, a, p=p: (0, head(p, s, j, a)))
            )
        in_specs.append(
            pl.BlockSpec((1, width, feat), lambda s, j, a, p=p: (head(p, s, j, a), 0, 0))
        )
        for n in range(SIDE):
            out_specs.append(
                pl.BlockSpec(
                    (1, srows, width),
                    lambda s, j, a, n=n: (
                        jnp.where(s < n, 0, jnp.where(s == n, j, SIDE - 1)),
                        0,
                        0,
                    ),
                )
            )
    states = pl.pallas_call(
        state_kernel,
        grid_spec=pltpu.PrefetchScalarGridSpec(
            num_scalar_prefetch=1,
            grid=(SIDE, SIDE),
            in_specs=in_specs,
            out_specs=out_specs,
        ),
        out_shape=[jax.ShapeDtypeStruct((SIDE, srows, width), BF16)] * (2 * SIDE),
        name="state",
    )(at, pk, pv, feat_k, pk, pv, feat_k)
    states = list(states)
    for p in range(2):
        for s in range(1, SIDE):
            i = SIDE * p + s
            states[i] = lax.ppermute(states[i], "dp", hop(s, 0) if p == 0 else hop(0, s))
    states = pl.pallas_call(
        add_kernel,
        in_specs=[pl.BlockSpec(memory_space=pltpu.SMEM)]
        + [pl.BlockSpec(memory_space=pltpu.VMEM)] * (2 * SIDE),
        out_shape=[jax.ShapeDtypeStruct((srows, width), BF16)] * (2 * SIDE),
        name="add",
    )(at, *states)
    states = list(states)
    for p in range(2):
        for s in range(1, SIDE):
            i = SIDE * p + s
            states[i] = lax.ppermute(states[i], "dp", hop(0, s) if p == 0 else hop(s, 0))

    inner = ()
    for p in range(2):
        specs = [pl.BlockSpec((length, width), lambda o, p=p: (0, 2 * o + p))] * 3
        specs += [pl.BlockSpec((1, width, feat), lambda o, p=p: (2 * o + p, 0, 0))] * 2
        inner = pl.pallas_call(
            intra_kernel,
            grid=(dp,),
            in_specs=specs + [pl.BlockSpec(memory_space=pl.ANY)] * p,
            out_specs=pl.BlockSpec((1, tall, width), lambda o, p=p: (o, 0, p)),
            out_shape=jax.ShapeDtypeStruct((dp, tall, two), BF16),
            input_output_aliases={5: 0} if p else {},
            name="intra",
        )(q, k, v, feat_q, feat_k, *inner)
        inner = (inner,)
    inner = lax.all_to_all(inner[0], "dp", 0, 0, tiled=True)

    total = dp * slots
    many = 4
    own_w = lax.dynamic_slice_in_dim(feat_q, 2 * me, 2, 0)
    row_spec = pl.BlockSpec((many, BLK, two), lambda i: (i, 0, 0))
    num, den = pl.pallas_call(
        prompt_kernel,
        grid=(total // many,),
        in_specs=[
            pl.BlockSpec(memory_space=pltpu.SMEM),
            pl.BlockSpec((dp, tall, two), lambda i: (0, 0, 0)),
            pl.BlockSpec((2, width, feat), lambda i: (0, 0, 0)),
        ]
        + [pl.BlockSpec((srows, width), lambda i: (0, 0))] * (2 * SIDE),
        out_specs=[row_spec, row_spec],
        out_shape=[jax.ShapeDtypeStruct((total, BLK, two), BF16)] * 2,
        scratch_shapes=[
            pltpu.VMEM((2, 2 * feat, width), BF16),
            pltpu.VMEM((2, width, 2 * feat), BF16),
        ],
        name="prompt",
    )(ids, q_all, own_w, *states)
    out = pl.pallas_call(
        combine_kernel,
        grid=(total // 8,),
        in_specs=[
            pl.BlockSpec(memory_space=pltpu.SMEM),
            pl.BlockSpec(memory_space=pltpu.SMEM),
            pl.BlockSpec((dp, tall, two), lambda i: (0, 0, 0)),
            pl.BlockSpec((8, BLK, two), lambda i: (i, 0, 0)),
            pl.BlockSpec((8, BLK, two), lambda i: (i, 0, 0)),
        ],
        out_specs=pl.BlockSpec((8 * BLK, two), lambda i: (i, 0)),
        out_shape=jax.ShapeDtypeStruct((total * BLK, two), BF16),
        name="combine",
    )(ids, lens, inner, num, den)
    out = lax.all_to_all(out.reshape(dp, slots * BLK, two), "dp", 0, 0, tiled=True)
    attn = pl.pallas_call(
        place_kernel,
        grid=(4,),
        in_specs=[pl.BlockSpec((dp // 4, slots * BLK, two), lambda i: (i, 0, 0))],
        out_specs=pl.BlockSpec((slots * BLK, heads * width // 4), lambda i: (0, i)),
        out_shape=jax.ShapeDtypeStruct((slots * BLK, heads * width), BF16),
        name="place",
    )(out)

    centred = reward_all - jnp.sum(reward_all) / dp
    spread = jnp.sum(centred * centred).reshape(1, 1)
    step = 1
    while step < groups:
        spread = spread + lax.ppermute(
            spread, "group", [(g, g ^ step) for g in range(groups)]
        )
        step *= 2
    advantage = centred / jnp.sqrt(spread[0, 0] / (groups * dp) + 1e-06)
    own = assign[0]
    picker = (own // pieces)[:, None] == jnp.arange(dp)[None, :]
    slot_adv = jnp.sum(jnp.where(picker, advantage[None, :], 0.0), axis=1)
    slot_len = jnp.sum(jnp.where(picker, lens[None, :], 0), axis=1)
    positions = (own % pieces)[:, None] * BLK + jnp.arange(BLK)[None, :]
    token_adv = jnp.where(positions < slot_len[:, None], slot_adv[:, None], F32(0.0))
    return (attn[None], token_adv.reshape(1, slots * BLK))


def solution(mesh):
    return jax.shard_map(
        body,
        mesh=mesh,
        in_specs=(
            P("group", "dp", None),
            P("group", "dp", None),
            P("group", "dp", None),
            P("group", "dp", None),
            P("group", "dp", None),
            P("group"),
            P("group", "dp"),
            P("group", "dp"),
            P("group", "dp"),
            P(),
            P(),
        ),
        out_specs=(P("group", "dp", None), P("group", "dp")),
        check_vma=False,
    )
```

time: 195 us -> 161 us (0.83)
  waiting for transfers between devices: 47.7 us -> 19.7 us
  blocking collectives: 13.4 us -> 0 us
  starting transfers between devices: 41.5 us -> 50.4 us
  local copies, waits for them, and re-layouts: 12.6 us -> 4.3 us
  Pallas kernels: 68.3 us -> 72.4 us
  between operations: 4 us -> 6.57 us
    all_to_all x7 -> x3, waiting for transfers between devices: 47.7 us -> 0.81 us  [the longest x1 0.8 us: body(): q_all = lax.all_to_all(q_all, 'dp', 0, 0, tiled=True)]
    ppermute x0 -> x16, starting transfers between devices: none -> 32.1 us  [the longest x4 16.1 us: body(): lax.ppermute(spread, 'group', [(g, g ^ step) for g in range(groups)])]
    all_to_all x7 -> x3, starting transfers between devices: 41.5 us -> 18.3 us  [the longest x1 7.39 us: body(): q_all = lax.all_to_all(q_all, 'dp', 0, 0, tiled=True)]
    ppermute x0 -> x16, waiting for transfers between devices: none -> 18.9 us  [the longest x6 11.9 us: body(): lax.ppermute(states[i], 'dp', hop(s, 0) if p == 0 else hop(0, s))]
    all_to_all x1 -> x0, blocking collectives: 13.4 us -> none  [body(): lax.all_to_all(jnp.broadcast_to(tiny[None], (dp, slots + 2)), 'dp', 0, 0,...]
    pallas_call x6 -> x7, Pallas kernels: 57.5 us -> 62.6 us  [the longest x2 29.1 us: body(): pl.pallas_call(intra_kernel, grid=(dp,), in_specs=specs + [pl.BlockSpec(m...]
    all_to_all x2 -> x0, local copies, waits for them, and re-layouts: 3.98 us -> none  [the longest x1 3.91 us: body(): lax.all_to_all(q, 'dp', split_axis=1, concat_axis=0, tiled=True)]
    unnamed x19 -> x31, local copies, waits for them, and re-layouts: 4.59 us -> 1.63 us
  transfers between devices with their start and end apart: 7 -> 19, of which waited for: 5 -> 12; matrix products, arithmetic and copies ran while one was open for 6% -> 4% of each run, Pallas kernels for 34% -> 38%
where the time goes in v2:
time: 161 us; the launch traced here: 158 us
  Pallas kernels  72.4 us (45%)
  starting transfers between devices  50.4 us (31%)
  waiting for transfers between devices  19.7 us (12%)
  between operations  6.57 us (4%)
  other arithmetic  4.59 us (3%)
  local copies, waits for them, and re-layouts  4.3 us (3%)
    pallas_call x2, Pallas kernels, body(): pl.pallas_call(intra_kernel, grid=(dp,), in_specs=specs + [pl.BlockSpec(m...  29.1 us
    pallas_call x1, Pallas kernels, body(): pl.pallas_call(state_kernel, grid_spec=pltpu.PrefetchScalarGridSpec(num_s...  18.7 us
    ppermute x4, starting transfers between devices, body(): lax.ppermute(spread, 'group', [(g, g ^ step) for g in range(groups)])  16.1 us
    ppermute x6, waiting for transfers between devices, body(): lax.ppermute(states[i], 'dp', hop(s, 0) if p == 0 else hop(0, s))  11.9 us
    pallas_call x1, Pallas kernels, body(): pl.pallas_call(prompt_kernel, grid=(total // many,), in_specs=[pl.BlockSp...  9.75 us
    ppermute x6, starting transfers between devices, body(): lax.ppermute(states[i], 'dp', hop(s, 0) if p == 0 else hop(0, s))  8.87 us
    all_to_all x1, starting transfers between devices, body(): q_all = lax.all_to_all(q_all, 'dp', 0, 0, tiled=True)  7.39 us
    ppermute x6, starting transfers between devices, body(): lax.ppermute(states[i], 'dp', hop(0, s) if p == 0 else hop(s, 0))  7.05 us
  transfers between devices with their start and end apart: 19, of which 12 were waited for; matrix products, arithmetic and copies ran while one was open for 4% of the time, Pallas kernels for 38%

profile of v2, /device:TPU:8, one launch (start us, length us, event | category | flops | bytes accessed | tf_op | source)
XLA Modules:
  0.0 157.9 jit_solution(12931657235912819534)
XLA Ops:
  1.9 0.7 bitcast_convert_fusion
  2.6 0.6 pad_maximum_fusion
  3.2 3.8 %spread.1 = bf16[16,264,256]{2,1,0:T(8,128)(2,1)} custom-call(f32[1,256]{1,0:T(1,128)} %bitcast.53, bf16[256,4096]{1,0:T(8,128)(2,1)} %bitcast.37), custom_call_target="tpu_custom_call" | custom-call | tf_op jit(solution)/shard_map/spread/pallas_call | solution.py:208
  7.0 7.4 %all-to-all-start = ((bf16[16,264,256]{2,1,0:T(8,128)(2,1)}), bf16[16,264,256]{2,1,0:T(8,128)(2,1)S(1)}, u32[]{:S(2)}, u32[]{:S(2)}) async-start(bf16[16,264,256]{2,1,0:T(8,128)(2,1)} %spread.1), calls=%async_computation | async-start | bytes 4325376 | tf_op jit(solution)/shard_map/all_to_all | solution.py:219
  14.4 14.5 %intra.2.rest_0_ = bf16[16,264,256]{2,1,0:T(8,128)(2,1)} custom-call(bf16[256,4096]{1,0:T(8,128)(2,1)} %bitcast.38, bf16[256,4096]{1,0:T(8,128)(2,1)} %bitcast.40, bf16[256,4096]{1,0:T(8,128)(2,1)} %bitcast.42, bf16[32,128,128]{2,1,0:T(8,128)(2,1)} %wq_ref.3, bf16[32,128,128]{2,1,0:T(8,128)(2,1)} %refs_5_.1), custom_call_target="tpu_custom_call" | custom-call | tf_op jit(solution)/shard_map/intra/pallas_call | solution.py:287
  28.9 14.5 %intra.3 = bf16[16,264,256]{2,1,0:T(8,128)(2,1)} custom-call(bf16[256,4096]{1,0:T(8,128)(2,1)} %bitcast.39, bf16[256,4096]{1,0:T(8,128)(2,1)} %bitcast.41, bf16[256,4096]{1,0:T(8,128)(2,1)} %bitcast.43, bf16[32,128,128]{2,1,0:T(8,128)(2,1)} %wq_ref.3, bf16[32,128,128]{2,1,0:T(8,128)(2,1)} %refs_5_.1, ...), custom_call_target="tpu_custom_call", output_to_operand_aliasing={{}: (5, {})} | custom-call | tf_op jit(solution)/shard_map/intra/pallas_call | solution.py:287
  43.5 0.8 all-to-all-done.q_ref
  44.3 6.4 %all-to-all-start.1 = ((bf16[16,264,256]{2,1,0:T(8,128)(2,1)}), bf16[16,264,256]{2,1,0:T(8,128)(2,1)}, u32[]{:S(2)}, u32[]{:S(2)}) async-start(bf16[16,264,256]{2,1,0:T(8,128)(2,1)} %intra.3), calls=%async_computation.1 | async-start | bytes 4325376 | tf_op jit(solution)/shard_map/all_to_all | solution.py:297
  51.4 0.7 pad_add_fusion.at_ref
  52.0 18.7 %state.1 = (bf16[4,264,128]{2,1,0:T(8,128)(2,1)}, bf16[4,264,128]{2,1,0:T(8,128)(2,1)}, bf16[4,264,128]{2,1,0:T(8,128)(2,1)}, bf16[4,264,128]{2,1,0:T(8,128)(2,1...) custom-call(s32[3]{0:T(128)} %pad_add_fusion.at_ref, ...), custom_call_target="tpu_custom_call" | custom-call | tf_op jit(solution)/shard_map/state/pallas_call | solution.py:254
  70.7 1.5 collective-permute-start
  72.3 2.7 %collective-permute-start.1 = (bf16[4,264,128]{2,1,0:T(8,128)(2,1)}, bf16[4,264,128]{2,1,0:T(8,128)(2,1)S(1)}, u32[]{:S(2)}, u32[]{:S(2)}) collective-permute-start(bf16[4,264,128]{2,1,0:T(8,128)(2,1)} %get-tuple-element.22), channel_id=1, source_target_pairs={{0,8},{1,9},{2,10},{3,11},{4,12},{5,13},{6,14},{7,15},{8,0},{9,1},... | collective-permute-start | bytes 811016 | tf_op jit(solution)/shard_map/ppermute | solution.py:269
  74.9 1.5 collective-permute-start.2
  76.4 1.5 collective-permute-start.3
  77.9 1.2 collective-permute-start.4
  79.0 5.4 %collective-permute-done.refs_1_ = bf16[4,264,128]{2,1,0:T(8,128)(2,1)S(1)} collective-permute-done((bf16[4,264,128]{2,1,0:T(8,128)(2,1)}, bf16[4,264,128]{2,1,0:T(8,128)(2,1)S(1)}, u32[]{:S(2)}, u32[]{:S(2)}) %collective-permute-start) | collective-permute-done | bytes 270368 | tf_op jit(solution)/shard_map/ppermute | solution.py:269
  84.4 0.6 collective-permute-start.5
  85.0 1.5 constant_dynamic-slice_fusion.w_ref
  86.5 1.8 %collective-permute-done.1.refs_2_ = bf16[4,264,128]{2,1,0:T(8,128)(2,1)S(1)} collective-permute-done((bf16[4,264,128]{2,1,0:T(8,128)(2,1)}, bf16[4,264,128]{2,1,0:T(8,128)(2,1)S(1)}, u32[]{:S(2)}, u32[]{:S(2)}) %collective-permute-start.1) | collective-permute-done | bytes 270368 | tf_op jit(solution)/shard_map/ppermute | solution.py:269
  88.3 0.0 collective-permute-done.2.refs_3_
  88.3 0.3 collective-permute-done.3.refs_5_
  88.5 0.0 collective-permute-done.4.refs_6_
  88.5 4.4 %collective-permute-done.5.refs_7_ = bf16[4,264,128]{2,1,0:T(8,128)(2,1)} collective-permute-done((bf16[4,264,128]{2,1,0:T(8,128)(2,1)}, bf16[4,264,128]{2,1,0:T(8,128)(2,1)}, u32[]{:S(2)}, u32[]{:S(2)}) %collective-permute-start.5) | collective-permute-done | bytes 270368 | tf_op jit(solution)/shard_map/ppermute | solution.py:269
  92.9 0.0 copy-done.2
  92.9 0.0 copy-done.3
  93.0 2.6 %add.108 = (bf16[264,128]{1,0:T(8,128)(2,1)}, bf16[264,128]{1,0:T(8,128)(2,1)}, bf16[264,128]{1,0:T(8,128)(2,1)}, bf16[264,128]{1,0:T(8,128)(2,1)}, bf16[264,128...) custom-call(s32[3]{0:T(128)} %pad_add_fusion.at_ref, ...), custom_call_target="tpu_custom_call" | custom-call | tf_op jit(solution)/shard_map/add/pallas_call | solution.py:270
  95.6 0.4 collective-permute-start.10
  96.0 1.6 %collective-permute-start.11 = (bf16[264,128]{1,0:T(8,128)(2,1)}, bf16[264,128]{1,0:T(8,128)(2,1)S(1)}, u32[]{:S(2)}, u32[]{:S(2)}) collective-permute-start(bf16[264,128]{1,0:T(8,128)(2,1)} %get-tuple-element.35), channel_id=1, source_target_pairs={{0,12},{1,13},{2,14},{3,15},{4,0},{5,1},{6,2},{7,3},{8,4},{9,5},{1... | collective-permute-start | bytes 202760 | tf_op jit(solution)/shard_map/ppermute | solution.py:281
  97.6 0.6 collective-permute-start.6
  98.2 2.5 %collective-permute-start.7 = (bf16[264,128]{1,0:T(8,128)(2,1)}, bf16[264,128]{1,0:T(8,128)(2,1)S(1)}, u32[]{:S(2)}, u32[]{:S(2)}) collective-permute-start(bf16[264,128]{1,0:T(8,128)(2,1)} %get-tuple-element.30), channel_id=1, source_target_pairs={{0,2},{1,3},{2,0},{3,1},{4,6},{5,7},{6,4},{7,5},{8,10},{9,11},{10,... | collective-permute-start | bytes 202760 | tf_op jit(solution)/shard_map/ppermute | solution.py:281
  100.7 1.1 collective-permute-start.8
  101.9 0.0 collective-permute-done.10.refs_6_
  101.9 0.8 collective-permute-start.9
  102.7 0.6 reshape.158.ids_ref
  103.3 0.0 collective-permute-done.11.refs_7_
  103.3 0.0 collective-permute-done.6.refs_1_
  103.3 0.9 collective-permute-done.7.refs_2_
  104.2 1.0 collective-permute-done.8.refs_3_
  105.2 2.6 %collective-permute-done.9.refs_5_ = bf16[264,128]{1,0:T(8,128)(2,1)S(1)} collective-permute-done((bf16[264,128]{1,0:T(8,128)(2,1)}, bf16[264,128]{1,0:T(8,128)(2,1)S(1)}, u32[]{:S(2)}, u32[]{:S(2)}) %collective-permute-start.9) | collective-permute-done | bytes 67616 | tf_op jit(solution)/shard_map/ppermute | solution.py:281
  107.9 0.0 copy-done.7
  107.9 0.6 copy-done.12
  108.5 9.8 %prompt.1 = (bf16[32,64,256]{2,1,0:T(8,128)(2,1)}, bf16[32,64,256]{2,1,0:T(8,128)(2,1)}) custom-call(s32[32]{0:T(128)} %reshape.158.ids_ref, bf16[16,264,256]{2,1,0:T(8,128)(2,1)} %copy-done, bf16[2,128,128]{2,1,0:T(8,128)(2,1)} %constant_dynamic-slice_fusion.w_ref, bf16[264,128]{1,0:T(8,128)(2,1)} %get-tuple-element.28.refs_0_, bf16[264,128]{1,0:T(8,128)(2,1)} %copy-done.9, ...), custom_call_target="tpu_custom_call" | custom-call | tf_op jit(solution)/shard_map/prompt/pallas_call | solution.py:303
  118.2 0.8 fusion.len_ref
  119.0 0.0 all-to-all-done.1.part_ref
  119.0 5.1 %combine.1 = bf16[2048,256]{1,0:T(8,128)(2,1)} custom-call(s32[32]{0:T(128)} %reshape.158.ids_ref, s32[16]{0:T(128)} %fusion.len_ref, bf16[16,264,256]{2,1,0:T(8,128)(2,1)} %all-to-all-done.1.part_ref, bf16[32,64,256]{2,1,0:T(8,128)(2,1)} %get-tuple-element.36.num_ref, bf16[32,64,256]{2,1,0:T(8,128)(2,1)} %get-tuple-element.37.den_ref), custom_call_target="tpu_custom_call" | custom-call | tf_op jit(solution)/shard_map/combine/pallas_call | solution.py:320
  124.1 4.5 %all-to-all-start.2 = ((bf16[16,128,256]{2,1,0:T(8,128)(2,1)}), bf16[16,128,256]{2,1,0:T(8,128)(2,1)S(1)}, u32[]{:S(2)}, u32[]{:S(2)}) async-start(bf16[16,128,256]{2,1,0:T(8,128)(2,1)} %bitcast.48), calls=%async_computation.2 | async-start | bytes 2097152 | tf_op jit(solution)/shard_map/all_to_all | solution.py:334
  128.7 0.7 fusion.2
  130.0 0.6 multiply_reduce_fusion
  130.6 0.0 collective-permute-start.12
  130.6 0.2 select_reduce_fusion.1
  130.8 1.2 collective-permute-done.12
  133.3 3.3 %collective-permute-start.13 = (f32[1,1]{1,0:T(1,128)}, f32[1,1]{1,0:T(1,128)}, u32[]{:S(2)}, u32[]{:S(2)}) collective-permute-start(f32[1,1]{1,0:T(1,128)} %add.85), channel_id=1, source_target_pairs={{0,32},{16,48},{32,0},{48,16},{64,96},{80,112},{96,64},{112,80},{1... | collective-permute-start | bytes 20 | tf_op jit(solution)/shard_map/ppermute | solution.py:348
  136.6 0.5 collective-permute-done.13
  137.7 4.6 %collective-permute-start.14 = (f32[1,1]{1,0:T(1,128)}, f32[1,1]{1,0:T(1,128)}, u32[]{:S(2)}, u32[]{:S(2)}) collective-permute-start(f32[1,1]{1,0:T(1,128)} %add.86), channel_id=1, source_target_pairs={{0,64},{16,80},{32,96},{48,112},{64,0},{80,16},{96,32},{112,48},{1... | collective-permute-start | bytes 20 | tf_op jit(solution)/shard_map/ppermute | solution.py:348
  142.3 0.4 collective-permute-done.14
  143.3 8.2 %collective-permute-start.15 = (f32[1,1]{1,0:T(1,128)}, f32[1,1]{1,0:T(1,128)}, u32[]{:S(2)}, u32[]{:S(2)}) collective-permute-start(f32[1,1]{1,0:T(1,128)} %add.87), channel_id=1, source_target_pairs={{0,128},{16,144},{32,160},{48,176},{64,192},{80,208},{96,224},{112... | collective-permute-start | bytes 20 | tf_op jit(solution)/shard_map/ppermute | solution.py:348
  151.5 0.4 collective-permute-done.15
  152.6 0.1 divide_reduce_fusion
  152.7 0.2 select_reduce_fusion
  152.9 0.1 compare_select_fusion
  152.9 0.6 select_n.63
  153.5 0.0 all-to-all-done.2.a_ref
  153.5 1.0 copy-done.1
  154.5 3.4 %place.1 = bf16[128,4096]{1,0:T(8,128)(2,1)} custom-call(bf16[16,128,256]{2,1,0:T(8,128)(2,1)} %copy-done.1), custom_call_target="tpu_custom_call" | custom-call | tf_op jit(solution)/shard_map/place/pallas_call | solution.py:335
  (31 shorter events, 0.1 us)
Async XLA Ops:
  7.0 37.2 %all-to-all-start = ((bf16[16,264,256]{2,1,0:T(8,128)(2,1)}), bf16[16,264,256]{2,1,0:T(8,128)(2,1)S(1)}, u32[]{:S(2)}, u32[]{:S(2)}) async-start(bf16[16,264,256]{2,1,0:T(8,128)(2,1)} %spread.1), calls=%async_computation | async-start | bytes 4325376 | tf_op jit(solution)/shard_map/all_to_all | solution.py:219
  44.3 57.6 %copy-start = (bf16[16,264,256]{2,1,0:T(8,128)(2,1)}, bf16[16,264,256]{2,1,0:T(8,128)(2,1)S(1)}, u32[]{:S(2)}) copy-start(bf16[16,264,256]{2,1,0:T(8,128)(2,1)S(1)} %all-to-all-done.q_ref) | copy-start | bytes 6488068
  44.3 74.7 %all-to-all-start.1 = ((bf16[16,264,256]{2,1,0:T(8,128)(2,1)}), bf16[16,264,256]{2,1,0:T(8,128)(2,1)}, u32[]{:S(2)}, u32[]{:S(2)}) async-start(bf16[16,264,256]{2,1,0:T(8,128)(2,1)} %intra.3), calls=%async_computation.1 | async-start | bytes 4325376 | tf_op jit(solution)/shard_map/all_to_all | solution.py:297
  70.7 13.7 %collective-permute-start = (bf16[4,264,128]{2,1,0:T(8,128)(2,1)}, bf16[4,264,128]{2,1,0:T(8,128)(2,1)S(1)}, u32[]{:S(2)}, u32[]{:S(2)}) collective-permute-start(bf16[4,264,128]{2,1,0:T(8,128)(2,1)} %get-tuple-element.21), channel_id=1, source_target_pairs={{0,4},{1,5},{2,6},{3,7},{4,8},{5,9},{6,10},{7,11},{8,12},{9,13},{1... | collective-permute-start | bytes 811016 | tf_op jit(solution)/shard_map/ppermute | solution.py:269
  72.3 16.0 %collective-permute-start.1 = (bf16[4,264,128]{2,1,0:T(8,128)(2,1)}, bf16[4,264,128]{2,1,0:T(8,128)(2,1)S(1)}, u32[]{:S(2)}, u32[]{:S(2)}) collective-permute-start(bf16[4,264,128]{2,1,0:T(8,128)(2,1)} %get-tuple-element.22), channel_id=1, source_target_pairs={{0,8},{1,9},{2,10},{3,11},{4,12},{5,13},{6,14},{7,15},{8,0},{9,1},... | collective-permute-start | bytes 811016 | tf_op jit(solution)/shard_map/ppermute | solution.py:269
  74.9 13.3 %collective-permute-start.2 = (bf16[4,264,128]{2,1,0:T(8,128)(2,1)}, bf16[4,264,128]{2,1,0:T(8,128)(2,1)S(1)}, u32[]{:S(2)}, u32[]{:S(2)}) collective-permute-start(bf16[4,264,128]{2,1,0:T(8,128)(2,1)} %get-tuple-element.23), channel_id=1, source_target_pairs={{0,12},{1,13},{2,14},{3,15},{4,0},{5,1},{6,2},{7,3},{8,4},{9,5},{1... | collective-permute-start | bytes 811016 | tf_op jit(solution)/shard_map/ppermute | solution.py:269
  76.4 12.1 %collective-permute-start.3 = (bf16[4,264,128]{2,1,0:T(8,128)(2,1)}, bf16[4,264,128]{2,1,0:T(8,128)(2,1)S(1)}, u32[]{:S(2)}, u32[]{:S(2)}) collective-permute-start(bf16[4,264,128]{2,1,0:T(8,128)(2,1)} %get-tuple-element.25), channel_id=1, source_target_pairs={{0,1},{1,2},{2,3},{3,0},{4,5},{5,6},{6,7},{7,4},{8,9},{9,10},{10,1... | collective-permute-start | bytes 811016 | tf_op jit(solution)/shard_map/ppermute | solution.py:269
  77.9 10.7 %collective-permute-start.4 = (bf16[4,264,128]{2,1,0:T(8,128)(2,1)}, bf16[4,264,128]{2,1,0:T(8,128)(2,1)S(1)}, u32[]{:S(2)}, u32[]{:S(2)}) collective-permute-start(bf16[4,264,128]{2,1,0:T(8,128)(2,1)} %get-tuple-element.26), channel_id=1, source_target_pairs={{0,2},{1,3},{2,0},{3,1},{4,6},{5,7},{6,4},{7,5},{8,10},{9,11},{10,... | collective-permute-start | bytes 811016 | tf_op jit(solution)/shard_map/ppermute | solution.py:269
  84.4 8.5 %copy-start.2 = (bf16[4,264,128]{2,1,0:T(8,128)(2,1)}, bf16[4,264,128]{2,1,0:T(8,128)(2,1)S(1)}, u32[]{:S(2)}) copy-start(bf16[4,264,128]{2,1,0:T(8,128)(2,1)S(1)} %collective-permute-done.refs_1_) | copy-start | bytes 811012
  84.4 8.5 %collective-permute-start.5 = (bf16[4,264,128]{2,1,0:T(8,128)(2,1)}, bf16[4,264,128]{2,1,0:T(8,128)(2,1)}, u32[]{:S(2)}, u32[]{:S(2)}) collective-permute-start(bf16[4,264,128]{2,1,0:T(8,128)(2,1)} %get-tuple-element.27), channel_id=1, source_target_pairs={{0,3},{1,0},{2,1},{3,2},{4,7},{5,4},{6,5},{7,6},{8,11},{9,8},{10,9... | collective-permute-start | bytes 811016 | tf_op jit(solution)/shard_map/ppermute | solution.py:269
  88.3 4.7 %copy-start.3 = (bf16[4,264,128]{2,1,0:T(8,128)(2,1)}, bf16[4,264,128]{2,1,0:T(8,128)(2,1)S(1)}, u32[]{:S(2)}) copy-start(bf16[4,264,128]{2,1,0:T(8,128)(2,1)S(1)} %collective-permute-done.1.refs_2_) | copy-start | bytes 811012
  88.3 4.7 %copy-start.4 = (bf16[4,264,128]{2,1,0:T(8,128)(2,1)}, bf16[4,264,128]{2,1,0:T(8,128)(2,1)S(1)}, u32[]{:S(2)}) copy-start(bf16[4,264,128]{2,1,0:T(8,128)(2,1)S(1)} %collective-permute-done.2.refs_3_) | copy-start | bytes 811012
  88.5 4.4 %copy-start.5 = (bf16[4,264,128]{2,1,0:T(8,128)(2,1)}, bf16[4,264,128]{2,1,0:T(8,128)(2,1)S(1)}, u32[]{:S(2)}) copy-start(bf16[4,264,128]{2,1,0:T(8,128)(2,1)S(1)} %collective-permute-done.3.refs_5_) | copy-start | bytes 811012
  88.5 4.4 %copy-start.6 = (bf16[4,264,128]{2,1,0:T(8,128)(2,1)}, bf16[4,264,128]{2,1,0:T(8,128)(2,1)S(1)}, u32[]{:S(2)}) copy-start(bf16[4,264,128]{2,1,0:T(8,128)(2,1)S(1)} %collective-permute-done.4.refs_6_) | copy-start | bytes 811012
  95.6 6.3 %collective-permute-start.10 = (bf16[264,128]{1,0:T(8,128)(2,1)}, bf16[264,128]{1,0:T(8,128)(2,1)S(1)}, u32[]{:S(2)}, u32[]{:S(2)}) collective-permute-start(bf16[264,128]{1,0:T(8,128)(2,1)} %get-tuple-element.34), channel_id=1, source_target_pairs={{0,8},{1,9},{2,10},{3,11},{4,12},{5,13},{6,14},{7,15},{8,0},{9,1},... | collective-permute-start | bytes 202760 | tf_op jit(solution)/shard_map/ppermute | solution.py:281
  96.0 7.3 %collective-permute-start.11 = (bf16[264,128]{1,0:T(8,128)(2,1)}, bf16[264,128]{1,0:T(8,128)(2,1)S(1)}, u32[]{:S(2)}, u32[]{:S(2)}) collective-permute-start(bf16[264,128]{1,0:T(8,128)(2,1)} %get-tuple-element.35), channel_id=1, source_target_pairs={{0,12},{1,13},{2,14},{3,15},{4,0},{5,1},{6,2},{7,3},{8,4},{9,5},{1... | collective-permute-start | bytes 202760 | tf_op jit(solution)/shard_map/ppermute | solution.py:281
  97.6 5.7 %collective-permute-start.6 = (bf16[264,128]{1,0:T(8,128)(2,1)}, bf16[264,128]{1,0:T(8,128)(2,1)S(1)}, u32[]{:S(2)}, u32[]{:S(2)}) collective-permute-start(bf16[264,128]{1,0:T(8,128)(2,1)} %get-tuple-element.29), channel_id=1, source_target_pairs={{0,1},{1,2},{2,3},{3,0},{4,5},{5,6},{6,7},{7,4},{8,9},{9,10},{10,1... | collective-permute-start | bytes 202760 | tf_op jit(solution)/shard_map/ppermute | solution.py:281
  98.2 6.0 %collective-permute-start.7 = (bf16[264,128]{1,0:T(8,128)(2,1)}, bf16[264,128]{1,0:T(8,128)(2,1)S(1)}, u32[]{:S(2)}, u32[]{:S(2)}) collective-permute-start(bf16[264,128]{1,0:T(8,128)(2,1)} %get-tuple-element.30), channel_id=1, source_target_pairs={{0,2},{1,3},{2,0},{3,1},{4,6},{5,7},{6,4},{7,5},{8,10},{9,11},{10,... | collective-permute-start | bytes 202760 | tf_op jit(solution)/shard_map/ppermute | solution.py:281
  100.7 4.5 %collective-permute-start.8 = (bf16[264,128]{1,0:T(8,128)(2,1)}, bf16[264,128]{1,0:T(8,128)(2,1)S(1)}, u32[]{:S(2)}, u32[]{:S(2)}) collective-permute-start(bf16[264,128]{1,0:T(8,128)(2,1)} %get-tuple-element.31), channel_id=1, source_target_pairs={{0,3},{1,0},{2,1},{3,2},{4,7},{5,4},{6,5},{7,6},{8,11},{9,8},{10,9... | collective-permute-start | bytes 202760 | tf_op jit(solution)/shard_map/ppermute | solution.py:281
  101.9 6.0 %copy-start.7 = (bf16[264,128]{1,0:T(8,128)(2,1)}, bf16[264,128]{1,0:T(8,128)(2,1)S(1)}, u32[]{:S(2)}) copy-start(bf16[264,128]{1,0:T(8,128)(2,1)S(1)} %collective-permute-done.10.refs_6_) | copy-start | bytes 202756
  101.9 6.0 %collective-permute-start.9 = (bf16[264,128]{1,0:T(8,128)(2,1)}, bf16[264,128]{1,0:T(8,128)(2,1)S(1)}, u32[]{:S(2)}, u32[]{:S(2)}) collective-permute-start(bf16[264,128]{1,0:T(8,128)(2,1)} %get-tuple-element.33), channel_id=1, source_target_pairs={{0,4},{1,5},{2,6},{3,7},{4,8},{5,9},{6,10},{7,11},{8,12},{9,13},{1... | collective-permute-start | bytes 202760 | tf_op jit(solution)/shard_map/ppermute | solution.py:281
  103.3 4.6 %copy-start.8 = (bf16[264,128]{1,0:T(8,128)(2,1)}, bf16[264,128]{1,0:T(8,128)(2,1)S(1)}, u32[]{:S(2)}) copy-start(bf16[264,128]{1,0:T(8,128)(2,1)S(1)} %collective-permute-done.11.refs_7_) | copy-start | bytes 202756
  103.3 4.6 %copy-start.9 = (bf16[264,128]{1,0:T(8,128)(2,1)}, bf16[264,128]{1,0:T(8,128)(2,1)S(1)}, u32[]{:S(2)}) copy-start(bf16[264,128]{1,0:T(8,128)(2,1)S(1)} %collective-permute-done.6.refs_1_) | copy-start | bytes 202756
  104.2 3.7 %copy-start.10 = (bf16[264,128]{1,0:T(8,128)(2,1)}, bf16[264,128]{1,0:T(8,128)(2,1)S(1)}, u32[]{:S(2)}) copy-start(bf16[264,128]{1,0:T(8,128)(2,1)S(1)} %collective-permute-done.7.refs_2_) | copy-start | bytes 202756
  105.2 2.7 %copy-start.11 = (bf16[264,128]{1,0:T(8,128)(2,1)}, bf16[264,128]{1,0:T(8,128)(2,1)S(1)}, u32[]{:S(2)}) copy-start(bf16[264,128]{1,0:T(8,128)(2,1)S(1)} %collective-permute-done.8.refs_3_) | copy-start | bytes 202756
  107.9 0.6 copy-start.12
  119.0 9.6 %copy-start.14 = (s32[1,2]{1,0:T(1,128)S(1)}, s32[1,2]{1,0:T(1,128)}, u32[]{:S(2)}) copy-start(s32[1,2]{1,0:T(1,128)} %param.18) | copy-start | bytes 28
  119.0 11.6 %copy-start.13 = (s32[16]{0:T(128)S(1)}, s32[16]{0:T(128)}, u32[]{:S(2)}) copy-start(s32[16]{0:T(128)} %fusion.len_ref) | copy-start | bytes 196
  124.1 29.4 %all-to-all-start.2 = ((bf16[16,128,256]{2,1,0:T(8,128)(2,1)}), bf16[16,128,256]{2,1,0:T(8,128)(2,1)S(1)}, u32[]{:S(2)}, u32[]{:S(2)}) async-start(bf16[16,128,256]{2,1,0:T(8,128)(2,1)} %bitcast.48), calls=%async_computation.2 | async-start | bytes 2097152 | tf_op jit(solution)/shard_map/all_to_all | solution.py:334
  130.6 1.4 collective-permute-start.12
  133.3 3.8 %collective-permute-start.13 = (f32[1,1]{1,0:T(1,128)}, f32[1,1]{1,0:T(1,128)}, u32[]{:S(2)}, u32[]{:S(2)}) collective-permute-start(f32[1,1]{1,0:T(1,128)} %add.85), channel_id=1, source_target_pairs={{0,32},{16,48},{32,0},{48,16},{64,96},{80,112},{96,64},{112,80},{1... | collective-permute-start | bytes 20 | tf_op jit(solution)/shard_map/ppermute | solution.py:348
  137.7 5.0 %collective-permute-start.14 = (f32[1,1]{1,0:T(1,128)}, f32[1,1]{1,0:T(1,128)}, u32[]{:S(2)}, u32[]{:S(2)}) collective-permute-start(f32[1,1]{1,0:T(1,128)} %add.86), channel_id=1, source_target_pairs={{0,64},{16,80},{32,96},{48,112},{64,0},{80,16},{96,32},{112,48},{1... | collective-permute-start | bytes 20 | tf_op jit(solution)/shard_map/ppermute | solution.py:348
  143.3 8.6 %collective-permute-start.15 = (f32[1,1]{1,0:T(1,128)}, f32[1,1]{1,0:T(1,128)}, u32[]{:S(2)}, u32[]{:S(2)}) collective-permute-start(f32[1,1]{1,0:T(1,128)} %add.87), channel_id=1, source_target_pairs={{0,128},{16,144},{32,160},{48,176},{64,192},{80,208},{96,224},{112... | collective-permute-start | bytes 20 | tf_op jit(solution)/shard_map/ppermute | solution.py:348
  153.5 1.0 copy-start.1

commit v3 on v2

v3 whole, which is shorter than its diff:
```python
import jax
import jax.numpy as jnp
from jax import lax
from jax.experimental import pallas as pl
from jax.experimental.pallas import tpu as pltpu
from jax.sharding import PartitionSpec as P


BLK = 64
SIDE = 4
EXTRA = 8
F32 = jnp.float32
BF16 = jnp.bfloat16
NT = (((1,), (1,)), ((), ()))
TN = (((0,), (0,)), ((), ()))
NN = (((1,), (0,)), ((), ()))


def mm(a, b, dims=NN):
    return lax.dot_general(a, b, dims, preferred_element_type=F32)


def feats(xs, ws):
    us = [mm(w.T, x, NT) for x, w in zip(xs, ws)]
    top = [jnp.max(u, axis=0, keepdims=True) for u in us]
    low = [jnp.min(u, axis=0, keepdims=True) for u in us]
    ep = [jnp.exp(u - m) for u, m in zip(us, top)]
    en = [jnp.exp(m - u) for u, m in zip(us, low)]
    rp = [1.0 / jnp.sum(e, axis=0, keepdims=True) for e in ep]
    rn = [1.0 / jnp.sum(e, axis=0, keepdims=True) for e in en]
    return [
        jnp.concatenate([(a * b).astype(BF16), (c * d).astype(BF16)], axis=0)
        for a, b, c, d in zip(ep, rp, en, rn)
    ]


def spread_kernel(own_ref, len_ref, rew_ref, q_ref, o_ref):
    length, width = q_ref.shape[0], o_ref.shape[2]
    part = width // 8
    slots = own_ref.shape[1]
    col = lax.broadcasted_iota(jnp.int32, (EXTRA, width), 1)
    r = jnp.where(col < part, 0.0, rew_ref[0, 0])
    for i in range(slots):
        r = jnp.where(col == i, own_ref[0, i].astype(F32), r)
    r = jnp.where(col == slots, len_ref[0, 0].astype(F32), r)
    r1 = r.astype(BF16).astype(F32)
    r2 = (r - r1).astype(BF16).astype(F32)
    r3 = r - r1 - r2
    tabs = jnp.where(col < 2 * part, r1, jnp.where(col < 3 * part, r2, r3)).astype(BF16)
    for o in range(o_ref.shape[0]):
        o_ref[o, :length, :] = q_ref[:, o * width : (o + 1) * width]
        o_ref[o, length:, :] = tabs


def state_kernel(n_ref, k_ref, v_ref, w_ref, *outs):
    rows, width = k_ref.shape[0], w_ref.shape[1]
    half = w_ref.shape[2]
    me = lax.axis_index("dp")
    mx, my, j = me // SIDE, me % SIDE, pl.program_id(0)
    keep = lax.broadcasted_iota(jnp.int32, (1, rows), 1) + me * rows < n_ref[0]
    rid = lax.broadcasted_iota(jnp.int32, (EXTRA, rows), 0)
    heads = [2 * ((mx + s) % SIDE * SIDE + j) for s in range(SIDE)]
    heads += [2 * (j * SIDE + (my + s) % SIDE) + 1 for s in range(SIDE)]
    cols = [pl.ds(pl.multiple_of(h * width, width), width) for h in heads]
    phis = feats([k_ref[:, c] for c in cols], [w_ref[h] for h in heads])
    for phi, c, o_ref in zip(phis, cols, outs):
        phi = jnp.where(keep, phi, jnp.zeros((), BF16))
        o_ref[0, : 2 * half, :] = mm(phi, v_ref[:, c]).astype(BF16)
        tail = mm((rid == 0).astype(BF16), phi[:half], NT)
        tail = tail + mm((rid == 1).astype(BF16), phi[half:], NT)
        o_ref[0, 2 * half :, :] = tail.astype(BF16)


def add_kernel(*refs):
    ins, outs = refs[: 2 * SIDE], refs[2 * SIDE :]
    me = lax.axis_index("dp")
    for p in range(2):
        for s in range(SIDE):
            j = ((me // SIDE if p else me % SIDE) + s) % SIDE
            acc = ins[SIDE * p][j].astype(F32)
            for i in range(1, SIDE):
                acc = acc + ins[SIDE * p + i][j].astype(F32)
            outs[SIDE * p + s][...] = acc.astype(BF16)


def intra_kernel(q_ref, k_ref, v_ref, wq_ref, wk_ref, *rest):
    o_ref = rest[-1]
    length, width = q_ref.shape[0], wq_ref.shape[1]
    half = length // 2
    many = wq_ref.shape[0]
    cols = [slice(h * width, (h + 1) * width) for h in range(many)]
    phis = feats(
        [q_ref[:, c] for c in cols] + [k_ref[:, c] for c in cols],
        [wq_ref[h] for h in range(many)] + [wk_ref[h] for h in range(many)],
    )
    scores = [mm(phis[h].T, phis[many + h]) for h in range(many)]
    t = lax.broadcasted_iota(jnp.int32, (length, length), 0)
    s = lax.broadcasted_iota(jnp.int32, (length, length), 1)
    scores = [jnp.where(s <= t, x, 0.0) for x in scores]
    rid = lax.broadcasted_iota(jnp.int32, (EXTRA, half), 0)
    ones = jnp.ones((EXTRA, length), BF16)
    for h, score in enumerate(scores):
        to = slice(h % 2 * width, (h % 2 + 1) * width)
        num = mm(score.astype(BF16), v_ref[:, cols[h]])
        o_ref[h // 2, :length, to] = num.astype(BF16)
        fold = score[:, :half] + score[:, half:]
        hi = fold.astype(BF16)
        lo = (fold - hi.astype(F32)).astype(BF16)
        den = mm(ones, jnp.concatenate([hi, lo], axis=1), NT)
        den = jnp.where(rid < 2, den[:, :half], den[:, half:])
        dhi = den.astype(BF16).astype(F32)
        den = jnp.where(rid % 2 == 1, den - dhi, dhi)
        o_ref[h // 2, length:, to] = den.astype(BF16)


def prompt_kernel(ids_ref, q_ref, w_ref, *refs):
    parts = refs[: 2 * SIDE]
    num_ref, den_ref, s_ref, t_ref = refs[2 * SIDE :]
    i = pl.program_id(0)
    width = w_ref.shape[1]
    full = 2 * w_ref.shape[2]
    many = num_ref.shape[0]

    @pl.when(i == 0)
    def _():
        for h in range(2):
            acc = parts[SIDE * h][...].astype(F32)
            for d in range(1, SIDE):
                acc = acc + parts[SIDE * h + d][...].astype(F32)
            s_ref[h] = acc[:full].astype(BF16)
            row = jnp.concatenate([acc[full : full + 1], acc[full + 1 : full + 2]], axis=1)
            t_ref[h] = jnp.broadcast_to(row, t_ref.shape[1:]).astype(BF16)

    pieces = q_ref.shape[1] // BLK
    xs = []
    for g in range(0, many, 4):
        rows = []
        for j in range(g, g + 4):
            b = ids_ref[i * many + j]
            rows.append(q_ref[b // pieces, pl.ds(pl.multiple_of(b % pieces * BLK, BLK), BLK), :])
        xs.append(jnp.concatenate(rows, axis=0))
    cols = [slice(h * width, (h + 1) * width) for h in range(2)]
    units = [(g, h) for g in range(len(xs)) for h in range(2)]
    phis = feats([xs[g][:, cols[h]] for g, h in units], [w_ref[h] for g, h in units])
    phis = [phi.T for phi in phis]
    for phi, (g, h) in zip(phis, units):
        num = mm(phi, s_ref[h]).astype(BF16)
        den = mm(phi, t_ref[h], NT).astype(BF16)
        num_ref[4 * g : 4 * g + 4, :, cols[h]] = num.reshape(4, BLK, width)
        den_ref[4 * g : 4 * g + 4, :, cols[h]] = den.reshape(4, BLK, width)


def combine_kernel(ids_ref, len_ref, part_ref, num_ref, den_ref, o_ref):
    length = part_ref.shape[1] - EXTRA
    width = part_ref.shape[2] // 2
    pieces = length // BLK
    many = num_ref.shape[0]
    i = pl.program_id(0)
    rid = lax.broadcasted_iota(jnp.int32, (EXTRA, width), 0)
    row = lax.broadcasted_iota(jnp.int32, (BLK, 1), 0)
    for j in range(many):
        b = ids_ref[i * many + j]
        r, c = b // pieces, b % pieces
        pick = (rid // 2 == c // 2).astype(BF16)
        for h in range(2):
            cols = slice(h * width, (h + 1) * width)
            num = part_ref[r, pl.ds(pl.multiple_of(c * BLK, BLK), BLK), cols].astype(F32)
            den = mm(part_ref[r, length:, cols], pick, TN)
            den = jnp.where(c % 2 == 0, den[:BLK], den[BLK:])
            num = num_ref[j, :, cols].astype(F32) + num
            den = den_ref[j, :, cols].astype(F32) + den
            out = jnp.where(row < len_ref[r] - c * BLK, num / den, 0.0)
            o_ref[j * BLK : (j + 1) * BLK, cols] = out.astype(BF16)


def hop(dx, dy):
    return [
        (x * SIDE + y, (x + dx) % SIDE * SIDE + (y + dy) % SIDE)
        for x in range(SIDE)
        for y in range(SIDE)
    ]


def body(
    resp_q,
    resp_k,
    resp_v,
    prompt_k,
    prompt_v,
    prompt_len,
    resp_len,
    assign,
    rewards,
    feat_q,
    feat_k,
):
    dp = lax.axis_size("dp")
    groups = lax.axis_size("group")
    me = lax.axis_index("dp")
    heads, width, feat = feat_q.shape
    length = resp_q.shape[1]
    pieces = length // BLK
    slots = assign.shape[1]
    two = 2 * width
    tall = length + EXTRA
    q, k, v, pk, pv = resp_q[0], resp_k[0], resp_v[0], prompt_k[0], prompt_v[0]

    part = two // 8
    q_all = pl.pallas_call(
        spread_kernel,
        grid=(2,),
        in_specs=[pl.BlockSpec(memory_space=pltpu.SMEM)] * 3
        + [pl.BlockSpec((length, heads * width // 2), lambda o: (0, o))],
        out_specs=pl.BlockSpec((dp // 2, tall, two), lambda o: (o, 0, 0)),
        out_shape=jax.ShapeDtypeStruct((dp, tall, two), BF16),
        name="spread",
    )(assign, resp_len, rewards, q)
    q_all = lax.all_to_all(q_all, "dp", 0, 0, tiled=True)
    tabs = q_all[:, length, :].astype(F32)
    ids = tabs[:, :slots].astype(jnp.int32).reshape(-1)
    lens = tabs[:, slots].astype(jnp.int32)
    reward_all = tabs[:, part] + tabs[:, 2 * part] + tabs[:, 3 * part]

    srows = 2 * feat + EXTRA
    states = pl.pallas_call(
        state_kernel,
        grid=(SIDE,),
        in_specs=[
            pl.BlockSpec(memory_space=pltpu.SMEM),
            pl.BlockSpec(pk.shape, lambda j: (0, 0)),
            pl.BlockSpec(pv.shape, lambda j: (0, 0)),
            pl.BlockSpec(feat_k.shape, lambda j: (0, 0, 0)),
        ],
        out_specs=[pl.BlockSpec((1, srows, width), lambda j: (j, 0, 0))] * (2 * SIDE),
        out_shape=[jax.ShapeDtypeStruct((SIDE, srows, width), BF16)] * (2 * SIDE),
        name="state",
    )(prompt_len, pk, pv, feat_k)
    states = list(states)
    for p in range(2):
        for s in range(1, SIDE):
            i = SIDE * p + s
            states[i] = lax.ppermute(states[i], "dp", hop(s, 0) if p == 0 else hop(0, s))
    states = pl.pallas_call(
        add_kernel,
        in_specs=[pl.BlockSpec(memory_space=pltpu.VMEM)] * (2 * SIDE),
        out_shape=[jax.ShapeDtypeStruct((srows, width), BF16)] * (2 * SIDE),
        name="add",
    )(*states)
    states = list(states)
    for p in range(2):
        for s in range(1, SIDE):
            i = SIDE * p + s
            states[i] = lax.ppermute(states[i], "dp", hop(0, s) if p == 0 else hop(s, 0))

    inner = ()
    for p in range(2):
        at = p * (heads // 8)
        specs = [pl.BlockSpec((length, 4 * width), lambda o, at=at: (0, o + at))] * 3
        specs += [pl.BlockSpec((4, width, feat), lambda o, at=at: (o + at, 0, 0))] * 2
        inner = pl.pallas_call(
            intra_kernel,
            grid=(heads // 8,),
            in_specs=specs + [pl.BlockSpec(memory_space=pl.ANY)] * p,
            out_specs=pl.BlockSpec((2, tall, two), lambda o, at=at: (o + at, 0, 0)),
            out_shape=jax.ShapeDtypeStruct((dp, tall, two), BF16),
            input_output_aliases={5: 0} if p else {},
            name="intra",
        )(q, k, v, feat_q, feat_k, *inner)
        inner = (inner,)
    inner = lax.all_to_all(inner[0], "dp", 0, 0, tiled=True)

    total = dp * slots
    many = 8
    own_w = lax.dynamic_slice_in_dim(feat_q, 2 * me, 2, 0)
    row_spec = pl.BlockSpec((many, BLK, two), lambda i: (i, 0, 0))
    num, den = pl.pallas_call(
        prompt_kernel,
        grid=(total // many,),
        in_specs=[
            pl.BlockSpec(memory_space=pltpu.SMEM),
            pl.BlockSpec((dp, tall, two), lambda i: (0, 0, 0)),
            pl.BlockSpec((2, width, feat), lambda i: (0, 0, 0)),
        ]
        + [pl.BlockSpec((srows, width), lambda i: (0, 0))] * (2 * SIDE),
        out_specs=[row_spec, row_spec],
        out_shape=[jax.ShapeDtypeStruct((total, BLK, two), BF16)] * 2,
        scratch_shapes=[
            pltpu.VMEM((2, 2 * feat, width), BF16),
            pltpu.VMEM((2, width, 2 * feat), BF16),
        ],
        name="prompt",
    )(ids, q_all, own_w, *states)
    out = pl.pallas_call(
        combine_kernel,
        grid=(total // 8,),
        in_specs=[
            pl.BlockSpec(memory_space=pltpu.SMEM),
            pl.BlockSpec(memory_space=pltpu.SMEM),
            pl.BlockSpec((dp, tall, two), lambda i: (0, 0, 0)),
            pl.BlockSpec((8, BLK, two), lambda i: (i, 0, 0)),
            pl.BlockSpec((8, BLK, two), lambda i: (i, 0, 0)),
        ],
        out_specs=pl.BlockSpec((8 * BLK, two), lambda i: (i, 0)),
        out_shape=jax.ShapeDtypeStruct((total * BLK, two), BF16),
        name="combine",
    )(ids, lens, inner, num, den)
    out = lax.all_to_all(out.reshape(dp, slots * BLK, two), "dp", 0, 0, tiled=True)
    attn = jnp.swapaxes(out, 0, 1).reshape(1, slots * BLK, heads * width)

    centred = reward_all - jnp.sum(reward_all) / dp
    spread = jnp.sum(centred * centred).reshape(1, 1)
    step = 1
    while step < groups:
        total_sq = spread
        for i in range(1, 4):
            total_sq = total_sq + lax.ppermute(
                spread, "group", [(g, g ^ (step * i)) for g in range(groups)]
            )
        spread = total_sq
        step *= 4
    advantage = centred / jnp.sqrt(spread[0, 0] / (groups * dp) + 1e-06)
    own = assign[0]
    picker = (own // pieces)[:, None] == jnp.arange(dp)[None, :]
    slot_adv = jnp.sum(jnp.where(picker, advantage[None, :], 0.0), axis=1)
    slot_len = jnp.sum(jnp.where(picker, lens[None, :], 0), axis=1)
    positions = (own % pieces)[:, None] * BLK + jnp.arange(BLK)[None, :]
    token_adv = jnp.where(positions < slot_len[:, None], slot_adv[:, None], F32(0.0))
    return (attn, token_adv.reshape(1, slots * BLK))


def solution(mesh):
    return jax.shard_map(
        body,
        mesh=mesh,
        in_specs=(
            P("group", "dp", None),
            P("group", "dp", None),
            P("group", "dp", None),
            P("group", "dp", None),
            P("group", "dp", None),
            P("group"),
            P("group", "dp"),
            P("group", "dp"),
            P("group", "dp"),
            P(),
            P(),
        ),
        out_specs=(P("group", "dp", None), P("group", "dp")),
        check_vma=False,
    )
```

time: 161 us -> 150 us (0.932); the launches traced: 158 us -> 149 us
  Pallas kernels: 72.4 us -> 35.9 us
  waiting for transfers between devices: 19.7 us -> 45.2 us
  other arithmetic: 4.59 us -> 2.56 us
    pallas_call x6 -> x5, Pallas kernels: 57.5 us -> 24.8 us  [the longest x2 13.4 us: body(): pl.pallas_call(intra_kernel, grid=(heads // 8,), in_specs=specs + [pl.Blo...]
    all_to_all x1, waiting for transfers between devices: 0.8 us -> 16.5 us  [body(): q_all = lax.all_to_all(q_all, 'dp', 0, 0, tiled=True)]
    ppermute x6, waiting for transfers between devices: 11.9 us -> 22.9 us  [body(): lax.ppermute(states[i], 'dp', hop(s, 0) if p == 0 else hop(0, s))]
    pallas_call x1, Pallas kernels: 9.75 us -> 5.94 us  [body(): pl.pallas_call(prompt_kernel, grid=(total // many,), in_specs=[pl.BlockSp...]
    ppermute x6, starting transfers between devices: 7.05 us -> 9.08 us  [body(): lax.ppermute(states[i], 'dp', hop(0, s) if p == 0 else hop(s, 0))]
    all_to_all x1, starting transfers between devices: 4.52 us -> 6.36 us  [body(): lax.all_to_all(out.reshape(dp, slots * BLK, two), 'dp', 0, 0, tiled=True)]
    ppermute x4 -> x6, starting transfers between devices: 16.1 us -> 14.3 us  [body(): lax.ppermute(spread, 'group', [(g, g ^ step * i) for g in range(groups)])]
    ppermute x6, waiting for transfers between devices: 4.54 us -> 2.93 us  [body(): lax.ppermute(states[i], 'dp', hop(0, s) if p == 0 else hop(s, 0))]
  transfers between devices with their start and end apart: 19 -> 21, of which waited for: 12 -> 9; matrix products, arithmetic and copies ran while one was open for 4% -> 4% of each run, Pallas kernels for 38% -> 19%
where the time goes in v3:
time: 150 us; the launch traced here: 149 us
  starting transfers between devices  51.8 us (35%)
  waiting for transfers between devices  45.2 us (30%)
  Pallas kernels  35.9 us (24%)
  between operations  7.97 us (5%)
  local copies, waits for them, and re-layouts  5.21 us (3%)
  other arithmetic  2.56 us (2%)
    ppermute x6, waiting for transfers between devices, body(): lax.ppermute(states[i], 'dp', hop(s, 0) if p == 0 else hop(0, s))  22.9 us
    all_to_all x1, waiting for transfers between devices, body(): q_all = lax.all_to_all(q_all, 'dp', 0, 0, tiled=True)  16.5 us
    ppermute x6, starting transfers between devices, body(): lax.ppermute(spread, 'group', [(g, g ^ step * i) for g in range(groups)])  14.3 us
    pallas_call x2, Pallas kernels, body(): pl.pallas_call(intra_kernel, grid=(heads // 8,), in_specs=specs + [pl.Blo...  13.4 us
    ppermute x6, starting transfers between devices, body(): lax.ppermute(states[i], 'dp', hop(0, s) if p == 0 else hop(s, 0))  9.08 us
    ppermute x6, starting transfers between devices, body(): lax.ppermute(states[i], 'dp', hop(s, 0) if p == 0 else hop(0, s))  9.06 us
    all_to_all x1, starting transfers between devices, body(): q_all = lax.all_to_all(q_all, 'dp', 0, 0, tiled=True)  7.39 us
    all_to_all x1, starting transfers between devices, body(): lax.all_to_all(out.reshape(dp, slots * BLK, two), 'dp', 0, 0, tiled=True)  6.36 us
  transfers between devices with their start and end apart: 21, of which 9 were waited for; matrix products, arithmetic and copies ran while one was open for 4% of the time, Pallas kernels for 19%

profile of v3, /device:TPU:8, one launch (start us, length us, event | category | flops | bytes accessed | tf_op | source)
XLA Modules:
  0.0 148.7 jit_solution(5135377924680277852)
XLA Ops:
  1.9 2.7 %spread.1 = bf16[16,264,256]{2,1,0:T(8,128)(2,1)} custom-call(s32[1,2]{1,0:T(1,128)} %own_ref.1, s32[1,1]{1,0:T(1,128)S(6)} %copy.22.len_ref, f32[1,1]{1,0:T(1,128)S(6)} %copy.23.rew_ref, bf16[256,4096]{1,0:T(8,128)(2,1)} %bitcast.27), custom_call_target="tpu_custom_call" | custom-call | tf_op jit(solution)/shard_map/spread/pallas_call | solution.py:209
  4.6 7.4 %all-to-all-start = ((bf16[16,264,256]{2,1,0:T(8,128)(2,1)}), bf16[16,264,256]{2,1,0:T(8,128)(2,1)S(1)}, u32[]{:S(2)}, u32[]{:S(2)}) async-start(bf16[16,264,256]{2,1,0:T(8,128)(2,1)} %spread.1), calls=%async_computation | async-start | bytes 4325376 | tf_op jit(solution)/shard_map/all_to_all | solution.py:218
  12.0 6.7 %intra.2.rest_0_ = bf16[16,264,256]{2,1,0:T(8,128)(2,1)} custom-call(bf16[256,4096]{1,0:T(8,128)(2,1)} %bitcast.28, bf16[256,4096]{1,0:T(8,128)(2,1)} %bitcast.30, bf16[256,4096]{1,0:T(8,128)(2,1)} %bitcast.32, bf16[32,128,128]{2,1,0:T(8,128)(2,1)} %wq_ref.3, bf16[32,128,128]{2,1,0:T(8,128)(2,1)} %w_ref.1), custom_call_target="tpu_custom_call" | custom-call | tf_op jit(solution)/shard_map/intra/pallas_call | solution.py:260
  18.7 6.7 %intra.3 = bf16[16,264,256]{2,1,0:T(8,128)(2,1)} custom-call(bf16[256,4096]{1,0:T(8,128)(2,1)} %bitcast.29, bf16[256,4096]{1,0:T(8,128)(2,1)} %bitcast.31, bf16[256,4096]{1,0:T(8,128)(2,1)} %bitcast.33, bf16[32,128,128]{2,1,0:T(8,128)(2,1)} %wq_ref.3, bf16[32,128,128]{2,1,0:T(8,128)(2,1)} %w_ref.1, ...), custom_call_target="tpu_custom_call", output_to_operand_aliasing={{}: (5, {})} | custom-call | tf_op jit(solution)/shard_map/intra/pallas_call | solution.py:260
  25.4 16.5 %all-to-all-done.q_ref = bf16[16,264,256]{2,1,0:T(8,128)(2,1)S(1)} async-done(((bf16[16,264,256]{2,1,0:T(8,128)(2,1)}), bf16[16,264,256]{2,1,0:T(8,128)(2,1)S(1)}, u32[]{:S(2)}, u32[]{:S(2)}) %all-to-all-start) | async-done | bytes 2162720 | tf_op jit(solution)/shard_map/all_to_all | solution.py:218
  41.9 5.6 %all-to-all-start.1 = ((bf16[16,264,256]{2,1,0:T(8,128)(2,1)}), bf16[16,264,256]{2,1,0:T(8,128)(2,1)}, u32[]{:S(2)}, u32[]{:S(2)}) async-start(bf16[16,264,256]{2,1,0:T(8,128)(2,1)} %intra.3), calls=%async_computation.1 | async-start | bytes 4325376 | tf_op jit(solution)/shard_map/all_to_all | solution.py:270
  48.1 6.2 %state.1 = (bf16[4,264,128]{2,1,0:T(8,128)(2,1)}, bf16[4,264,128]{2,1,0:T(8,128)(2,1)}, bf16[4,264,128]{2,1,0:T(8,128)(2,1)}, bf16[4,264,128]{2,1,0:T(8,128)(2,1...) custom-call(s32[1]{0:T(128)S(6)} %copy.21.n_ref, ...), custom_call_target="tpu_custom_call" | custom-call | tf_op jit(solution)/shard_map/state/pallas_call | solution.py:225
  54.3 1.5 %collective-permute-start = (bf16[4,264,128]{2,1,0:T(8,128)(2,1)}, bf16[4,264,128]{2,1,0:T(8,128)(2,1)S(1)}, u32[]{:S(2)}, u32[]{:S(2)}) collective-permute-start(bf16[4,264,128]{2,1,0:T(8,128)(2,1)} %get-tuple-element.21), channel_id=1, source_target_pairs={{0,4},{1,5},{2,6},{3,7},{4,8},{5,9},{6,10},{7,11},{8,12},{9,13},{1... | collective-permute-start | bytes 811016 | tf_op jit(solution)/shard_map/ppermute | solution.py:242
  55.8 2.7 %collective-permute-start.1 = (bf16[4,264,128]{2,1,0:T(8,128)(2,1)}, bf16[4,264,128]{2,1,0:T(8,128)(2,1)S(1)}, u32[]{:S(2)}, u32[]{:S(2)}) collective-permute-start(bf16[4,264,128]{2,1,0:T(8,128)(2,1)} %get-tuple-element.22), channel_id=1, source_target_pairs={{0,8},{1,9},{2,10},{3,11},{4,12},{5,13},{6,14},{7,15},{8,0},{9,1},... | collective-permute-start | bytes 811016 | tf_op jit(solution)/shard_map/ppermute | solution.py:242
  58.5 1.4 collective-permute-start.2
  60.0 1.5 collective-permute-start.3
  61.4 1.2 collective-permute-start.4
  62.6 18.4 %collective-permute-done.refs_1_ = bf16[4,264,128]{2,1,0:T(8,128)(2,1)S(1)} collective-permute-done((bf16[4,264,128]{2,1,0:T(8,128)(2,1)}, bf16[4,264,128]{2,1,0:T(8,128)(2,1)S(1)}, u32[]{:S(2)}, u32[]{:S(2)}) %collective-permute-start) | collective-permute-done | bytes 270368 | tf_op jit(solution)/shard_map/ppermute | solution.py:242
  81.0 0.8 collective-permute-start.5
  81.7 1.5 constant_dynamic-slice_fusion.w_ref
  83.2 1.2 collective-permute-done.1.refs_2_
  84.4 0.0 collective-permute-done.2.refs_3_
  84.4 0.0 collective-permute-done.3.refs_5_
  84.4 0.0 copy-start.4
  84.4 0.0 collective-permute-done.4.refs_6_
  84.4 3.3 %collective-permute-done.5.refs_7_ = bf16[4,264,128]{2,1,0:T(8,128)(2,1)} collective-permute-done((bf16[4,264,128]{2,1,0:T(8,128)(2,1)}, bf16[4,264,128]{2,1,0:T(8,128)(2,1)}, u32[]{:S(2)}, u32[]{:S(2)}) %collective-permute-start.5) | collective-permute-done | bytes 270368 | tf_op jit(solution)/shard_map/ppermute | solution.py:242
  87.8 0.0 copy-done.3
  87.8 0.0 copy-done.4
  87.8 2.6 %add.106 = (bf16[264,128]{1,0:T(8,128)(2,1)}, bf16[264,128]{1,0:T(8,128)(2,1)}, bf16[264,128]{1,0:T(8,128)(2,1)}, bf16[264,128]{1,0:T(8,128)(2,1)}, bf16[264,128...) custom-call(bf16[4,264,128]{2,1,0:T(8,128)(2,1)} %get-tuple-element.20.refs_0_, ...), custom_call_target="tpu_custom_call" | custom-call | tf_op jit(solution)/shard_map/add/pallas_call | solution.py:243
  90.4 0.9 collective-permute-start.6
  91.3 2.0 %collective-permute-start.7 = (bf16[264,128]{1,0:T(8,128)(2,1)}, bf16[264,128]{1,0:T(8,128)(2,1)S(1)}, u32[]{:S(2)}, u32[]{:S(2)}) collective-permute-start(bf16[264,128]{1,0:T(8,128)(2,1)} %get-tuple-element.30), channel_id=1, source_target_pairs={{0,2},{1,3},{2,0},{3,1},{4,6},{5,7},{6,4},{7,5},{8,10},{9,11},{10,... | collective-permute-start | bytes 202760 | tf_op jit(solution)/shard_map/ppermute | solution.py:253
  93.2 2.5 %collective-permute-start.8 = (bf16[264,128]{1,0:T(8,128)(2,1)}, bf16[264,128]{1,0:T(8,128)(2,1)S(1)}, u32[]{:S(2)}, u32[]{:S(2)}) collective-permute-start(bf16[264,128]{1,0:T(8,128)(2,1)} %get-tuple-element.31), channel_id=1, source_target_pairs={{0,3},{1,0},{2,1},{3,2},{4,7},{5,4},{6,5},{7,6},{8,11},{9,8},{10,9... | collective-permute-start | bytes 202760 | tf_op jit(solution)/shard_map/ppermute | solution.py:253
  95.8 0.0 collective-permute-start.9
  95.8 2.2 %collective-permute-start.10 = (bf16[264,128]{1,0:T(8,128)(2,1)}, bf16[264,128]{1,0:T(8,128)(2,1)S(1)}, u32[]{:S(2)}, u32[]{:S(2)}) collective-permute-start(bf16[264,128]{1,0:T(8,128)(2,1)} %get-tuple-element.34), channel_id=1, source_target_pairs={{0,8},{1,9},{2,10},{3,11},{4,12},{5,13},{6,14},{7,15},{8,0},{9,1},... | collective-permute-start | bytes 202760 | tf_op jit(solution)/shard_map/ppermute | solution.py:253
  98.0 0.0 collective-permute-done.6.refs_1_
  98.0 1.5 %collective-permute-start.11 = (bf16[264,128]{1,0:T(8,128)(2,1)}, bf16[264,128]{1,0:T(8,128)(2,1)S(1)}, u32[]{:S(2)}, u32[]{:S(2)}) collective-permute-start(bf16[264,128]{1,0:T(8,128)(2,1)} %get-tuple-element.35), channel_id=1, source_target_pairs={{0,12},{1,13},{2,14},{3,15},{4,0},{5,1},{6,2},{7,3},{8,4},{9,5},{1... | collective-permute-start | bytes 202760 | tf_op jit(solution)/shard_map/ppermute | solution.py:253
  99.5 0.6 reshape.155.ids_ref
  100.1 0.0 collective-permute-done.7.refs_2_
  100.1 0.0 collective-permute-done.8.refs_3_
  100.1 2.1 %collective-permute-done.9.refs_5_ = bf16[264,128]{1,0:T(8,128)(2,1)S(1)} collective-permute-done((bf16[264,128]{1,0:T(8,128)(2,1)}, bf16[264,128]{1,0:T(8,128)(2,1)S(1)}, u32[]{:S(2)}, u32[]{:S(2)}) %collective-permute-start.9) | collective-permute-done | bytes 67616 | tf_op jit(solution)/shard_map/ppermute | solution.py:253
  102.2 0.0 collective-permute-done.10.refs_6_
  102.2 0.8 collective-permute-done.11.refs_7_
  103.1 0.6 copy-done.11
  103.7 5.9 %prompt.1 = (bf16[32,64,256]{2,1,0:T(8,128)(2,1)}, bf16[32,64,256]{2,1,0:T(8,128)(2,1)}) custom-call(s32[32]{0:T(128)} %reshape.155.ids_ref, bf16[16,264,256]{2,1,0:T(8,128)(2,1)} %copy-done, bf16[2,128,128]{2,1,0:T(8,128)(2,1)} %constant_dynamic-slice_fusion.w_ref, bf16[264,128]{1,0:T(8,128)(2,1)} %get-tuple-element.28.refs_0_, bf16[264,128]{1,0:T(8,128)(2,1)} %copy-done.6, ...), custom_call_target="tpu_custom_call" | custom-call | tf_op jit(solution)/shard_map/prompt/pallas_call | solution.py:276
  109.6 0.7 fusion.len_ref
  110.3 0.0 all-to-all-done.1.part_ref
  110.3 5.1 %combine.1 = bf16[2048,256]{1,0:T(8,128)(2,1)} custom-call(s32[32]{0:T(128)} %reshape.155.ids_ref, s32[16]{0:T(128)} %fusion.len_ref, bf16[16,264,256]{2,1,0:T(8,128)(2,1)} %all-to-all-done.1.part_ref, bf16[32,64,256]{2,1,0:T(8,128)(2,1)} %get-tuple-element.36.num_ref, bf16[32,64,256]{2,1,0:T(8,128)(2,1)} %get-tuple-element.37.den_ref), custom_call_target="tpu_custom_call" | custom-call | tf_op jit(solution)/shard_map/combine/pallas_call | solution.py:293
  115.4 6.4 %all-to-all-start.2 = ((bf16[16,128,256]{2,1,0:T(8,128)(2,1)}), bf16[16,128,256]{2,1,0:T(8,128)(2,1)S(1)}, u32[]{:S(2)}, u32[]{:S(2)}) async-start(bf16[16,128,256]{2,1,0:T(8,128)(2,1)} %bitcast.35), calls=%async_computation.2 | async-start | bytes 2097152 | tf_op jit(solution)/shard_map/all_to_all | solution.py:307
  121.8 0.7 fusion.2
  123.1 0.6 multiply_reduce_fusion
  123.8 0.0 collective-permute-start.14
  123.8 1.9 %collective-permute-start.13 = (f32[1,1]{1,0:T(1,128)}, f32[1,1]{1,0:T(1,128)}, u32[]{:S(2)}, u32[]{:S(2)}) collective-permute-start(f32[1,1]{1,0:T(1,128)} %bitcast.8), channel_id=1, source_target_pairs={{0,32},{16,48},{32,0},{48,16},{64,96},{80,112},{96,64},{112,80},{1... | collective-permute-start | bytes 20 | tf_op jit(solution)/shard_map/ppermute | solution.py:316
  125.7 0.1 collective-permute-start.12
  125.8 0.2 select_reduce_fusion.1
  126.0 1.0 collective-permute-done.12
  128.3 0.0 collective-permute-done.13
  128.9 0.0 collective-permute-done.14
  129.6 7.3 %collective-permute-start.17 = (f32[1,1]{1,0:T(1,128)}, f32[1,1]{1,0:T(1,128)}, u32[]{:S(2)}, u32[]{:S(2)}) collective-permute-start(f32[1,1]{1,0:T(1,128)} %add.87), channel_id=1, source_target_pairs={{0,192},{16,208},{32,224},{48,240},{64,128},{80,144},{96,160},{112... | collective-permute-start | bytes 20 | tf_op jit(solution)/shard_map/ppermute | solution.py:316
  136.9 2.2 %collective-permute-start.16 = (f32[1,1]{1,0:T(1,128)}, f32[1,1]{1,0:T(1,128)}, u32[]{:S(2)}, u32[]{:S(2)}) collective-permute-start(f32[1,1]{1,0:T(1,128)} %add.87), channel_id=1, source_target_pairs={{0,128},{16,144},{32,160},{48,176},{64,192},{80,208},{96,224},{112... | collective-permute-start | bytes 20 | tf_op jit(solution)/shard_map/ppermute | solution.py:316
  139.1 2.7 %collective-permute-start.15 = (f32[1,1]{1,0:T(1,128)}, f32[1,1]{1,0:T(1,128)}, u32[]{:S(2)}, u32[]{:S(2)}) collective-permute-start(f32[1,1]{1,0:T(1,128)} %add.87), channel_id=1, source_target_pairs={{0,64},{16,80},{32,96},{48,112},{64,0},{80,16},{96,32},{112,48},{1... | collective-permute-start | bytes 20 | tf_op jit(solution)/shard_map/ppermute | solution.py:316
  141.8 1.7 %collective-permute-done.15 = f32[1,1]{1,0:T(1,128)} collective-permute-done((f32[1,1]{1,0:T(1,128)}, f32[1,1]{1,0:T(1,128)}, u32[]{:S(2)}, u32[]{:S(2)}) %collective-permute-start.15) | collective-permute-done | bytes 36 | tf_op jit(solution)/shard_map/ppermute | solution.py:316
  144.2 0.3 collective-permute-done.16
  145.8 0.1 divide_reduce_fusion
  145.9 0.2 select_reduce_fusion
  146.1 0.1 compare_select_fusion
  146.1 0.6 select_n.51
  146.8 0.0 all-to-all-done.2
  146.8 0.6 copy.16
  147.3 1.3 reshape.157
  (29 shorter events, 0.1 us)
Async XLA Ops:
  4.6 37.2 %all-to-all-start = ((bf16[16,264,256]{2,1,0:T(8,128)(2,1)}), bf16[16,264,256]{2,1,0:T(8,128)(2,1)S(1)}, u32[]{:S(2)}, u32[]{:S(2)}) async-start(bf16[16,264,256]{2,1,0:T(8,128)(2,1)} %spread.1), calls=%async_computation | async-start | bytes 4325376 | tf_op jit(solution)/shard_map/all_to_all | solution.py:218
  41.9 56.1 %copy-start = (bf16[16,264,256]{2,1,0:T(8,128)(2,1)}, bf16[16,264,256]{2,1,0:T(8,128)(2,1)S(1)}, u32[]{:S(2)}) copy-start(bf16[16,264,256]{2,1,0:T(8,128)(2,1)S(1)} %all-to-all-done.q_ref) | copy-start | bytes 6488068
  41.9 68.5 %all-to-all-start.1 = ((bf16[16,264,256]{2,1,0:T(8,128)(2,1)}), bf16[16,264,256]{2,1,0:T(8,128)(2,1)}, u32[]{:S(2)}, u32[]{:S(2)}) async-start(bf16[16,264,256]{2,1,0:T(8,128)(2,1)} %intra.3), calls=%async_computation.1 | async-start | bytes 4325376 | tf_op jit(solution)/shard_map/all_to_all | solution.py:270
  54.3 26.7 %collective-permute-start = (bf16[4,264,128]{2,1,0:T(8,128)(2,1)}, bf16[4,264,128]{2,1,0:T(8,128)(2,1)S(1)}, u32[]{:S(2)}, u32[]{:S(2)}) collective-permute-start(bf16[4,264,128]{2,1,0:T(8,128)(2,1)} %get-tuple-element.21), channel_id=1, source_target_pairs={{0,4},{1,5},{2,6},{3,7},{4,8},{5,9},{6,10},{7,11},{8,12},{9,13},{1... | collective-permute-start | bytes 811016 | tf_op jit(solution)/shard_map/ppermute | solution.py:242
  55.8 28.6 %collective-permute-start.1 = (bf16[4,264,128]{2,1,0:T(8,128)(2,1)}, bf16[4,264,128]{2,1,0:T(8,128)(2,1)S(1)}, u32[]{:S(2)}, u32[]{:S(2)}) collective-permute-start(bf16[4,264,128]{2,1,0:T(8,128)(2,1)} %get-tuple-element.22), channel_id=1, source_target_pairs={{0,8},{1,9},{2,10},{3,11},{4,12},{5,13},{6,14},{7,15},{8,0},{9,1},... | collective-permute-start | bytes 811016 | tf_op jit(solution)/shard_map/ppermute | solution.py:242
  58.5 25.8 %collective-permute-start.2 = (bf16[4,264,128]{2,1,0:T(8,128)(2,1)}, bf16[4,264,128]{2,1,0:T(8,128)(2,1)S(1)}, u32[]{:S(2)}, u32[]{:S(2)}) collective-permute-start(bf16[4,264,128]{2,1,0:T(8,128)(2,1)} %get-tuple-element.23), channel_id=1, source_target_pairs={{0,12},{1,13},{2,14},{3,15},{4,0},{5,1},{6,2},{7,3},{8,4},{9,5},{1... | collective-permute-start | bytes 811016 | tf_op jit(solution)/shard_map/ppermute | solution.py:242
  60.0 24.4 %collective-permute-start.3 = (bf16[4,264,128]{2,1,0:T(8,128)(2,1)}, bf16[4,264,128]{2,1,0:T(8,128)(2,1)S(1)}, u32[]{:S(2)}, u32[]{:S(2)}) collective-permute-start(bf16[4,264,128]{2,1,0:T(8,128)(2,1)} %get-tuple-element.25), channel_id=1, source_target_pairs={{0,1},{1,2},{2,3},{3,0},{4,5},{5,6},{6,7},{7,4},{8,9},{9,10},{10,1... | collective-permute-start | bytes 811016 | tf_op jit(solution)/shard_map/ppermute | solution.py:242
  61.4 23.0 %collective-permute-start.4 = (bf16[4,264,128]{2,1,0:T(8,128)(2,1)}, bf16[4,264,128]{2,1,0:T(8,128)(2,1)S(1)}, u32[]{:S(2)}, u32[]{:S(2)}) collective-permute-start(bf16[4,264,128]{2,1,0:T(8,128)(2,1)} %get-tuple-element.26), channel_id=1, source_target_pairs={{0,2},{1,3},{2,0},{3,1},{4,6},{5,7},{6,4},{7,5},{8,10},{9,11},{10,... | collective-permute-start | bytes 811016 | tf_op jit(solution)/shard_map/ppermute | solution.py:242
  81.0 6.8 %copy-start.1 = (bf16[4,264,128]{2,1,0:T(8,128)(2,1)}, bf16[4,264,128]{2,1,0:T(8,128)(2,1)S(1)}, u32[]{:S(2)}) copy-start(bf16[4,264,128]{2,1,0:T(8,128)(2,1)S(1)} %collective-permute-done.refs_1_) | copy-start | bytes 811012
  81.0 6.8 %collective-permute-start.5 = (bf16[4,264,128]{2,1,0:T(8,128)(2,1)}, bf16[4,264,128]{2,1,0:T(8,128)(2,1)}, u32[]{:S(2)}, u32[]{:S(2)}) collective-permute-start(bf16[4,264,128]{2,1,0:T(8,128)(2,1)} %get-tuple-element.27), channel_id=1, source_target_pairs={{0,3},{1,0},{2,1},{3,2},{4,7},{5,4},{6,5},{7,6},{8,11},{9,8},{10,9... | collective-permute-start | bytes 811016 | tf_op jit(solution)/shard_map/ppermute | solution.py:242
  84.4 3.4 %copy-start.2 = (bf16[4,264,128]{2,1,0:T(8,128)(2,1)}, bf16[4,264,128]{2,1,0:T(8,128)(2,1)S(1)}, u32[]{:S(2)}) copy-start(bf16[4,264,128]{2,1,0:T(8,128)(2,1)S(1)} %collective-permute-done.1.refs_2_) | copy-start | bytes 811012
  84.4 3.4 %copy-start.3 = (bf16[4,264,128]{2,1,0:T(8,128)(2,1)}, bf16[4,264,128]{2,1,0:T(8,128)(2,1)S(1)}, u32[]{:S(2)}) copy-start(bf16[4,264,128]{2,1,0:T(8,128)(2,1)S(1)} %collective-permute-done.2.refs_3_) | copy-start | bytes 811012
  84.4 3.4 %copy-start.4 = (bf16[4,264,128]{2,1,0:T(8,128)(2,1)}, bf16[4,264,128]{2,1,0:T(8,128)(2,1)S(1)}, u32[]{:S(2)}) copy-start(bf16[4,264,128]{2,1,0:T(8,128)(2,1)S(1)} %collective-permute-done.3.refs_5_) | copy-start | bytes 811012
  84.4 3.4 %copy-start.5 = (bf16[4,264,128]{2,1,0:T(8,128)(2,1)}, bf16[4,264,128]{2,1,0:T(8,128)(2,1)S(1)}, u32[]{:S(2)}) copy-start(bf16[4,264,128]{2,1,0:T(8,128)(2,1)S(1)} %collective-permute-done.4.refs_6_) | copy-start | bytes 811012
  90.4 7.6 %collective-permute-start.6 = (bf16[264,128]{1,0:T(8,128)(2,1)}, bf16[264,128]{1,0:T(8,128)(2,1)S(1)}, u32[]{:S(2)}, u32[]{:S(2)}) collective-permute-start(bf16[264,128]{1,0:T(8,128)(2,1)} %get-tuple-element.29), channel_id=1, source_target_pairs={{0,1},{1,2},{2,3},{3,0},{4,5},{5,6},{6,7},{7,4},{8,9},{9,10},{10,1... | collective-permute-start | bytes 202760 | tf_op jit(solution)/shard_map/ppermute | solution.py:253
  91.3 8.8 %collective-permute-start.7 = (bf16[264,128]{1,0:T(8,128)(2,1)}, bf16[264,128]{1,0:T(8,128)(2,1)S(1)}, u32[]{:S(2)}, u32[]{:S(2)}) collective-permute-start(bf16[264,128]{1,0:T(8,128)(2,1)} %get-tuple-element.30), channel_id=1, source_target_pairs={{0,2},{1,3},{2,0},{3,1},{4,6},{5,7},{6,4},{7,5},{8,10},{9,11},{10,... | collective-permute-start | bytes 202760 | tf_op jit(solution)/shard_map/ppermute | solution.py:253
  93.2 6.9 %collective-permute-start.8 = (bf16[264,128]{1,0:T(8,128)(2,1)}, bf16[264,128]{1,0:T(8,128)(2,1)S(1)}, u32[]{:S(2)}, u32[]{:S(2)}) collective-permute-start(bf16[264,128]{1,0:T(8,128)(2,1)} %get-tuple-element.31), channel_id=1, source_target_pairs={{0,3},{1,0},{2,1},{3,2},{4,7},{5,4},{6,5},{7,6},{8,11},{9,8},{10,9... | collective-permute-start | bytes 202760 | tf_op jit(solution)/shard_map/ppermute | solution.py:253
  95.8 6.4 %collective-permute-start.9 = (bf16[264,128]{1,0:T(8,128)(2,1)}, bf16[264,128]{1,0:T(8,128)(2,1)S(1)}, u32[]{:S(2)}, u32[]{:S(2)}) collective-permute-start(bf16[264,128]{1,0:T(8,128)(2,1)} %get-tuple-element.33), channel_id=1, source_target_pairs={{0,4},{1,5},{2,6},{3,7},{4,8},{5,9},{6,10},{7,11},{8,12},{9,13},{1... | collective-permute-start | bytes 202760 | tf_op jit(solution)/shard_map/ppermute | solution.py:253
  95.8 6.4 %collective-permute-start.10 = (bf16[264,128]{1,0:T(8,128)(2,1)}, bf16[264,128]{1,0:T(8,128)(2,1)S(1)}, u32[]{:S(2)}, u32[]{:S(2)}) collective-permute-start(bf16[264,128]{1,0:T(8,128)(2,1)} %get-tuple-element.34), channel_id=1, source_target_pairs={{0,8},{1,9},{2,10},{3,11},{4,12},{5,13},{6,14},{7,15},{8,0},{9,1},... | collective-permute-start | bytes 202760 | tf_op jit(solution)/shard_map/ppermute | solution.py:253
  98.0 5.1 %copy-start.6 = (bf16[264,128]{1,0:T(8,128)(2,1)}, bf16[264,128]{1,0:T(8,128)(2,1)S(1)}, u32[]{:S(2)}) copy-start(bf16[264,128]{1,0:T(8,128)(2,1)S(1)} %collective-permute-done.6.refs_1_) | copy-start | bytes 202756
  98.0 5.0 %collective-permute-start.11 = (bf16[264,128]{1,0:T(8,128)(2,1)}, bf16[264,128]{1,0:T(8,128)(2,1)S(1)}, u32[]{:S(2)}, u32[]{:S(2)}) collective-permute-start(bf16[264,128]{1,0:T(8,128)(2,1)} %get-tuple-element.35), channel_id=1, source_target_pairs={{0,12},{1,13},{2,14},{3,15},{4,0},{5,1},{6,2},{7,3},{8,4},{9,5},{1... | collective-permute-start | bytes 202760 | tf_op jit(solution)/shard_map/ppermute | solution.py:253
  100.1 2.9 %copy-start.7 = (bf16[264,128]{1,0:T(8,128)(2,1)}, bf16[264,128]{1,0:T(8,128)(2,1)S(1)}, u32[]{:S(2)}) copy-start(bf16[264,128]{1,0:T(8,128)(2,1)S(1)} %collective-permute-done.7.refs_2_) | copy-start | bytes 202756
  100.1 2.9 %copy-start.8 = (bf16[264,128]{1,0:T(8,128)(2,1)}, bf16[264,128]{1,0:T(8,128)(2,1)S(1)}, u32[]{:S(2)}) copy-start(bf16[264,128]{1,0:T(8,128)(2,1)S(1)} %collective-permute-done.8.refs_3_) | copy-start | bytes 202756
  102.2 0.9 copy-start.9
  102.2 0.9 copy-start.10
  103.1 0.6 copy-start.11
  110.3 11.5 %copy-start.13 = (s32[1,2]{1,0:T(1,128)S(1)}, s32[1,2]{1,0:T(1,128)}, u32[]{:S(2)}) copy-start(s32[1,2]{1,0:T(1,128)} %own_ref.1) | copy-start | bytes 28
  110.3 15.5 %copy-start.12 = (s32[16]{0:T(128)S(1)}, s32[16]{0:T(128)}, u32[]{:S(2)}) copy-start(s32[16]{0:T(128)} %fusion.len_ref) | copy-start | bytes 196
  115.4 31.3 %all-to-all-start.2 = ((bf16[16,128,256]{2,1,0:T(8,128)(2,1)}), bf16[16,128,256]{2,1,0:T(8,128)(2,1)S(1)}, u32[]{:S(2)}, u32[]{:S(2)}) async-start(bf16[16,128,256]{2,1,0:T(8,128)(2,1)} %bitcast.35), calls=%async_computation.2 | async-start | bytes 2097152 | tf_op jit(solution)/shard_map/all_to_all | solution.py:307
  123.8 5.1 %collective-permute-start.14 = (f32[1,1]{1,0:T(1,128)}, f32[1,1]{1,0:T(1,128)}, u32[]{:S(2)}, u32[]{:S(2)}) collective-permute-start(f32[1,1]{1,0:T(1,128)} %bitcast.8), channel_id=1, source_target_pairs={{0,48},{16,32},{32,16},{48,0},{64,112},{80,96},{96,80},{112,64},{1... | collective-permute-start | bytes 20 | tf_op jit(solution)/shard_map/ppermute | solution.py:316
  123.8 4.5 %collective-permute-start.13 = (f32[1,1]{1,0:T(1,128)}, f32[1,1]{1,0:T(1,128)}, u32[]{:S(2)}, u32[]{:S(2)}) collective-permute-start(f32[1,1]{1,0:T(1,128)} %bitcast.8), channel_id=1, source_target_pairs={{0,32},{16,48},{32,0},{48,16},{64,96},{80,112},{96,64},{112,80},{1... | collective-permute-start | bytes 20 | tf_op jit(solution)/shard_map/ppermute | solution.py:316
  125.7 1.3 collective-permute-start.12
  129.6 15.5 %collective-permute-start.17 = (f32[1,1]{1,0:T(1,128)}, f32[1,1]{1,0:T(1,128)}, u32[]{:S(2)}, u32[]{:S(2)}) collective-permute-start(f32[1,1]{1,0:T(1,128)} %add.87), channel_id=1, source_target_pairs={{0,192},{16,208},{32,224},{48,240},{64,128},{80,144},{96,160},{112... | collective-permute-start | bytes 20 | tf_op jit(solution)/shard_map/ppermute | solution.py:316
  136.9 7.6 %collective-permute-start.16 = (f32[1,1]{1,0:T(1,128)}, f32[1,1]{1,0:T(1,128)}, u32[]{:S(2)}, u32[]{:S(2)}) collective-permute-start(f32[1,1]{1,0:T(1,128)} %add.87), channel_id=1, source_target_pairs={{0,128},{16,144},{32,160},{48,176},{64,192},{80,208},{96,224},{112... | collective-permute-start | bytes 20 | tf_op jit(solution)/shard_map/ppermute | solution.py:316
  139.1 4.4 %collective-permute-start.15 = (f32[1,1]{1,0:T(1,128)}, f32[1,1]{1,0:T(1,128)}, u32[]{:S(2)}, u32[]{:S(2)}) collective-permute-start(f32[1,1]{1,0:T(1,128)} %add.87), channel_id=1, source_target_pairs={{0,64},{16,80},{32,96},{48,112},{64,0},{80,16},{96,32},{112,48},{1... | collective-permute-start | bytes 20 | tf_op jit(solution)/shard_map/ppermute | solution.py:316

commit v4 on v3

--- a/solution.py
+++ b/solution.py
@@ -39,10 +39,10 @@
     part = width // 8
     slots = own_ref.shape[1]
     col = lax.broadcasted_iota(jnp.int32, (EXTRA, width), 1)
-    r = jnp.where(col < part, 0.0, rew_ref[0, 0])
+    r = jnp.where(col < part, 0.0, rew_ref[...])
     for i in range(slots):
-        r = jnp.where(col == i, own_ref[0, i].astype(F32), r)
-    r = jnp.where(col == slots, len_ref[0, 0].astype(F32), r)
+        r = jnp.where(col == i, own_ref[:, i : i + 1].astype(F32), r)
+    r = jnp.where(col == slots, len_ref[...].astype(F32), r)
     r1 = r.astype(BF16).astype(F32)
     r2 = (r - r1).astype(BF16).astype(F32)
     r3 = r - r1 - r2
@@ -83,8 +83,7 @@
             outs[SIDE * p + s][...] = acc.astype(BF16)
 
 
-def intra_kernel(q_ref, k_ref, v_ref, wq_ref, wk_ref, *rest):
-    o_ref = rest[-1]
+def intra_kernel(q_ref, k_ref, v_ref, wq_ref, wk_ref, o_ref):
     length, width = q_ref.shape[0], wq_ref.shape[1]
     half = length // 2
     many = wq_ref.shape[0]
@@ -209,8 +208,12 @@
     q_all = pl.pallas_call(
         spread_kernel,
         grid=(2,),
-        in_specs=[pl.BlockSpec(memory_space=pltpu.SMEM)] * 3
-        + [pl.BlockSpec((length, heads * width // 2), lambda o: (0, o))],
+        in_specs=[
+            pl.BlockSpec(assign.shape, lambda o: (0, 0)),
+            pl.BlockSpec(resp_len.shape, lambda o: (0, 0)),
+            pl.BlockSpec(rewards.shape, lambda o: (0, 0)),
+            pl.BlockSpec((length, heads * width // 2), lambda o: (0, o)),
+        ],
         out_specs=pl.BlockSpec((dp // 2, tall, two), lambda o: (o, 0, 0)),
         out_shape=jax.ShapeDtypeStruct((dp, tall, two), BF16),
         name="spread",
@@ -252,22 +255,16 @@
             i = SIDE * p + s
             states[i] = lax.ppermute(states[i], "dp", hop(0, s) if p == 0 else hop(s, 0))
 
-    inner = ()
-    for p in range(2):
-        at = p * (heads // 8)
-        specs = [pl.BlockSpec((length, 4 * width), lambda o, at=at: (0, o + at))] * 3
-        specs += [pl.BlockSpec((4, width, feat), lambda o, at=at: (o + at, 0, 0))] * 2
-        inner = pl.pallas_call(
-            intra_kernel,
-            grid=(heads // 8,),
-            in_specs=specs + [pl.BlockSpec(memory_space=pl.ANY)] * p,
-            out_specs=pl.BlockSpec((2, tall, two), lambda o, at=at: (o + at, 0, 0)),
-            out_shape=jax.ShapeDtypeStruct((dp, tall, two), BF16),
-            input_output_aliases={5: 0} if p else {},
-            name="intra",
-        )(q, k, v, feat_q, feat_k, *inner)
-        inner = (inner,)
-    inner = lax.all_to_all(inner[0], "dp", 0, 0, tiled=True)
+    inner = pl.pallas_call(
+        intra_kernel,
+        grid=(heads // 4,),
+        in_specs=[pl.BlockSpec((length, 4 * width), lambda o: (0, o))] * 3
+        + [pl.BlockSpec((4, width, feat), lambda o: (o, 0, 0))] * 2,
+        out_specs=pl.BlockSpec((2, tall, two), lambda o: (o, 0, 0)),
+        out_shape=jax.ShapeDtypeStruct((dp, tall, two), BF16),
+        name="intra",
+    )(q, k, v, feat_q, feat_k)
+    inner = lax.all_to_all(inner, "dp", 0, 0, tiled=True)
 
     total = dp * slots
     many = 8

time: 150 us -> 149 us (level)
  Pallas kernels: 35.9 us -> 34.1 us
  waiting for transfers between devices: 45.2 us -> 46.9 us
    pallas_call x3 -> x2, Pallas kernels: 16.1 us -> 14.3 us  [the longest x1 11.6 us: body(): pl.pallas_call(intra_kernel, grid=(heads // 4,), in_specs=[pl.BlockSpec((...]
    all_to_all x1, waiting for transfers between devices: 16.5 us -> 18.3 us  [body(): q_all = lax.all_to_all(q_all, 'dp', 0, 0, tiled=True)]
  transfers between devices with their start and end apart: 21 -> 21, of which waited for: 9 -> 9; matrix products, arithmetic and copies ran while one was open for 4% -> 4% of each run, Pallas kernels for 19% -> 18%
where the time goes in v4:
time: 149 us; the launch traced here: 148 us
  starting transfers between devices  51.8 us (35%)
  waiting for transfers between devices  46.9 us (31%)
  Pallas kernels  34.1 us (23%)
  between operations  7.82 us (5%)
  local copies, waits for them, and re-layouts  5.21 us (3%)
  other arithmetic  2.62 us (2%)
    ppermute x6, waiting for transfers between devices, body(): lax.ppermute(states[i], 'dp', hop(s, 0) if p == 0 else hop(0, s))  22.9 us
    all_to_all x1, waiting for transfers between devices, body(): q_all = lax.all_to_all(q_all, 'dp', 0, 0, tiled=True)  18.3 us
    ppermute x6, starting transfers between devices, body(): lax.ppermute(spread, 'group', [(g, g ^ step * i) for g in range(groups)])  14.3 us
    pallas_call x1, Pallas kernels, body(): pl.pallas_call(intra_kernel, grid=(heads // 4,), in_specs=[pl.BlockSpec((...  11.6 us
    ppermute x6, starting transfers between devices, body(): lax.ppermute(states[i], 'dp', hop(0, s) if p == 0 else hop(s, 0))  9.08 us
    ppermute x6, starting transfers between devices, body(): lax.ppermute(states[i], 'dp', hop(s, 0) if p == 0 else hop(0, s))  9.06 us
    all_to_all x1, starting transfers between devices, body(): q_all = lax.all_to_all(q_all, 'dp', 0, 0, tiled=True)  7.39 us
    all_to_all x1, starting transfers between devices, body(): lax.all_to_all(out.reshape(dp, slots * BLK, two), 'dp', 0, 0, tiled=True)  6.36 us
  transfers between devices with their start and end apart: 21, of which 9 were waited for; matrix products, arithmetic and copies ran while one was open for 4% of the time, Pallas kernels for 18%

profile of v4, /device:TPU:8, one launch (start us, length us, event | category | flops | bytes accessed | tf_op | source)
XLA Modules:
  0.0 148.5 jit_solution(5941330292237084334)
XLA Ops:
  1.9 2.7 %spread.1 = bf16[16,264,256]{2,1,0:T(8,128)(2,1)} custom-call(s32[1,2]{1,0:T(1,128)} %own_ref.1, s32[1,1]{1,0:T(1,128)S(6)} %copy.20.len_ref, f32[1,1]{1,0:T(1,128)S(6)} %copy.21.rew_ref, bf16[256,4096]{1,0:T(8,128)(2,1)} %bitcast.27), custom_call_target="tpu_custom_call" | custom-call | tf_op jit(solution)/shard_map/spread/pallas_call | solution.py:208
  4.6 7.4 %all-to-all-start = ((bf16[16,264,256]{2,1,0:T(8,128)(2,1)}), bf16[16,264,256]{2,1,0:T(8,128)(2,1)S(1)}, u32[]{:S(2)}, u32[]{:S(2)}) async-start(bf16[16,264,256]{2,1,0:T(8,128)(2,1)} %spread.1), calls=%async_computation | async-start | bytes 4325376 | tf_op jit(solution)/shard_map/all_to_all | solution.py:221
  12.0 11.6 %intra.1 = bf16[16,264,256]{2,1,0:T(8,128)(2,1)} custom-call(bf16[256,4096]{1,0:T(8,128)(2,1)} %bitcast.28, bf16[256,4096]{1,0:T(8,128)(2,1)} %bitcast.31, bf16[256,4096]{1,0:T(8,128)(2,1)} %bitcast.32, bf16[32,128,128]{2,1,0:T(8,128)(2,1)} %wq_ref.1, bf16[32,128,128]{2,1,0:T(8,128)(2,1)} %w_ref.1), custom_call_target="tpu_custom_call" | custom-call | tf_op jit(solution)/shard_map/intra/pallas_call | solution.py:258
  23.6 18.3 %all-to-all-done.q_ref = bf16[16,264,256]{2,1,0:T(8,128)(2,1)S(1)} async-done(((bf16[16,264,256]{2,1,0:T(8,128)(2,1)}), bf16[16,264,256]{2,1,0:T(8,128)(2,1)S(1)}, u32[]{:S(2)}, u32[]{:S(2)}) %all-to-all-start) | async-done | bytes 2162720 | tf_op jit(solution)/shard_map/all_to_all | solution.py:221
  41.9 5.6 %all-to-all-start.1 = ((bf16[16,264,256]{2,1,0:T(8,128)(2,1)}), bf16[16,264,256]{2,1,0:T(8,128)(2,1)}, u32[]{:S(2)}, u32[]{:S(2)}) async-start(bf16[16,264,256]{2,1,0:T(8,128)(2,1)} %intra.1), calls=%async_computation.1 | async-start | bytes 4325376 | tf_op jit(solution)/shard_map/all_to_all | solution.py:267
  48.1 6.2 %state.1 = (bf16[4,264,128]{2,1,0:T(8,128)(2,1)}, bf16[4,264,128]{2,1,0:T(8,128)(2,1)}, bf16[4,264,128]{2,1,0:T(8,128)(2,1)}, bf16[4,264,128]{2,1,0:T(8,128)(2,1...) custom-call(s32[1]{0:T(128)S(6)} %copy.19.n_ref, ...), custom_call_target="tpu_custom_call" | custom-call | tf_op jit(solution)/shard_map/state/pallas_call | solution.py:228
  54.3 1.5 %collective-permute-start = (bf16[4,264,128]{2,1,0:T(8,128)(2,1)}, bf16[4,264,128]{2,1,0:T(8,128)(2,1)S(1)}, u32[]{:S(2)}, u32[]{:S(2)}) collective-permute-start(bf16[4,264,128]{2,1,0:T(8,128)(2,1)} %get-tuple-element.21), channel_id=1, source_target_pairs={{0,4},{1,5},{2,6},{3,7},{4,8},{5,9},{6,10},{7,11},{8,12},{9,13},{1... | collective-permute-start | bytes 811016 | tf_op jit(solution)/shard_map/ppermute | solution.py:245
  55.8 2.7 %collective-permute-start.1 = (bf16[4,264,128]{2,1,0:T(8,128)(2,1)}, bf16[4,264,128]{2,1,0:T(8,128)(2,1)S(1)}, u32[]{:S(2)}, u32[]{:S(2)}) collective-permute-start(bf16[4,264,128]{2,1,0:T(8,128)(2,1)} %get-tuple-element.22), channel_id=1, source_target_pairs={{0,8},{1,9},{2,10},{3,11},{4,12},{5,13},{6,14},{7,15},{8,0},{9,1},... | collective-permute-start | bytes 811016 | tf_op jit(solution)/shard_map/ppermute | solution.py:245
  58.5 1.4 collective-permute-start.2
  59.9 1.5 collective-permute-start.3
  61.4 1.2 collective-permute-start.4
  62.6 18.4 %collective-permute-done.refs_1_ = bf16[4,264,128]{2,1,0:T(8,128)(2,1)S(1)} collective-permute-done((bf16[4,264,128]{2,1,0:T(8,128)(2,1)}, bf16[4,264,128]{2,1,0:T(8,128)(2,1)S(1)}, u32[]{:S(2)}, u32[]{:S(2)}) %collective-permute-start) | collective-permute-done | bytes 270368 | tf_op jit(solution)/shard_map/ppermute | solution.py:245
  81.0 0.8 collective-permute-start.5
  81.7 1.5 constant_dynamic-slice_fusion.w_ref
  83.2 1.2 collective-permute-done.1.refs_2_
  84.3 0.0 collective-permute-done.2.refs_3_
  84.4 0.0 collective-permute-done.3.refs_5_
  84.4 0.0 collective-permute-done.4.refs_6_
  84.4 3.3 %collective-permute-done.5.refs_7_ = bf16[4,264,128]{2,1,0:T(8,128)(2,1)} collective-permute-done((bf16[4,264,128]{2,1,0:T(8,128)(2,1)}, bf16[4,264,128]{2,1,0:T(8,128)(2,1)}, u32[]{:S(2)}, u32[]{:S(2)}) %collective-permute-start.5) | collective-permute-done | bytes 270368 | tf_op jit(solution)/shard_map/ppermute | solution.py:245
  87.7 0.0 copy-done.1
  87.8 2.6 %add.106 = (bf16[264,128]{1,0:T(8,128)(2,1)}, bf16[264,128]{1,0:T(8,128)(2,1)}, bf16[264,128]{1,0:T(8,128)(2,1)}, bf16[264,128]{1,0:T(8,128)(2,1)}, bf16[264,128...) custom-call(bf16[4,264,128]{2,1,0:T(8,128)(2,1)} %get-tuple-element.20.refs_0_, ...), custom_call_target="tpu_custom_call" | custom-call | tf_op jit(solution)/shard_map/add/pallas_call | solution.py:246
  90.4 0.9 collective-permute-start.6
  91.3 2.0 %collective-permute-start.7 = (bf16[264,128]{1,0:T(8,128)(2,1)}, bf16[264,128]{1,0:T(8,128)(2,1)S(1)}, u32[]{:S(2)}, u32[]{:S(2)}) collective-permute-start(bf16[264,128]{1,0:T(8,128)(2,1)} %get-tuple-element.30), channel_id=1, source_target_pairs={{0,2},{1,3},{2,0},{3,1},{4,6},{5,7},{6,4},{7,5},{8,10},{9,11},{10,... | collective-permute-start | bytes 202760 | tf_op jit(solution)/shard_map/ppermute | solution.py:256
  93.2 2.5 %collective-permute-start.8 = (bf16[264,128]{1,0:T(8,128)(2,1)}, bf16[264,128]{1,0:T(8,128)(2,1)S(1)}, u32[]{:S(2)}, u32[]{:S(2)}) collective-permute-start(bf16[264,128]{1,0:T(8,128)(2,1)} %get-tuple-element.31), channel_id=1, source_target_pairs={{0,3},{1,0},{2,1},{3,2},{4,7},{5,4},{6,5},{7,6},{8,11},{9,8},{10,9... | collective-permute-start | bytes 202760 | tf_op jit(solution)/shard_map/ppermute | solution.py:256
  95.8 0.0 collective-permute-start.9
  95.8 2.2 %collective-permute-start.10 = (bf16[264,128]{1,0:T(8,128)(2,1)}, bf16[264,128]{1,0:T(8,128)(2,1)S(1)}, u32[]{:S(2)}, u32[]{:S(2)}) collective-permute-start(bf16[264,128]{1,0:T(8,128)(2,1)} %get-tuple-element.34), channel_id=1, source_target_pairs={{0,8},{1,9},{2,10},{3,11},{4,12},{5,13},{6,14},{7,15},{8,0},{9,1},... | collective-permute-start | bytes 202760 | tf_op jit(solution)/shard_map/ppermute | solution.py:256
  98.0 0.0 copy-done
  98.0 0.0 collective-permute-done.6.refs_1_
  98.0 0.0 copy-start.6
  98.0 1.5 %collective-permute-start.11 = (bf16[264,128]{1,0:T(8,128)(2,1)}, bf16[264,128]{1,0:T(8,128)(2,1)S(1)}, u32[]{:S(2)}, u32[]{:S(2)}) collective-permute-start(bf16[264,128]{1,0:T(8,128)(2,1)} %get-tuple-element.35), channel_id=1, source_target_pairs={{0,12},{1,13},{2,14},{3,15},{4,0},{5,1},{6,2},{7,3},{8,4},{9,5},{1... | collective-permute-start | bytes 202760 | tf_op jit(solution)/shard_map/ppermute | solution.py:256
  99.5 0.6 reshape.155.ids_ref
  100.1 0.0 collective-permute-done.7.refs_2_
  100.1 0.0 collective-permute-done.8.refs_3_
  100.1 2.1 %collective-permute-done.9.refs_5_ = bf16[264,128]{1,0:T(8,128)(2,1)S(1)} collective-permute-done((bf16[264,128]{1,0:T(8,128)(2,1)}, bf16[264,128]{1,0:T(8,128)(2,1)S(1)}, u32[]{:S(2)}, u32[]{:S(2)}) %collective-permute-start.9) | collective-permute-done | bytes 67616 | tf_op jit(solution)/shard_map/ppermute | solution.py:256
  102.2 0.0 collective-permute-done.10.refs_6_
  102.2 0.8 collective-permute-done.11.refs_7_
  103.1 0.0 copy-done.7
  103.1 0.6 copy-done.11
  103.7 5.9 %prompt.1 = (bf16[32,64,256]{2,1,0:T(8,128)(2,1)}, bf16[32,64,256]{2,1,0:T(8,128)(2,1)}) custom-call(s32[32]{0:T(128)} %reshape.155.ids_ref, bf16[16,264,256]{2,1,0:T(8,128)(2,1)} %copy-done, bf16[2,128,128]{2,1,0:T(8,128)(2,1)} %constant_dynamic-slice_fusion.w_ref, bf16[264,128]{1,0:T(8,128)(2,1)} %get-tuple-element.28.refs_0_, bf16[264,128]{1,0:T(8,128)(2,1)} %copy-done.6, ...), custom_call_target="tpu_custom_call" | custom-call | tf_op jit(solution)/shard_map/prompt/pallas_call | solution.py:273
  109.6 0.8 fusion.len_ref
  110.4 0.0 all-to-all-done.1.part_ref
  110.4 5.1 %combine.1 = bf16[2048,256]{1,0:T(8,128)(2,1)} custom-call(s32[32]{0:T(128)} %reshape.155.ids_ref, s32[16]{0:T(128)} %fusion.len_ref, bf16[16,264,256]{2,1,0:T(8,128)(2,1)} %all-to-all-done.1.part_ref, bf16[32,64,256]{2,1,0:T(8,128)(2,1)} %get-tuple-element.36.num_ref, bf16[32,64,256]{2,1,0:T(8,128)(2,1)} %get-tuple-element.37.den_ref), custom_call_target="tpu_custom_call" | custom-call | tf_op jit(solution)/shard_map/combine/pallas_call | solution.py:290
  115.5 6.4 %all-to-all-start.2 = ((bf16[16,128,256]{2,1,0:T(8,128)(2,1)}), bf16[16,128,256]{2,1,0:T(8,128)(2,1)S(1)}, u32[]{:S(2)}, u32[]{:S(2)}) async-start(bf16[16,128,256]{2,1,0:T(8,128)(2,1)} %bitcast.30), calls=%async_computation.2 | async-start | bytes 2097152 | tf_op jit(solution)/shard_map/all_to_all | solution.py:304
  121.9 0.7 fusion.2
  123.2 0.6 multiply_reduce_fusion
  123.8 0.0 collective-permute-start.14
  123.8 1.9 %collective-permute-start.13 = (f32[1,1]{1,0:T(1,128)}, f32[1,1]{1,0:T(1,128)}, u32[]{:S(2)}, u32[]{:S(2)}) collective-permute-start(f32[1,1]{1,0:T(1,128)} %bitcast.8), channel_id=1, source_target_pairs={{0,32},{16,48},{32,0},{48,16},{64,96},{80,112},{96,64},{112,80},{1... | collective-permute-start | bytes 20 | tf_op jit(solution)/shard_map/ppermute | solution.py:313
  125.7 0.1 collective-permute-start.12
  125.8 0.2 select_reduce_fusion.1
  126.0 1.0 collective-permute-done.12
  128.3 0.0 collective-permute-done.13
  128.9 0.0 collective-permute-done.14
  129.5 7.3 %collective-permute-start.17 = (f32[1,1]{1,0:T(1,128)}, f32[1,1]{1,0:T(1,128)}, u32[]{:S(2)}, u32[]{:S(2)}) collective-permute-start(f32[1,1]{1,0:T(1,128)} %add.87), channel_id=1, source_target_pairs={{0,192},{16,208},{32,224},{48,240},{64,128},{80,144},{96,160},{112... | collective-permute-start | bytes 20 | tf_op jit(solution)/shard_map/ppermute | solution.py:313
  136.8 2.2 %collective-permute-start.16 = (f32[1,1]{1,0:T(1,128)}, f32[1,1]{1,0:T(1,128)}, u32[]{:S(2)}, u32[]{:S(2)}) collective-permute-start(f32[1,1]{1,0:T(1,128)} %add.87), channel_id=1, source_target_pairs={{0,128},{16,144},{32,160},{48,176},{64,192},{80,208},{96,224},{112... | collective-permute-start | bytes 20 | tf_op jit(solution)/shard_map/ppermute | solution.py:313
  139.1 2.7 %collective-permute-start.15 = (f32[1,1]{1,0:T(1,128)}, f32[1,1]{1,0:T(1,128)}, u32[]{:S(2)}, u32[]{:S(2)}) collective-permute-start(f32[1,1]{1,0:T(1,128)} %add.87), channel_id=1, source_target_pairs={{0,64},{16,80},{32,96},{48,112},{64,0},{80,16},{96,32},{112,48},{1... | collective-permute-start | bytes 20 | tf_op jit(solution)/shard_map/ppermute | solution.py:313
  141.8 1.7 %collective-permute-done.15 = f32[1,1]{1,0:T(1,128)} collective-permute-done((f32[1,1]{1,0:T(1,128)}, f32[1,1]{1,0:T(1,128)}, u32[]{:S(2)}, u32[]{:S(2)}) %collective-permute-start.15) | collective-permute-done | bytes 36 | tf_op jit(solution)/shard_map/ppermute | solution.py:313
  144.1 0.2 collective-permute-done.16
  145.6 0.1 divide_reduce_fusion
  145.7 0.2 select_reduce_fusion
  145.9 0.1 compare_select_fusion
  146.0 0.6 select_n.51
  146.6 0.0 all-to-all-done.2
  146.6 0.6 copy.15
  147.1 1.3 reshape.157
  (28 shorter events, 0.1 us)
Async XLA Ops:
  4.6 37.2 %all-to-all-start = ((bf16[16,264,256]{2,1,0:T(8,128)(2,1)}), bf16[16,264,256]{2,1,0:T(8,128)(2,1)S(1)}, u32[]{:S(2)}, u32[]{:S(2)}) async-start(bf16[16,264,256]{2,1,0:T(8,128)(2,1)} %spread.1), calls=%async_computation | async-start | bytes 4325376 | tf_op jit(solution)/shard_map/all_to_all | solution.py:221
  41.8 56.1 %copy-start = (bf16[16,264,256]{2,1,0:T(8,128)(2,1)}, bf16[16,264,256]{2,1,0:T(8,128)(2,1)S(1)}, u32[]{:S(2)}) copy-start(bf16[16,264,256]{2,1,0:T(8,128)(2,1)S(1)} %all-to-all-done.q_ref) | copy-start | bytes 6488068
  41.9 68.5 %all-to-all-start.1 = ((bf16[16,264,256]{2,1,0:T(8,128)(2,1)}), bf16[16,264,256]{2,1,0:T(8,128)(2,1)}, u32[]{:S(2)}, u32[]{:S(2)}) async-start(bf16[16,264,256]{2,1,0:T(8,128)(2,1)} %intra.1), calls=%async_computation.1 | async-start | bytes 4325376 | tf_op jit(solution)/shard_map/all_to_all | solution.py:267
  54.3 26.7 %collective-permute-start = (bf16[4,264,128]{2,1,0:T(8,128)(2,1)}, bf16[4,264,128]{2,1,0:T(8,128)(2,1)S(1)}, u32[]{:S(2)}, u32[]{:S(2)}) collective-permute-start(bf16[4,264,128]{2,1,0:T(8,128)(2,1)} %get-tuple-element.21), channel_id=1, source_target_pairs={{0,4},{1,5},{2,6},{3,7},{4,8},{5,9},{6,10},{7,11},{8,12},{9,13},{1... | collective-permute-start | bytes 811016 | tf_op jit(solution)/shard_map/ppermute | solution.py:245
  55.8 28.6 %collective-permute-start.1 = (bf16[4,264,128]{2,1,0:T(8,128)(2,1)}, bf16[4,264,128]{2,1,0:T(8,128)(2,1)S(1)}, u32[]{:S(2)}, u32[]{:S(2)}) collective-permute-start(bf16[4,264,128]{2,1,0:T(8,128)(2,1)} %get-tuple-element.22), channel_id=1, source_target_pairs={{0,8},{1,9},{2,10},{3,11},{4,12},{5,13},{6,14},{7,15},{8,0},{9,1},... | collective-permute-start | bytes 811016 | tf_op jit(solution)/shard_map/ppermute | solution.py:245
  58.5 25.8 %collective-permute-start.2 = (bf16[4,264,128]{2,1,0:T(8,128)(2,1)}, bf16[4,264,128]{2,1,0:T(8,128)(2,1)S(1)}, u32[]{:S(2)}, u32[]{:S(2)}) collective-permute-start(bf16[4,264,128]{2,1,0:T(8,128)(2,1)} %get-tuple-element.23), channel_id=1, source_target_pairs={{0,12},{1,13},{2,14},{3,15},{4,0},{5,1},{6,2},{7,3},{8,4},{9,5},{1... | collective-permute-start | bytes 811016 | tf_op jit(solution)/shard_map/ppermute | solution.py:245
  59.9 24.4 %collective-permute-start.3 = (bf16[4,264,128]{2,1,0:T(8,128)(2,1)}, bf16[4,264,128]{2,1,0:T(8,128)(2,1)S(1)}, u32[]{:S(2)}, u32[]{:S(2)}) collective-permute-start(bf16[4,264,128]{2,1,0:T(8,128)(2,1)} %get-tuple-element.25), channel_id=1, source_target_pairs={{0,1},{1,2},{2,3},{3,0},{4,5},{5,6},{6,7},{7,4},{8,9},{9,10},{10,1... | collective-permute-start | bytes 811016 | tf_op jit(solution)/shard_map/ppermute | solution.py:245
  61.4 23.0 %collective-permute-start.4 = (bf16[4,264,128]{2,1,0:T(8,128)(2,1)}, bf16[4,264,128]{2,1,0:T(8,128)(2,1)S(1)}, u32[]{:S(2)}, u32[]{:S(2)}) collective-permute-start(bf16[4,264,128]{2,1,0:T(8,128)(2,1)} %get-tuple-element.26), channel_id=1, source_target_pairs={{0,2},{1,3},{2,0},{3,1},{4,6},{5,7},{6,4},{7,5},{8,10},{9,11},{10,... | collective-permute-start | bytes 811016 | tf_op jit(solution)/shard_map/ppermute | solution.py:245
  80.9 6.8 %copy-start.1 = (bf16[4,264,128]{2,1,0:T(8,128)(2,1)}, bf16[4,264,128]{2,1,0:T(8,128)(2,1)S(1)}, u32[]{:S(2)}) copy-start(bf16[4,264,128]{2,1,0:T(8,128)(2,1)S(1)} %collective-permute-done.refs_1_) | copy-start | bytes 811012
  81.0 6.8 %collective-permute-start.5 = (bf16[4,264,128]{2,1,0:T(8,128)(2,1)}, bf16[4,264,128]{2,1,0:T(8,128)(2,1)}, u32[]{:S(2)}, u32[]{:S(2)}) collective-permute-start(bf16[4,264,128]{2,1,0:T(8,128)(2,1)} %get-tuple-element.27), channel_id=1, source_target_pairs={{0,3},{1,0},{2,1},{3,2},{4,7},{5,4},{6,5},{7,6},{8,11},{9,8},{10,9... | collective-permute-start | bytes 811016 | tf_op jit(solution)/shard_map/ppermute | solution.py:245
  84.3 3.4 %copy-start.2 = (bf16[4,264,128]{2,1,0:T(8,128)(2,1)}, bf16[4,264,128]{2,1,0:T(8,128)(2,1)S(1)}, u32[]{:S(2)}) copy-start(bf16[4,264,128]{2,1,0:T(8,128)(2,1)S(1)} %collective-permute-done.1.refs_2_) | copy-start | bytes 811012
  84.3 3.4 %copy-start.3 = (bf16[4,264,128]{2,1,0:T(8,128)(2,1)}, bf16[4,264,128]{2,1,0:T(8,128)(2,1)S(1)}, u32[]{:S(2)}) copy-start(bf16[4,264,128]{2,1,0:T(8,128)(2,1)S(1)} %collective-permute-done.2.refs_3_) | copy-start | bytes 811012
  84.4 3.4 %copy-start.4 = (bf16[4,264,128]{2,1,0:T(8,128)(2,1)}, bf16[4,264,128]{2,1,0:T(8,128)(2,1)S(1)}, u32[]{:S(2)}) copy-start(bf16[4,264,128]{2,1,0:T(8,128)(2,1)S(1)} %collective-permute-done.3.refs_5_) | copy-start | bytes 811012
  84.4 3.4 %copy-start.5 = (bf16[4,264,128]{2,1,0:T(8,128)(2,1)}, bf16[4,264,128]{2,1,0:T(8,128)(2,1)S(1)}, u32[]{:S(2)}) copy-start(bf16[4,264,128]{2,1,0:T(8,128)(2,1)S(1)} %collective-permute-done.4.refs_6_) | copy-start | bytes 811012
  90.4 7.6 %collective-permute-start.6 = (bf16[264,128]{1,0:T(8,128)(2,1)}, bf16[264,128]{1,0:T(8,128)(2,1)S(1)}, u32[]{:S(2)}, u32[]{:S(2)}) collective-permute-start(bf16[264,128]{1,0:T(8,128)(2,1)} %get-tuple-element.29), channel_id=1, source_target_pairs={{0,1},{1,2},{2,3},{3,0},{4,5},{5,6},{6,7},{7,4},{8,9},{9,10},{10,1... | collective-permute-start | bytes 202760 | tf_op jit(solution)/shard_map/ppermute | solution.py:256
  91.3 8.8 %collective-permute-start.7 = (bf16[264,128]{1,0:T(8,128)(2,1)}, bf16[264,128]{1,0:T(8,128)(2,1)S(1)}, u32[]{:S(2)}, u32[]{:S(2)}) collective-permute-start(bf16[264,128]{1,0:T(8,128)(2,1)} %get-tuple-element.30), channel_id=1, source_target_pairs={{0,2},{1,3},{2,0},{3,1},{4,6},{5,7},{6,4},{7,5},{8,10},{9,11},{10,... | collective-permute-start | bytes 202760 | tf_op jit(solution)/shard_map/ppermute | solution.py:256
  93.2 6.9 %collective-permute-start.8 = (bf16[264,128]{1,0:T(8,128)(2,1)}, bf16[264,128]{1,0:T(8,128)(2,1)S(1)}, u32[]{:S(2)}, u32[]{:S(2)}) collective-permute-start(bf16[264,128]{1,0:T(8,128)(2,1)} %get-tuple-element.31), channel_id=1, source_target_pairs={{0,3},{1,0},{2,1},{3,2},{4,7},{5,4},{6,5},{7,6},{8,11},{9,8},{10,9... | collective-permute-start | bytes 202760 | tf_op jit(solution)/shard_map/ppermute | solution.py:256
  95.8 6.4 %collective-permute-start.9 = (bf16[264,128]{1,0:T(8,128)(2,1)}, bf16[264,128]{1,0:T(8,128)(2,1)S(1)}, u32[]{:S(2)}, u32[]{:S(2)}) collective-permute-start(bf16[264,128]{1,0:T(8,128)(2,1)} %get-tuple-element.33), channel_id=1, source_target_pairs={{0,4},{1,5},{2,6},{3,7},{4,8},{5,9},{6,10},{7,11},{8,12},{9,13},{1... | collective-permute-start | bytes 202760 | tf_op jit(solution)/shard_map/ppermute | solution.py:256
  95.8 6.4 %collective-permute-start.10 = (bf16[264,128]{1,0:T(8,128)(2,1)}, bf16[264,128]{1,0:T(8,128)(2,1)S(1)}, u32[]{:S(2)}, u32[]{:S(2)}) collective-permute-start(bf16[264,128]{1,0:T(8,128)(2,1)} %get-tuple-element.34), channel_id=1, source_target_pairs={{0,8},{1,9},{2,10},{3,11},{4,12},{5,13},{6,14},{7,15},{8,0},{9,1},... | collective-permute-start | bytes 202760 | tf_op jit(solution)/shard_map/ppermute | solution.py:256
  98.0 5.1 %copy-start.6 = (bf16[264,128]{1,0:T(8,128)(2,1)}, bf16[264,128]{1,0:T(8,128)(2,1)S(1)}, u32[]{:S(2)}) copy-start(bf16[264,128]{1,0:T(8,128)(2,1)S(1)} %collective-permute-done.6.refs_1_) | copy-start | bytes 202756
  98.0 5.0 %collective-permute-start.11 = (bf16[264,128]{1,0:T(8,128)(2,1)}, bf16[264,128]{1,0:T(8,128)(2,1)S(1)}, u32[]{:S(2)}, u32[]{:S(2)}) collective-permute-start(bf16[264,128]{1,0:T(8,128)(2,1)} %get-tuple-element.35), channel_id=1, source_target_pairs={{0,12},{1,13},{2,14},{3,15},{4,0},{5,1},{6,2},{7,3},{8,4},{9,5},{1... | collective-permute-start | bytes 202760 | tf_op jit(solution)/shard_map/ppermute | solution.py:256
  100.1 2.9 %copy-start.7 = (bf16[264,128]{1,0:T(8,128)(2,1)}, bf16[264,128]{1,0:T(8,128)(2,1)S(1)}, u32[]{:S(2)}) copy-start(bf16[264,128]{1,0:T(8,128)(2,1)S(1)} %collective-permute-done.7.refs_2_) | copy-start | bytes 202756
  100.1 2.9 %copy-start.8 = (bf16[264,128]{1,0:T(8,128)(2,1)}, bf16[264,128]{1,0:T(8,128)(2,1)S(1)}, u32[]{:S(2)}) copy-start(bf16[264,128]{1,0:T(8,128)(2,1)S(1)} %collective-permute-done.8.refs_3_) | copy-start | bytes 202756
  102.2 0.9 copy-start.9
  102.2 0.9 copy-start.10
  103.0 0.6 copy-start.11
  110.4 11.5 %copy-start.13 = (s32[1,2]{1,0:T(1,128)S(1)}, s32[1,2]{1,0:T(1,128)}, u32[]{:S(2)}) copy-start(s32[1,2]{1,0:T(1,128)} %own_ref.1) | copy-start | bytes 28
  110.4 15.5 %copy-start.12 = (s32[16]{0:T(128)S(1)}, s32[16]{0:T(128)}, u32[]{:S(2)}) copy-start(s32[16]{0:T(128)} %fusion.len_ref) | copy-start | bytes 196
  115.5 31.1 %all-to-all-start.2 = ((bf16[16,128,256]{2,1,0:T(8,128)(2,1)}), bf16[16,128,256]{2,1,0:T(8,128)(2,1)S(1)}, u32[]{:S(2)}, u32[]{:S(2)}) async-start(bf16[16,128,256]{2,1,0:T(8,128)(2,1)} %bitcast.30), calls=%async_computation.2 | async-start | bytes 2097152 | tf_op jit(solution)/shard_map/all_to_all | solution.py:304
  123.8 5.1 %collective-permute-start.14 = (f32[1,1]{1,0:T(1,128)}, f32[1,1]{1,0:T(1,128)}, u32[]{:S(2)}, u32[]{:S(2)}) collective-permute-start(f32[1,1]{1,0:T(1,128)} %bitcast.8), channel_id=1, source_target_pairs={{0,48},{16,32},{32,16},{48,0},{64,112},{80,96},{96,80},{112,64},{1... | collective-permute-start | bytes 20 | tf_op jit(solution)/shard_map/ppermute | solution.py:313
  123.8 4.5 %collective-permute-start.13 = (f32[1,1]{1,0:T(1,128)}, f32[1,1]{1,0:T(1,128)}, u32[]{:S(2)}, u32[]{:S(2)}) collective-permute-start(f32[1,1]{1,0:T(1,128)} %bitcast.8), channel_id=1, source_target_pairs={{0,32},{16,48},{32,0},{48,16},{64,96},{80,112},{96,64},{112,80},{1... | collective-permute-start | bytes 20 | tf_op jit(solution)/shard_map/ppermute | solution.py:313
  125.7 1.3 collective-permute-start.12
  129.5 15.4 %collective-permute-start.17 = (f32[1,1]{1,0:T(1,128)}, f32[1,1]{1,0:T(1,128)}, u32[]{:S(2)}, u32[]{:S(2)}) collective-permute-start(f32[1,1]{1,0:T(1,128)} %add.87), channel_id=1, source_target_pairs={{0,192},{16,208},{32,224},{48,240},{64,128},{80,144},{96,160},{112... | collective-permute-start | bytes 20 | tf_op jit(solution)/shard_map/ppermute | solution.py:313
  136.8 7.4 %collective-permute-start.16 = (f32[1,1]{1,0:T(1,128)}, f32[1,1]{1,0:T(1,128)}, u32[]{:S(2)}, u32[]{:S(2)}) collective-permute-start(f32[1,1]{1,0:T(1,128)} %add.87), channel_id=1, source_target_pairs={{0,128},{16,144},{32,160},{48,176},{64,192},{80,208},{96,224},{112... | collective-permute-start | bytes 20 | tf_op jit(solution)/shard_map/ppermute | solution.py:313
  139.1 4.4 %collective-permute-start.15 = (f32[1,1]{1,0:T(1,128)}, f32[1,1]{1,0:T(1,128)}, u32[]{:S(2)}, u32[]{:S(2)}) collective-permute-start(f32[1,1]{1,0:T(1,128)} %add.87), channel_id=1, source_target_pairs={{0,64},{16,80},{32,96},{48,112},{64,0},{80,16},{96,32},{112,48},{1... | collective-permute-start | bytes 20 | tf_op jit(solution)/shard_map/ppermute | solution.py:313

commit v5 on v4

--- a/solution.py
+++ b/solution.py
@@ -112,13 +112,37 @@
         o_ref[h // 2, length:, to] = den.astype(BF16)
 
 
-def prompt_kernel(ids_ref, q_ref, w_ref, *refs):
+def phi_kernel(ids_ref, q_ref, w_ref, o_ref):
+    i = pl.program_id(0)
+    me = lax.axis_index("dp")
+    width = w_ref.shape[1]
+    many = o_ref.shape[1] // BLK
+    pieces = q_ref.shape[1] // BLK
+    xs = []
+    for g in range(0, many, 4):
+        rows = []
+        for j in range(g, g + 4):
+            b = ids_ref[i * many + j]
+            rows.append(q_ref[b // pieces, pl.ds(pl.multiple_of(b % pieces * BLK, BLK), BLK), :])
+        xs.append(jnp.concatenate(rows, axis=0))
+    units = [(g, h) for g in range(len(xs)) for h in range(2)]
+    phis = feats(
+        [xs[g][:, h * width : (h + 1) * width] for g, h in units],
+        [w_ref[2 * me + h] for g, h in units],
+    )
+    for phi, (g, h) in zip(phis, units):
+        o_ref[h, 4 * g * BLK : 4 * (g + 1) * BLK, :] = phi.T
+
+
+def combine_kernel(ids_ref, len_ref, part_ref, phi_ref, *refs):
     parts = refs[: 2 * SIDE]
-    num_ref, den_ref, s_ref, t_ref = refs[2 * SIDE :]
+    o_ref, s_ref, t_ref = refs[2 * SIDE :]
+    length = part_ref.shape[1] - EXTRA
+    width = part_ref.shape[2] // 2
+    full = phi_ref.shape[2]
+    pieces = length // BLK
+    many = phi_ref.shape[1] // BLK
     i = pl.program_id(0)
-    width = w_ref.shape[1]
-    full = 2 * w_ref.shape[2]
-    many = num_ref.shape[0]
 
     @pl.when(i == 0)
     def _():
@@ -130,46 +154,24 @@
             row = jnp.concatenate([acc[full : full + 1], acc[full + 1 : full + 2]], axis=1)
             t_ref[h] = jnp.broadcast_to(row, t_ref.shape[1:]).astype(BF16)
 
-    pieces = q_ref.shape[1] // BLK
-    xs = []
-    for g in range(0, many, 4):
-        rows = []
-        for j in range(g, g + 4):
-            b = ids_ref[i * many + j]
-            rows.append(q_ref[b // pieces, pl.ds(pl.multiple_of(b % pieces * BLK, BLK), BLK), :])
-        xs.append(jnp.concatenate(rows, axis=0))
-    cols = [slice(h * width, (h + 1) * width) for h in range(2)]
-    units = [(g, h) for g in range(len(xs)) for h in range(2)]
-    phis = feats([xs[g][:, cols[h]] for g, h in units], [w_ref[h] for g, h in units])
-    phis = [phi.T for phi in phis]
-    for phi, (g, h) in zip(phis, units):
-        num = mm(phi, s_ref[h]).astype(BF16)
-        den = mm(phi, t_ref[h], NT).astype(BF16)
-        num_ref[4 * g : 4 * g + 4, :, cols[h]] = num.reshape(4, BLK, width)
-        den_ref[4 * g : 4 * g + 4, :, cols[h]] = den.reshape(4, BLK, width)
-
-
-def combine_kernel(ids_ref, len_ref, part_ref, num_ref, den_ref, o_ref):
-    length = part_ref.shape[1] - EXTRA
-    width = part_ref.shape[2] // 2
-    pieces = length // BLK
-    many = num_ref.shape[0]
-    i = pl.program_id(0)
+    nums = [mm(phi_ref[h], s_ref[h]).astype(BF16) for h in range(2)]
+    dens = [mm(phi_ref[h], t_ref[h], NT).astype(BF16) for h in range(2)]
     rid = lax.broadcasted_iota(jnp.int32, (EXTRA, width), 0)
     row = lax.broadcasted_iota(jnp.int32, (BLK, 1), 0)
     for j in range(many):
         b = ids_ref[i * many + j]
         r, c = b // pieces, b % pieces
         pick = (rid // 2 == c // 2).astype(BF16)
+        rows = slice(j * BLK, (j + 1) * BLK)
         for h in range(2):
             cols = slice(h * width, (h + 1) * width)
             num = part_ref[r, pl.ds(pl.multiple_of(c * BLK, BLK), BLK), cols].astype(F32)
             den = mm(part_ref[r, length:, cols], pick, TN)
             den = jnp.where(c % 2 == 0, den[:BLK], den[BLK:])
-            num = num_ref[j, :, cols].astype(F32) + num
-            den = den_ref[j, :, cols].astype(F32) + den
+            num = nums[h][rows].astype(F32) + num
+            den = dens[h][rows].astype(F32) + den
             out = jnp.where(row < len_ref[r] - c * BLK, num / den, 0.0)
-            o_ref[j * BLK : (j + 1) * BLK, cols] = out.astype(BF16)
+            o_ref[rows, cols] = out.astype(BF16)
 
 
 def hop(dx, dy):
@@ -195,7 +197,6 @@
 ):
     dp = lax.axis_size("dp")
     groups = lax.axis_size("group")
-    me = lax.axis_index("dp")
     heads, width, feat = feat_q.shape
     length = resp_q.shape[1]
     pieces = length // BLK
@@ -268,39 +269,36 @@
 
     total = dp * slots
     many = 8
-    own_w = lax.dynamic_slice_in_dim(feat_q, 2 * me, 2, 0)
-    row_spec = pl.BlockSpec((many, BLK, two), lambda i: (i, 0, 0))
-    num, den = pl.pallas_call(
-        prompt_kernel,
+    phi = pl.pallas_call(
+        phi_kernel,
         grid=(total // many,),
         in_specs=[
             pl.BlockSpec(memory_space=pltpu.SMEM),
             pl.BlockSpec((dp, tall, two), lambda i: (0, 0, 0)),
-            pl.BlockSpec((2, width, feat), lambda i: (0, 0, 0)),
+            pl.BlockSpec(feat_q.shape, lambda i: (0, 0, 0)),
+        ],
+        out_specs=pl.BlockSpec((2, many * BLK, 2 * feat), lambda i: (0, i, 0)),
+        out_shape=jax.ShapeDtypeStruct((2, total * BLK, 2 * feat), BF16),
+        name="phi",
+    )(ids, q_all, feat_q)
+    out = pl.pallas_call(
+        combine_kernel,
+        grid=(total // many,),
+        in_specs=[
+            pl.BlockSpec(memory_space=pltpu.SMEM),
+            pl.BlockSpec(memory_space=pltpu.SMEM),
+            pl.BlockSpec((dp, tall, two), lambda i: (0, 0, 0)),
+            pl.BlockSpec((2, many * BLK, 2 * feat), lambda i: (0, i, 0)),
         ]
         + [pl.BlockSpec((srows, width), lambda i: (0, 0))] * (2 * SIDE),
-        out_specs=[row_spec, row_spec],
-        out_shape=[jax.ShapeDtypeStruct((total, BLK, two), BF16)] * 2,
+        out_specs=pl.BlockSpec((many * BLK, two), lambda i: (i, 0)),
+        out_shape=jax.ShapeDtypeStruct((total * BLK, two), BF16),
         scratch_shapes=[
             pltpu.VMEM((2, 2 * feat, width), BF16),
             pltpu.VMEM((2, width, 2 * feat), BF16),
         ],
-        name="prompt",
-    )(ids, q_all, own_w, *states)
-    out = pl.pallas_call(
-        combine_kernel,
-        grid=(total // 8,),
-        in_specs=[
-            pl.BlockSpec(memory_space=pltpu.SMEM),
-            pl.BlockSpec(memory_space=pltpu.SMEM),
-            pl.BlockSpec((dp, tall, two), lambda i: (0, 0, 0)),
-            pl.BlockSpec((8, BLK, two), lambda i: (i, 0, 0)),
-            pl.BlockSpec((8, BLK, two), lambda i: (i, 0, 0)),
-        ],
-        out_specs=pl.BlockSpec((8 * BLK, two), lambda i: (i, 0)),
-        out_shape=jax.ShapeDtypeStruct((total * BLK, two), BF16),
         name="combine",
-    )(ids, lens, inner, num, den)
+    )(ids, lens, inner, phi, *states)
     out = lax.all_to_all(out.reshape(dp, slots * BLK, two), "dp", 0, 0, tiled=True)
     attn = jnp.swapaxes(out, 0, 1).reshape(1, slots * BLK, heads * width)
 

time: 149 us -> 149 us (level)
  transfers between devices with their start and end apart: 21 -> 21, of which waited for: 9 -> 8; matrix products, arithmetic and copies ran while one was open for 4% -> 3% of each run, Pallas kernels for 18% -> 17%
where the time goes in v5:
time: 149 us; the launch traced here: 148 us
  starting transfers between devices  52.1 us (35%)
  waiting for transfers between devices  47.8 us (32%)
  Pallas kernels  34.1 us (23%)
  between operations  8 us (5%)
  local copies, waits for them, and re-layouts  3.74 us (3%)
  other arithmetic  2.58 us (2%)
    ppermute x6, waiting for transfers between devices, body(): lax.ppermute(states[i], 'dp', hop(s, 0) if p == 0 else hop(0, s))  24.3 us
    all_to_all x1, waiting for transfers between devices, body(): q_all = lax.all_to_all(q_all, 'dp', 0, 0, tiled=True)  18.3 us
    ppermute x6, starting transfers between devices, body(): lax.ppermute(spread, 'group', [(g, g ^ step * i) for g in range(groups)])  14.3 us
    pallas_call x1, Pallas kernels, body(): pl.pallas_call(intra_kernel, grid=(heads // 4,), in_specs=[pl.BlockSpec((...  11.6 us
    ppermute x6, starting transfers between devices, body(): lax.ppermute(states[i], 'dp', hop(0, s) if p == 0 else hop(s, 0))  9.11 us
    ppermute x6, starting transfers between devices, body(): lax.ppermute(states[i], 'dp', hop(s, 0) if p == 0 else hop(0, s))  9.06 us
    all_to_all x1, starting transfers between devices, body(): q_all = lax.all_to_all(q_all, 'dp', 0, 0, tiled=True)  7.39 us
    all_to_all x1, starting transfers between devices, body(): lax.all_to_all(out.reshape(dp, slots * BLK, two), 'dp', 0, 0, tiled=True)  6.65 us
  transfers between devices with their start and end apart: 21, of which 8 were waited for; matrix products, arithmetic and copies ran while one was open for 3% of the time, Pallas kernels for 17%

profile of v5, /device:TPU:8, one launch (start us, length us, event | category | flops | bytes accessed | tf_op | source)
XLA Modules:
  0.0 148.4 jit_solution(10905434886751500995)
XLA Ops:
  1.9 2.7 %spread.1 = bf16[16,264,256]{2,1,0:T(8,128)(2,1)} custom-call(s32[1,2]{1,0:T(1,128)} %own_ref.1, s32[1,1]{1,0:T(1,128)S(6)} %copy.20.len_ref, f32[1,1]{1,0:T(1,128)S(6)} %copy.21.rew_ref, bf16[256,4096]{1,0:T(8,128)(2,1)} %bitcast.27), custom_call_target="tpu_custom_call" | custom-call | tf_op jit(solution)/shard_map/spread/pallas_call | solution.py:209
  4.6 7.4 %all-to-all-start = ((bf16[16,264,256]{2,1,0:T(8,128)(2,1)}), bf16[16,264,256]{2,1,0:T(8,128)(2,1)S(1)}, u32[]{:S(2)}, u32[]{:S(2)}) async-start(bf16[16,264,256]{2,1,0:T(8,128)(2,1)} %spread.1), calls=%async_computation | async-start | bytes 4325376 | tf_op jit(solution)/shard_map/all_to_all | solution.py:222
  12.0 11.6 %intra.1 = bf16[16,264,256]{2,1,0:T(8,128)(2,1)} custom-call(bf16[256,4096]{1,0:T(8,128)(2,1)} %bitcast.28, bf16[256,4096]{1,0:T(8,128)(2,1)} %bitcast.31, bf16[256,4096]{1,0:T(8,128)(2,1)} %bitcast.32, bf16[32,128,128]{2,1,0:T(8,128)(2,1)} %w_ref.2, bf16[32,128,128]{2,1,0:T(8,128)(2,1)} %w_ref.3), custom_call_target="tpu_custom_call" | custom-call | tf_op jit(solution)/shard_map/intra/pallas_call | solution.py:259
  23.6 18.3 %all-to-all-done.q_ref = bf16[16,264,256]{2,1,0:T(8,128)(2,1)S(1)} async-done(((bf16[16,264,256]{2,1,0:T(8,128)(2,1)}), bf16[16,264,256]{2,1,0:T(8,128)(2,1)S(1)}, u32[]{:S(2)}, u32[]{:S(2)}) %all-to-all-start) | async-done | bytes 2162720 | tf_op jit(solution)/shard_map/all_to_all | solution.py:222
  41.9 5.6 %all-to-all-start.1 = ((bf16[16,264,256]{2,1,0:T(8,128)(2,1)}), bf16[16,264,256]{2,1,0:T(8,128)(2,1)}, u32[]{:S(2)}, u32[]{:S(2)}) async-start(bf16[16,264,256]{2,1,0:T(8,128)(2,1)} %intra.1), calls=%async_computation.1 | async-start | bytes 4325376 | tf_op jit(solution)/shard_map/all_to_all | solution.py:268
  48.1 6.2 %state.1 = (bf16[4,264,128]{2,1,0:T(8,128)(2,1)}, bf16[4,264,128]{2,1,0:T(8,128)(2,1)}, bf16[4,264,128]{2,1,0:T(8,128)(2,1)}, bf16[4,264,128]{2,1,0:T(8,128)(2,1...) custom-call(s32[1]{0:T(128)S(6)} %copy.19.n_ref, ...), custom_call_target="tpu_custom_call" | custom-call | tf_op jit(solution)/shard_map/state/pallas_call | solution.py:229
  54.3 1.5 %collective-permute-start = (bf16[4,264,128]{2,1,0:T(8,128)(2,1)}, bf16[4,264,128]{2,1,0:T(8,128)(2,1)S(1)}, u32[]{:S(2)}, u32[]{:S(2)}) collective-permute-start(bf16[4,264,128]{2,1,0:T(8,128)(2,1)} %get-tuple-element.19), channel_id=1, source_target_pairs={{0,4},{1,5},{2,6},{3,7},{4,8},{5,9},{6,10},{7,11},{8,12},{9,13},{1... | collective-permute-start | bytes 811016 | tf_op jit(solution)/shard_map/ppermute | solution.py:246
  55.8 2.7 %collective-permute-start.1 = (bf16[4,264,128]{2,1,0:T(8,128)(2,1)}, bf16[4,264,128]{2,1,0:T(8,128)(2,1)S(1)}, u32[]{:S(2)}, u32[]{:S(2)}) collective-permute-start(bf16[4,264,128]{2,1,0:T(8,128)(2,1)} %get-tuple-element.20), channel_id=1, source_target_pairs={{0,8},{1,9},{2,10},{3,11},{4,12},{5,13},{6,14},{7,15},{8,0},{9,1},... | collective-permute-start | bytes 811016 | tf_op jit(solution)/shard_map/ppermute | solution.py:246
  58.5 1.4 collective-permute-start.2
  59.9 1.5 collective-permute-start.3
  61.4 1.2 collective-permute-start.4
  62.6 18.4 %collective-permute-done.refs_1_ = bf16[4,264,128]{2,1,0:T(8,128)(2,1)S(1)} collective-permute-done((bf16[4,264,128]{2,1,0:T(8,128)(2,1)}, bf16[4,264,128]{2,1,0:T(8,128)(2,1)S(1)}, u32[]{:S(2)}, u32[]{:S(2)}) %collective-permute-start) | collective-permute-done | bytes 270368 | tf_op jit(solution)/shard_map/ppermute | solution.py:246
  81.0 0.8 collective-permute-start.5
  81.7 2.6 %collective-permute-done.1.refs_2_ = bf16[4,264,128]{2,1,0:T(8,128)(2,1)S(1)} collective-permute-done((bf16[4,264,128]{2,1,0:T(8,128)(2,1)}, bf16[4,264,128]{2,1,0:T(8,128)(2,1)S(1)}, u32[]{:S(2)}, u32[]{:S(2)}) %collective-permute-start.1) | collective-permute-done | bytes 270368 | tf_op jit(solution)/shard_map/ppermute | solution.py:246
  84.3 0.0 collective-permute-done.2.refs_3_
  84.4 0.0 collective-permute-done.3.refs_5_
  84.4 0.0 copy-start.4
  84.4 0.0 collective-permute-done.4.refs_6_
  84.4 0.0 copy-start.5
  84.4 3.3 %collective-permute-done.5.refs_7_ = bf16[4,264,128]{2,1,0:T(8,128)(2,1)} collective-permute-done((bf16[4,264,128]{2,1,0:T(8,128)(2,1)}, bf16[4,264,128]{2,1,0:T(8,128)(2,1)}, u32[]{:S(2)}, u32[]{:S(2)}) %collective-permute-start.5) | collective-permute-done | bytes 270368 | tf_op jit(solution)/shard_map/ppermute | solution.py:246
  87.7 0.0 copy-done.1
  87.7 0.0 copy-done.2
  87.8 2.6 %add.102 = (bf16[264,128]{1,0:T(8,128)(2,1)}, bf16[264,128]{1,0:T(8,128)(2,1)}, bf16[264,128]{1,0:T(8,128)(2,1)}, bf16[264,128]{1,0:T(8,128)(2,1)}, bf16[264,128...) custom-call(bf16[4,264,128]{2,1,0:T(8,128)(2,1)} %get-tuple-element.18.refs_0_, ...), custom_call_target="tpu_custom_call" | custom-call | tf_op jit(solution)/shard_map/add/pallas_call | solution.py:247
  90.3 0.9 collective-permute-start.6
  91.2 2.0 %collective-permute-start.7 = (bf16[264,128]{1,0:T(8,128)(2,1)}, bf16[264,128]{1,0:T(8,128)(2,1)S(1)}, u32[]{:S(2)}, u32[]{:S(2)}) collective-permute-start(bf16[264,128]{1,0:T(8,128)(2,1)} %get-tuple-element.28), channel_id=1, source_target_pairs={{0,2},{1,3},{2,0},{3,1},{4,6},{5,7},{6,4},{7,5},{8,10},{9,11},{10,... | collective-permute-start | bytes 202760 | tf_op jit(solution)/shard_map/ppermute | solution.py:257
  93.2 2.5 %collective-permute-start.8 = (bf16[264,128]{1,0:T(8,128)(2,1)}, bf16[264,128]{1,0:T(8,128)(2,1)S(1)}, u32[]{:S(2)}, u32[]{:S(2)}) collective-permute-start(bf16[264,128]{1,0:T(8,128)(2,1)} %get-tuple-element.29), channel_id=1, source_target_pairs={{0,3},{1,0},{2,1},{3,2},{4,7},{5,4},{6,5},{7,6},{8,11},{9,8},{10,9... | collective-permute-start | bytes 202760 | tf_op jit(solution)/shard_map/ppermute | solution.py:257
  95.7 0.0 collective-permute-start.9
  95.7 2.2 %collective-permute-start.10 = (bf16[264,128]{1,0:T(8,128)(2,1)}, bf16[264,128]{1,0:T(8,128)(2,1)S(1)}, u32[]{:S(2)}, u32[]{:S(2)}) collective-permute-start(bf16[264,128]{1,0:T(8,128)(2,1)} %get-tuple-element.32), channel_id=1, source_target_pairs={{0,8},{1,9},{2,10},{3,11},{4,12},{5,13},{6,14},{7,15},{8,0},{9,1},... | collective-permute-start | bytes 202760 | tf_op jit(solution)/shard_map/ppermute | solution.py:257
  98.0 0.6 reshape.155.ids_ref
  98.6 5.3 %phi.1.phi_ref = bf16[2,2048,256]{2,1,0:T(8,128)(2,1)} custom-call(s32[32]{0:T(128)} %reshape.155.ids_ref, bf16[16,264,256]{2,1,0:T(8,128)(2,1)} %copy-done, bf16[32,128,128]{2,1,0:T(8,128)(2,1)} %w_ref.2), custom_call_target="tpu_custom_call" | custom-call | tf_op jit(solution)/shard_map/phi/pallas_call | solution.py:272
  103.9 0.0 collective-permute-done.6.refs_1_
  103.9 1.5 %collective-permute-start.11 = (bf16[264,128]{1,0:T(8,128)(2,1)S(1)}, bf16[264,128]{1,0:T(8,128)(2,1)S(1)}, u32[]{:S(2)}, u32[]{:S(2)}) collective-permute-start(bf16[264,128]{1,0:T(8,128)(2,1)S(1)} %copy-done.14), channel_id=1, source_target_pairs={{0,12},{1,13},{2,14},{3,15},{4,0},{5,1},{6,2},{7,3},{8,4},{9,5},{1... | collective-permute-start | bytes 202760 | tf_op jit(solution)/shard_map/ppermute | solution.py:257
  105.4 0.7 fusion.len_ref
  106.1 0.0 collective-permute-done.7.refs_2_
  106.1 0.0 collective-permute-done.8.refs_3_
  106.1 0.0 collective-permute-done.9.refs_5_
  106.1 0.0 collective-permute-done.10.refs_6_
  106.1 0.0 copy-start.10
  106.1 2.3 %collective-permute-done.11.refs_7_ = bf16[264,128]{1,0:T(8,128)(2,1)S(1)} collective-permute-done((bf16[264,128]{1,0:T(8,128)(2,1)S(1)}, bf16[264,128]{1,0:T(8,128)(2,1)S(1)}, u32[]{:S(2)}, u32[]{:S(2)}) %collective-permute-start.11) | collective-permute-done | bytes 67616 | tf_op jit(solution)/shard_map/ppermute | solution.py:257
  108.4 0.0 all-to-all-done.1.part_ref
  108.5 0.6 copy-done.11
  109.1 5.8 %combine.1 = bf16[2048,256]{1,0:T(8,128)(2,1)} custom-call(s32[32]{0:T(128)} %reshape.155.ids_ref, s32[16]{0:T(128)} %fusion.len_ref, bf16[16,264,256]{2,1,0:T(8,128)(2,1)} %all-to-all-done.1.part_ref, bf16[2,2048,256]{2,1,0:T(8,128)(2,1)} %phi.1.phi_ref, bf16[264,128]{1,0:T(8,128)(2,1)} %get-tuple-element.26.refs_0_, bf16[264,128]{1,0:T(8,128)(2,1)} %copy-done.6, ...), custom_call_target="tpu_custom_call" | custom-call | tf_op jit(solution)/shard_map/combine/pallas_call | solution.py:284
  114.9 6.6 %all-to-all-start.2 = ((bf16[16,128,256]{2,1,0:T(8,128)(2,1)}), bf16[16,128,256]{2,1,0:T(8,128)(2,1)S(1)}, u32[]{:S(2)}, u32[]{:S(2)}) async-start(bf16[16,128,256]{2,1,0:T(8,128)(2,1)} %bitcast.29), calls=%async_computation.2 | async-start | bytes 2097152 | tf_op jit(solution)/shard_map/all_to_all | solution.py:302
  121.5 0.7 fusion.2
  122.9 0.6 multiply_reduce_fusion
  123.5 0.0 collective-permute-start.14
  123.5 1.9 %collective-permute-start.13 = (f32[1,1]{1,0:T(1,128)}, f32[1,1]{1,0:T(1,128)}, u32[]{:S(2)}, u32[]{:S(2)}) collective-permute-start(f32[1,1]{1,0:T(1,128)} %bitcast.8), channel_id=1, source_target_pairs={{0,32},{16,48},{32,0},{48,16},{64,96},{80,112},{96,64},{112,80},{1... | collective-permute-start | bytes 20 | tf_op jit(solution)/shard_map/ppermute | solution.py:311
  125.4 0.1 collective-permute-start.12
  125.5 0.2 select_reduce_fusion.1
  125.7 1.0 collective-permute-done.12
  128.0 0.0 collective-permute-done.13
  128.6 0.0 collective-permute-done.14
  129.3 7.3 %collective-permute-start.17 = (f32[1,1]{1,0:T(1,128)}, f32[1,1]{1,0:T(1,128)}, u32[]{:S(2)}, u32[]{:S(2)}) collective-permute-start(f32[1,1]{1,0:T(1,128)} %add.83), channel_id=1, source_target_pairs={{0,192},{16,208},{32,224},{48,240},{64,128},{80,144},{96,160},{112... | collective-permute-start | bytes 20 | tf_op jit(solution)/shard_map/ppermute | solution.py:311
  136.6 2.2 %collective-permute-start.16 = (f32[1,1]{1,0:T(1,128)}, f32[1,1]{1,0:T(1,128)}, u32[]{:S(2)}, u32[]{:S(2)}) collective-permute-start(f32[1,1]{1,0:T(1,128)} %add.83), channel_id=1, source_target_pairs={{0,128},{16,144},{32,160},{48,176},{64,192},{80,208},{96,224},{112... | collective-permute-start | bytes 20 | tf_op jit(solution)/shard_map/ppermute | solution.py:311
  138.8 2.7 %collective-permute-start.15 = (f32[1,1]{1,0:T(1,128)}, f32[1,1]{1,0:T(1,128)}, u32[]{:S(2)}, u32[]{:S(2)}) collective-permute-start(f32[1,1]{1,0:T(1,128)} %add.83), channel_id=1, source_target_pairs={{0,64},{16,80},{32,96},{48,112},{64,0},{80,16},{96,32},{112,48},{1... | collective-permute-start | bytes 20 | tf_op jit(solution)/shard_map/ppermute | solution.py:311
  141.5 1.7 %collective-permute-done.15 = f32[1,1]{1,0:T(1,128)} collective-permute-done((f32[1,1]{1,0:T(1,128)}, f32[1,1]{1,0:T(1,128)}, u32[]{:S(2)}, u32[]{:S(2)}) %collective-permute-start.15) | collective-permute-done | bytes 36 | tf_op jit(solution)/shard_map/ppermute | solution.py:311
  143.9 0.3 collective-permute-done.16
  145.5 0.1 divide_reduce_fusion
  145.6 0.2 select_reduce_fusion
  145.8 0.1 compare_select_fusion
  145.9 0.6 select_n.47
  146.5 0.0 all-to-all-done.2
  146.5 0.6 copy.15
  147.1 1.3 reshape.157
  (29 shorter events, 0.1 us)
Async XLA Ops:
  4.6 37.2 %all-to-all-start = ((bf16[16,264,256]{2,1,0:T(8,128)(2,1)}), bf16[16,264,256]{2,1,0:T(8,128)(2,1)S(1)}, u32[]{:S(2)}, u32[]{:S(2)}) async-start(bf16[16,264,256]{2,1,0:T(8,128)(2,1)} %spread.1), calls=%async_computation | async-start | bytes 4325376 | tf_op jit(solution)/shard_map/all_to_all | solution.py:222
  41.8 56.1 %copy-start = (bf16[16,264,256]{2,1,0:T(8,128)(2,1)}, bf16[16,264,256]{2,1,0:T(8,128)(2,1)S(1)}, u32[]{:S(2)}) copy-start(bf16[16,264,256]{2,1,0:T(8,128)(2,1)S(1)} %all-to-all-done.q_ref) | copy-start | bytes 6488068
  41.9 66.6 %all-to-all-start.1 = ((bf16[16,264,256]{2,1,0:T(8,128)(2,1)}), bf16[16,264,256]{2,1,0:T(8,128)(2,1)}, u32[]{:S(2)}, u32[]{:S(2)}) async-start(bf16[16,264,256]{2,1,0:T(8,128)(2,1)} %intra.1), calls=%async_computation.1 | async-start | bytes 4325376 | tf_op jit(solution)/shard_map/all_to_all | solution.py:268
  54.3 26.7 %collective-permute-start = (bf16[4,264,128]{2,1,0:T(8,128)(2,1)}, bf16[4,264,128]{2,1,0:T(8,128)(2,1)S(1)}, u32[]{:S(2)}, u32[]{:S(2)}) collective-permute-start(bf16[4,264,128]{2,1,0:T(8,128)(2,1)} %get-tuple-element.19), channel_id=1, source_target_pairs={{0,4},{1,5},{2,6},{3,7},{4,8},{5,9},{6,10},{7,11},{8,12},{9,13},{1... | collective-permute-start | bytes 811016 | tf_op jit(solution)/shard_map/ppermute | solution.py:246
  55.8 28.6 %collective-permute-start.1 = (bf16[4,264,128]{2,1,0:T(8,128)(2,1)}, bf16[4,264,128]{2,1,0:T(8,128)(2,1)S(1)}, u32[]{:S(2)}, u32[]{:S(2)}) collective-permute-start(bf16[4,264,128]{2,1,0:T(8,128)(2,1)} %get-tuple-element.20), channel_id=1, source_target_pairs={{0,8},{1,9},{2,10},{3,11},{4,12},{5,13},{6,14},{7,15},{8,0},{9,1},... | collective-permute-start | bytes 811016 | tf_op jit(solution)/shard_map/ppermute | solution.py:246
  58.5 25.8 %collective-permute-start.2 = (bf16[4,264,128]{2,1,0:T(8,128)(2,1)}, bf16[4,264,128]{2,1,0:T(8,128)(2,1)S(1)}, u32[]{:S(2)}, u32[]{:S(2)}) collective-permute-start(bf16[4,264,128]{2,1,0:T(8,128)(2,1)} %get-tuple-element.21), channel_id=1, source_target_pairs={{0,12},{1,13},{2,14},{3,15},{4,0},{5,1},{6,2},{7,3},{8,4},{9,5},{1... | collective-permute-start | bytes 811016 | tf_op jit(solution)/shard_map/ppermute | solution.py:246
  59.9 24.4 %collective-permute-start.3 = (bf16[4,264,128]{2,1,0:T(8,128)(2,1)}, bf16[4,264,128]{2,1,0:T(8,128)(2,1)S(1)}, u32[]{:S(2)}, u32[]{:S(2)}) collective-permute-start(bf16[4,264,128]{2,1,0:T(8,128)(2,1)} %get-tuple-element.23), channel_id=1, source_target_pairs={{0,1},{1,2},{2,3},{3,0},{4,5},{5,6},{6,7},{7,4},{8,9},{9,10},{10,1... | collective-permute-start | bytes 811016 | tf_op jit(solution)/shard_map/ppermute | solution.py:246
  61.4 23.0 %collective-permute-start.4 = (bf16[4,264,128]{2,1,0:T(8,128)(2,1)}, bf16[4,264,128]{2,1,0:T(8,128)(2,1)S(1)}, u32[]{:S(2)}, u32[]{:S(2)}) collective-permute-start(bf16[4,264,128]{2,1,0:T(8,128)(2,1)} %get-tuple-element.24), channel_id=1, source_target_pairs={{0,2},{1,3},{2,0},{3,1},{4,6},{5,7},{6,4},{7,5},{8,10},{9,11},{10,... | collective-permute-start | bytes 811016 | tf_op jit(solution)/shard_map/ppermute | solution.py:246
  80.9 6.8 %copy-start.1 = (bf16[4,264,128]{2,1,0:T(8,128)(2,1)}, bf16[4,264,128]{2,1,0:T(8,128)(2,1)S(1)}, u32[]{:S(2)}) copy-start(bf16[4,264,128]{2,1,0:T(8,128)(2,1)S(1)} %collective-permute-done.refs_1_) | copy-start | bytes 811012
  81.0 6.8 %collective-permute-start.5 = (bf16[4,264,128]{2,1,0:T(8,128)(2,1)}, bf16[4,264,128]{2,1,0:T(8,128)(2,1)}, u32[]{:S(2)}, u32[]{:S(2)}) collective-permute-start(bf16[4,264,128]{2,1,0:T(8,128)(2,1)} %get-tuple-element.25), channel_id=1, source_target_pairs={{0,3},{1,0},{2,1},{3,2},{4,7},{5,4},{6,5},{7,6},{8,11},{9,8},{10,9... | collective-permute-start | bytes 811016 | tf_op jit(solution)/shard_map/ppermute | solution.py:246
  84.3 3.4 %copy-start.2 = (bf16[4,264,128]{2,1,0:T(8,128)(2,1)}, bf16[4,264,128]{2,1,0:T(8,128)(2,1)S(1)}, u32[]{:S(2)}) copy-start(bf16[4,264,128]{2,1,0:T(8,128)(2,1)S(1)} %collective-permute-done.1.refs_2_) | copy-start | bytes 811012
  84.3 3.4 %copy-start.3 = (bf16[4,264,128]{2,1,0:T(8,128)(2,1)}, bf16[4,264,128]{2,1,0:T(8,128)(2,1)S(1)}, u32[]{:S(2)}) copy-start(bf16[4,264,128]{2,1,0:T(8,128)(2,1)S(1)} %collective-permute-done.2.refs_3_) | copy-start | bytes 811012
  84.4 3.4 %copy-start.4 = (bf16[4,264,128]{2,1,0:T(8,128)(2,1)}, bf16[4,264,128]{2,1,0:T(8,128)(2,1)S(1)}, u32[]{:S(2)}) copy-start(bf16[4,264,128]{2,1,0:T(8,128)(2,1)S(1)} %collective-permute-done.3.refs_5_) | copy-start | bytes 811012
  84.4 3.4 %copy-start.5 = (bf16[4,264,128]{2,1,0:T(8,128)(2,1)}, bf16[4,264,128]{2,1,0:T(8,128)(2,1)S(1)}, u32[]{:S(2)}) copy-start(bf16[4,264,128]{2,1,0:T(8,128)(2,1)S(1)} %collective-permute-done.4.refs_6_) | copy-start | bytes 811012
  90.3 13.5 %collective-permute-start.6 = (bf16[264,128]{1,0:T(8,128)(2,1)}, bf16[264,128]{1,0:T(8,128)(2,1)S(1)}, u32[]{:S(2)}, u32[]{:S(2)}) collective-permute-start(bf16[264,128]{1,0:T(8,128)(2,1)} %get-tuple-element.27), channel_id=1, source_target_pairs={{0,1},{1,2},{2,3},{3,0},{4,5},{5,6},{6,7},{7,4},{8,9},{9,10},{10,1... | collective-permute-start | bytes 202760 | tf_op jit(solution)/shard_map/ppermute | solution.py:257
  91.2 14.8 %collective-permute-start.7 = (bf16[264,128]{1,0:T(8,128)(2,1)}, bf16[264,128]{1,0:T(8,128)(2,1)S(1)}, u32[]{:S(2)}, u32[]{:S(2)}) collective-permute-start(bf16[264,128]{1,0:T(8,128)(2,1)} %get-tuple-element.28), channel_id=1, source_target_pairs={{0,2},{1,3},{2,0},{3,1},{4,6},{5,7},{6,4},{7,5},{8,10},{9,11},{10,... | collective-permute-start | bytes 202760 | tf_op jit(solution)/shard_map/ppermute | solution.py:257
  93.2 12.9 %collective-permute-start.8 = (bf16[264,128]{1,0:T(8,128)(2,1)}, bf16[264,128]{1,0:T(8,128)(2,1)S(1)}, u32[]{:S(2)}, u32[]{:S(2)}) collective-permute-start(bf16[264,128]{1,0:T(8,128)(2,1)} %get-tuple-element.29), channel_id=1, source_target_pairs={{0,3},{1,0},{2,1},{3,2},{4,7},{5,4},{6,5},{7,6},{8,11},{9,8},{10,9... | collective-permute-start | bytes 202760 | tf_op jit(solution)/shard_map/ppermute | solution.py:257
  95.7 10.4 %collective-permute-start.9 = (bf16[264,128]{1,0:T(8,128)(2,1)}, bf16[264,128]{1,0:T(8,128)(2,1)S(1)}, u32[]{:S(2)}, u32[]{:S(2)}) collective-permute-start(bf16[264,128]{1,0:T(8,128)(2,1)} %get-tuple-element.31), channel_id=1, source_target_pairs={{0,4},{1,5},{2,6},{3,7},{4,8},{5,9},{6,10},{7,11},{8,12},{9,13},{1... | collective-permute-start | bytes 202760 | tf_op jit(solution)/shard_map/ppermute | solution.py:257
  95.7 10.4 %collective-permute-start.10 = (bf16[264,128]{1,0:T(8,128)(2,1)}, bf16[264,128]{1,0:T(8,128)(2,1)S(1)}, u32[]{:S(2)}, u32[]{:S(2)}) collective-permute-start(bf16[264,128]{1,0:T(8,128)(2,1)} %get-tuple-element.32), channel_id=1, source_target_pairs={{0,8},{1,9},{2,10},{3,11},{4,12},{5,13},{6,14},{7,15},{8,0},{9,1},... | collective-permute-start | bytes 202760 | tf_op jit(solution)/shard_map/ppermute | solution.py:257
  98.6 5.3 %copy-start.14 = (bf16[264,128]{1,0:T(8,128)(2,1)S(1)}, bf16[264,128]{1,0:T(8,128)(2,1)}, u32[]{:S(2)}) copy-start(bf16[264,128]{1,0:T(8,128)(2,1)} %get-tuple-element.33) | copy-start | bytes 202756
  103.9 4.6 %copy-start.6 = (bf16[264,128]{1,0:T(8,128)(2,1)}, bf16[264,128]{1,0:T(8,128)(2,1)S(1)}, u32[]{:S(2)}) copy-start(bf16[264,128]{1,0:T(8,128)(2,1)S(1)} %collective-permute-done.6.refs_1_) | copy-start | bytes 202756
  103.9 4.5 %collective-permute-start.11 = (bf16[264,128]{1,0:T(8,128)(2,1)S(1)}, bf16[264,128]{1,0:T(8,128)(2,1)S(1)}, u32[]{:S(2)}, u32[]{:S(2)}) collective-permute-start(bf16[264,128]{1,0:T(8,128)(2,1)S(1)} %copy-done.14), channel_id=1, source_target_pairs={{0,12},{1,13},{2,14},{3,15},{4,0},{5,1},{6,2},{7,3},{8,4},{9,5},{1... | collective-permute-start | bytes 202760 | tf_op jit(solution)/shard_map/ppermute | solution.py:257
  106.1 2.3 %copy-start.7 = (bf16[264,128]{1,0:T(8,128)(2,1)}, bf16[264,128]{1,0:T(8,128)(2,1)S(1)}, u32[]{:S(2)}) copy-start(bf16[264,128]{1,0:T(8,128)(2,1)S(1)} %collective-permute-done.7.refs_2_) | copy-start | bytes 202756
  106.1 2.4 %copy-start.8 = (bf16[264,128]{1,0:T(8,128)(2,1)}, bf16[264,128]{1,0:T(8,128)(2,1)S(1)}, u32[]{:S(2)}) copy-start(bf16[264,128]{1,0:T(8,128)(2,1)S(1)} %collective-permute-done.8.refs_3_) | copy-start | bytes 202756
  106.1 2.3 %copy-start.9 = (bf16[264,128]{1,0:T(8,128)(2,1)}, bf16[264,128]{1,0:T(8,128)(2,1)S(1)}, u32[]{:S(2)}) copy-start(bf16[264,128]{1,0:T(8,128)(2,1)S(1)} %collective-permute-done.9.refs_5_) | copy-start | bytes 202756
  106.1 2.3 %copy-start.10 = (bf16[264,128]{1,0:T(8,128)(2,1)}, bf16[264,128]{1,0:T(8,128)(2,1)S(1)}, u32[]{:S(2)}) copy-start(bf16[264,128]{1,0:T(8,128)(2,1)S(1)} %collective-permute-done.10.refs_6_) | copy-start | bytes 202756
  108.4 0.6 copy-start.11
  109.0 12.5 %copy-start.13 = (s32[1,2]{1,0:T(1,128)S(1)}, s32[1,2]{1,0:T(1,128)}, u32[]{:S(2)}) copy-start(s32[1,2]{1,0:T(1,128)} %own_ref.1) | copy-start | bytes 28
  109.1 16.5 %copy-start.12 = (s32[16]{0:T(128)S(1)}, s32[16]{0:T(128)}, u32[]{:S(2)}) copy-start(s32[16]{0:T(128)} %fusion.len_ref) | copy-start | bytes 196
  114.9 31.6 %all-to-all-start.2 = ((bf16[16,128,256]{2,1,0:T(8,128)(2,1)}), bf16[16,128,256]{2,1,0:T(8,128)(2,1)S(1)}, u32[]{:S(2)}, u32[]{:S(2)}) async-start(bf16[16,128,256]{2,1,0:T(8,128)(2,1)} %bitcast.29), calls=%async_computation.2 | async-start | bytes 2097152 | tf_op jit(solution)/shard_map/all_to_all | solution.py:302
  123.5 5.1 %collective-permute-start.14 = (f32[1,1]{1,0:T(1,128)}, f32[1,1]{1,0:T(1,128)}, u32[]{:S(2)}, u32[]{:S(2)}) collective-permute-start(f32[1,1]{1,0:T(1,128)} %bitcast.8), channel_id=1, source_target_pairs={{0,48},{16,32},{32,16},{48,0},{64,112},{80,96},{96,80},{112,64},{1... | collective-permute-start | bytes 20 | tf_op jit(solution)/shard_map/ppermute | solution.py:311
  123.5 4.5 %collective-permute-start.13 = (f32[1,1]{1,0:T(1,128)}, f32[1,1]{1,0:T(1,128)}, u32[]{:S(2)}, u32[]{:S(2)}) collective-permute-start(f32[1,1]{1,0:T(1,128)} %bitcast.8), channel_id=1, source_target_pairs={{0,32},{16,48},{32,0},{48,16},{64,96},{80,112},{96,64},{112,80},{1... | collective-permute-start | bytes 20 | tf_op jit(solution)/shard_map/ppermute | solution.py:311
  125.4 1.3 collective-permute-start.12
  129.3 15.5 %collective-permute-start.17 = (f32[1,1]{1,0:T(1,128)}, f32[1,1]{1,0:T(1,128)}, u32[]{:S(2)}, u32[]{:S(2)}) collective-permute-start(f32[1,1]{1,0:T(1,128)} %add.83), channel_id=1, source_target_pairs={{0,192},{16,208},{32,224},{48,240},{64,128},{80,144},{96,160},{112... | collective-permute-start | bytes 20 | tf_op jit(solution)/shard_map/ppermute | solution.py:311
  136.6 7.6 %collective-permute-start.16 = (f32[1,1]{1,0:T(1,128)}, f32[1,1]{1,0:T(1,128)}, u32[]{:S(2)}, u32[]{:S(2)}) collective-permute-start(f32[1,1]{1,0:T(1,128)} %add.83), channel_id=1, source_target_pairs={{0,128},{16,144},{32,160},{48,176},{64,192},{80,208},{96,224},{112... | collective-permute-start | bytes 20 | tf_op jit(solution)/shard_map/ppermute | solution.py:311
  138.8 4.4 %collective-permute-start.15 = (f32[1,1]{1,0:T(1,128)}, f32[1,1]{1,0:T(1,128)}, u32[]{:S(2)}, u32[]{:S(2)}) collective-permute-start(f32[1,1]{1,0:T(1,128)} %add.83), channel_id=1, source_target_pairs={{0,64},{16,80},{32,96},{48,112},{64,0},{80,16},{96,32},{112,48},{1... | collective-permute-start | bytes 20 | tf_op jit(solution)/shard_map/ppermute | solution.py:311

commit v6 on v5

--- a/solution.py
+++ b/solution.py
@@ -134,7 +134,7 @@
         o_ref[h, 4 * g * BLK : 4 * (g + 1) * BLK, :] = phi.T
 
 
-def combine_kernel(ids_ref, len_ref, part_ref, phi_ref, *refs):
+def combine_kernel(ids_ref, len_ref, sq_ref, part_ref, phi_ref, *refs):
     parts = refs[: 2 * SIDE]
     o_ref, s_ref, t_ref = refs[2 * SIDE :]
     length = part_ref.shape[1] - EXTRA
@@ -154,6 +154,16 @@
             row = jnp.concatenate([acc[full : full + 1], acc[full + 1 : full + 2]], axis=1)
             t_ref[h] = jnp.broadcast_to(row, t_ref.shape[1:]).astype(BF16)
 
+    per = (o_ref.shape[1] - EXTRA) // BLK
+    cut = 2 * width // 8
+    col = lax.broadcasted_iota(jnp.int32, (EXTRA, 2 * width), 1)
+    r = jnp.broadcast_to(sq_ref[...], col.shape)
+    r1 = r.astype(BF16).astype(F32)
+    r2 = (r - r1).astype(BF16).astype(F32)
+    r3 = r - r1 - r2
+    low = jnp.where(col < cut, r1, jnp.where(col < 2 * cut, r2, r3)).astype(BF16)
+    for d in range(o_ref.shape[0]):
+        o_ref[d, per * BLK :, :] = low
     nums = [mm(phi_ref[h], s_ref[h]).astype(BF16) for h in range(2)]
     dens = [mm(phi_ref[h], t_ref[h], NT).astype(BF16) for h in range(2)]
     rid = lax.broadcasted_iota(jnp.int32, (EXTRA, width), 0)
@@ -171,7 +181,7 @@
             num = nums[h][rows].astype(F32) + num
             den = dens[h][rows].astype(F32) + den
             out = jnp.where(row < len_ref[r] - c * BLK, num / den, 0.0)
-            o_ref[rows, cols] = out.astype(BF16)
+            o_ref[j // per, j % per * BLK : (j % per + 1) * BLK, cols] = out.astype(BF16)
 
 
 def hop(dx, dy):
@@ -267,6 +277,14 @@
     )(q, k, v, feat_q, feat_k)
     inner = lax.all_to_all(inner, "dp", 0, 0, tiled=True)
 
+    centred = reward_all - jnp.sum(reward_all) / dp
+    squares = lax.ppermute(
+        jnp.sum(centred * centred).reshape(1, 1),
+        ("group", "dp"),
+        [(g * dp + d, (g + d) % groups * dp + d) for g in range(groups) for d in range(dp)],
+    )
+
+    short = slots * BLK + EXTRA
     total = dp * slots
     many = 8
     phi = pl.pallas_call(
@@ -287,33 +305,25 @@
         in_specs=[
             pl.BlockSpec(memory_space=pltpu.SMEM),
             pl.BlockSpec(memory_space=pltpu.SMEM),
+            pl.BlockSpec((1, 1), lambda i: (0, 0)),
             pl.BlockSpec((dp, tall, two), lambda i: (0, 0, 0)),
             pl.BlockSpec((2, many * BLK, 2 * feat), lambda i: (0, i, 0)),
         ]
         + [pl.BlockSpec((srows, width), lambda i: (0, 0))] * (2 * SIDE),
-        out_specs=pl.BlockSpec((many * BLK, two), lambda i: (i, 0)),
-        out_shape=jax.ShapeDtypeStruct((total * BLK, two), BF16),
+        out_specs=pl.BlockSpec((many // slots, short, two), lambda i: (i, 0, 0)),
+        out_shape=jax.ShapeDtypeStruct((dp, short, two), BF16),
         scratch_shapes=[
             pltpu.VMEM((2, 2 * feat, width), BF16),
             pltpu.VMEM((2, width, 2 * feat), BF16),
         ],
         name="combine",
-    )(ids, lens, inner, phi, *states)
-    out = lax.all_to_all(out.reshape(dp, slots * BLK, two), "dp", 0, 0, tiled=True)
-    attn = jnp.swapaxes(out, 0, 1).reshape(1, slots * BLK, heads * width)
-
-    centred = reward_all - jnp.sum(reward_all) / dp
-    spread = jnp.sum(centred * centred).reshape(1, 1)
-    step = 1
-    while step < groups:
-        total_sq = spread
-        for i in range(1, 4):
-            total_sq = total_sq + lax.ppermute(
-                spread, "group", [(g, g ^ (step * i)) for g in range(groups)]
-            )
-        spread = total_sq
-        step *= 4
-    advantage = centred / jnp.sqrt(spread[0, 0] / (groups * dp) + 1e-06)
+    )(ids, lens, squares, inner, phi, *states)
+    out = lax.all_to_all(out, "dp", 0, 0, tiled=True)
+    attn = jnp.swapaxes(out[:, : slots * BLK], 0, 1).reshape(1, slots * BLK, heads * width)
+
+    squares = out[:, slots * BLK, :].astype(F32)
+    spread = jnp.sum(squares[:, 0] + squares[:, part] + squares[:, 2 * part])
+    advantage = centred / jnp.sqrt(spread / (groups * dp) + 1e-06)
     own = assign[0]
     picker = (own // pieces)[:, None] == jnp.arange(dp)[None, :]
     slot_adv = jnp.sum(jnp.where(picker, advantage[None, :], 0.0), axis=1)

time: 149 us -> 155 us (1.040)
  waiting for transfers between devices: 47.8 us -> 65.4 us
  starting transfers between devices: 52.1 us -> 41.9 us
  between operations: 8 us -> 4.15 us
    all_to_all x1, waiting for transfers between devices: 0.01 us -> 18.7 us  [body(): out = lax.all_to_all(out, 'dp', 0, 0, tiled=True)]
    ppermute x6 -> x1, starting transfers between devices: 14.3 us -> 1.91 us  [body(): lax.ppermute(jnp.sum(centred * centred).reshape(1, 1), ('group', 'dp'), [...]
    all_to_all x1, starting transfers between devices: 6.65 us -> 9.05 us  [body(): out = lax.all_to_all(out, 'dp', 0, 0, tiled=True)]
    ppermute x6, waiting for transfers between devices: 2.29 us -> 0.4 us  [body(): lax.ppermute(states[i], 'dp', hop(0, s) if p == 0 else hop(s, 0))]
    ppermute x6 -> x1, waiting for transfers between devices: 2.92 us -> 3.73 us  [body(): lax.ppermute(jnp.sum(centred * centred).reshape(1, 1), ('group', 'dp'), [...]
  transfers between devices with their start and end apart: 21 -> 16, of which waited for: 8 -> 7; matrix products, arithmetic and copies ran while one was open for 3% -> 2% of each run, Pallas kernels for 17% -> 17%
where the time goes in v6:
time: 155 us; the launch traced here: 153 us
  waiting for transfers between devices  65.4 us (42%)
  starting transfers between devices  41.9 us (27%)
  Pallas kernels  34.9 us (23%)
  between operations  4.15 us (3%)
  local copies, waits for them, and re-layouts  3.34 us (2%)
  other arithmetic  3.2 us (2%)
    ppermute x6, waiting for transfers between devices, body(): lax.ppermute(states[i], 'dp', hop(s, 0) if p == 0 else hop(0, s))  24.3 us
    all_to_all x1, waiting for transfers between devices, body(): out = lax.all_to_all(out, 'dp', 0, 0, tiled=True)  18.7 us
    all_to_all x1, waiting for transfers between devices, body(): q_all = lax.all_to_all(q_all, 'dp', 0, 0, tiled=True)  18.3 us
    pallas_call x1, Pallas kernels, body(): pl.pallas_call(intra_kernel, grid=(heads // 4,), in_specs=[pl.BlockSpec((...  11.6 us
    all_to_all x1, starting transfers between devices, body(): out = lax.all_to_all(out, 'dp', 0, 0, tiled=True)  9.05 us
    ppermute x6, starting transfers between devices, body(): lax.ppermute(states[i], 'dp', hop(s, 0) if p == 0 else hop(0, s))  9.05 us
    ppermute x6, starting transfers between devices, body(): lax.ppermute(states[i], 'dp', hop(0, s) if p == 0 else hop(s, 0))  8.83 us
    all_to_all x1, starting transfers between devices, body(): q_all = lax.all_to_all(q_all, 'dp', 0, 0, tiled=True)  7.39 us
  transfers between devices with their start and end apart: 16, of which 7 were waited for; matrix products, arithmetic and copies ran while one was open for 2% of the time, Pallas kernels for 17%

profile of v6, /device:TPU:8, one launch (start us, length us, event | category | flops | bytes accessed | tf_op | source)
XLA Modules:
  0.0 152.9 jit_solution(11766242544162090680)
XLA Ops:
  1.9 2.7 %spread.1 = bf16[16,264,256]{2,1,0:T(8,128)(2,1)} custom-call(s32[1,2]{1,0:T(1,128)} %own_ref.1, s32[1,1]{1,0:T(1,128)S(6)} %copy.24.len_ref, f32[1,1]{1,0:T(1,128)S(6)} %copy.25.rew_ref, bf16[256,4096]{1,0:T(8,128)(2,1)} %bitcast.30), custom_call_target="tpu_custom_call" | custom-call | tf_op jit(solution)/shard_map/spread/pallas_call | solution.py:219
  4.6 7.4 %all-to-all-start = ((bf16[16,264,256]{2,1,0:T(8,128)(2,1)}), bf16[16,264,256]{2,1,0:T(8,128)(2,1)S(1)}, u32[]{:S(2)}, u32[]{:S(2)}) async-start(bf16[16,264,256]{2,1,0:T(8,128)(2,1)} %spread.1), calls=%async_computation | async-start | bytes 4325376 | tf_op jit(solution)/shard_map/all_to_all | solution.py:232
  12.0 11.6 %intra.1 = bf16[16,264,256]{2,1,0:T(8,128)(2,1)} custom-call(bf16[256,4096]{1,0:T(8,128)(2,1)} %bitcast.31, bf16[256,4096]{1,0:T(8,128)(2,1)} %bitcast.33, bf16[256,4096]{1,0:T(8,128)(2,1)} %bitcast.34, bf16[32,128,128]{2,1,0:T(8,128)(2,1)} %w_ref.2, bf16[32,128,128]{2,1,0:T(8,128)(2,1)} %w_ref.3), custom_call_target="tpu_custom_call" | custom-call | tf_op jit(solution)/shard_map/intra/pallas_call | solution.py:269
  23.6 18.3 %all-to-all-done.q_ref = bf16[16,264,256]{2,1,0:T(8,128)(2,1)S(1)} async-done(((bf16[16,264,256]{2,1,0:T(8,128)(2,1)}), bf16[16,264,256]{2,1,0:T(8,128)(2,1)S(1)}, u32[]{:S(2)}, u32[]{:S(2)}) %all-to-all-start) | async-done | bytes 2162720 | tf_op jit(solution)/shard_map/all_to_all | solution.py:232
  41.9 5.6 %all-to-all-start.1 = ((bf16[16,264,256]{2,1,0:T(8,128)(2,1)}), bf16[16,264,256]{2,1,0:T(8,128)(2,1)}, u32[]{:S(2)}, u32[]{:S(2)}) async-start(bf16[16,264,256]{2,1,0:T(8,128)(2,1)} %intra.1), calls=%async_computation.1 | async-start | bytes 4325376 | tf_op jit(solution)/shard_map/all_to_all | solution.py:278
  48.1 6.2 %state.1 = (bf16[4,264,128]{2,1,0:T(8,128)(2,1)}, bf16[4,264,128]{2,1,0:T(8,128)(2,1)}, bf16[4,264,128]{2,1,0:T(8,128)(2,1)}, bf16[4,264,128]{2,1,0:T(8,128)(2,1...) custom-call(s32[1]{0:T(128)S(6)} %copy.23.n_ref, ...), custom_call_target="tpu_custom_call" | custom-call | tf_op jit(solution)/shard_map/state/pallas_call | solution.py:239
  54.3 1.5 collective-permute-start.1
  55.8 2.7 %collective-permute-start.2 = (bf16[4,264,128]{2,1,0:T(8,128)(2,1)}, bf16[4,264,128]{2,1,0:T(8,128)(2,1)S(1)}, u32[]{:S(2)}, u32[]{:S(2)}) collective-permute-start(bf16[4,264,128]{2,1,0:T(8,128)(2,1)} %get-tuple-element.20), channel_id=1, source_target_pairs={{0,8},{1,9},{2,10},{3,11},{4,12},{5,13},{6,14},{7,15},{8,0},{9,1},... | collective-permute-start | bytes 811016 | tf_op jit(solution)/shard_map/ppermute | solution.py:256
  58.5 1.4 collective-permute-start.3
  60.0 1.5 collective-permute-start.4
  61.4 1.2 collective-permute-start.5
  62.6 18.4 %collective-permute-done.1.refs_1_ = bf16[4,264,128]{2,1,0:T(8,128)(2,1)S(1)} collective-permute-done((bf16[4,264,128]{2,1,0:T(8,128)(2,1)}, bf16[4,264,128]{2,1,0:T(8,128)(2,1)S(1)}, u32[]{:S(2)}, u32[]{:S(2)}) %collective-permute-start.1) | collective-permute-done | bytes 270368 | tf_op jit(solution)/shard_map/ppermute | solution.py:256
  81.0 0.8 collective-permute-start.6
  81.7 2.6 %collective-permute-done.2.refs_2_ = bf16[4,264,128]{2,1,0:T(8,128)(2,1)S(1)} collective-permute-done((bf16[4,264,128]{2,1,0:T(8,128)(2,1)}, bf16[4,264,128]{2,1,0:T(8,128)(2,1)S(1)}, u32[]{:S(2)}, u32[]{:S(2)}) %collective-permute-start.2) | collective-permute-done | bytes 270368 | tf_op jit(solution)/shard_map/ppermute | solution.py:256
  84.4 0.0 collective-permute-done.3.refs_3_
  84.4 0.0 collective-permute-done.4.refs_5_
  84.4 0.0 copy-start.4
  84.4 0.0 collective-permute-done.5.refs_6_
  84.4 0.0 copy-start.5
  84.4 3.3 %collective-permute-done.6.refs_7_ = bf16[4,264,128]{2,1,0:T(8,128)(2,1)} collective-permute-done((bf16[4,264,128]{2,1,0:T(8,128)(2,1)}, bf16[4,264,128]{2,1,0:T(8,128)(2,1)}, u32[]{:S(2)}, u32[]{:S(2)}) %collective-permute-start.6) | collective-permute-done | bytes 270368 | tf_op jit(solution)/shard_map/ppermute | solution.py:256
  87.8 0.0 copy-done.1
  87.8 0.0 copy-done.2
  87.8 0.0 copy-done.3
  87.8 0.0 copy-done.4
  87.8 0.0 copy-done.5
  87.8 2.5 %add.93 = (bf16[264,128]{1,0:T(8,128)(2,1)}, bf16[264,128]{1,0:T(8,128)(2,1)}, bf16[264,128]{1,0:T(8,128)(2,1)}, bf16[264,128]{1,0:T(8,128)(2,1)}, bf16[264,128]...) custom-call(bf16[4,264,128]{2,1,0:T(8,128)(2,1)} %get-tuple-element.18.refs_0_, ...), custom_call_target="tpu_custom_call" | custom-call | tf_op jit(solution)/shard_map/add/pallas_call | solution.py:257
  90.3 0.9 collective-permute-start.7
  91.2 2.0 %collective-permute-start.8 = (bf16[264,128]{1,0:T(8,128)(2,1)}, bf16[264,128]{1,0:T(8,128)(2,1)S(1)}, u32[]{:S(2)}, u32[]{:S(2)}) collective-permute-start(bf16[264,128]{1,0:T(8,128)(2,1)} %get-tuple-element.28), channel_id=1, source_target_pairs={{0,2},{1,3},{2,0},{3,1},{4,6},{5,7},{6,4},{7,5},{8,10},{9,11},{10,... | collective-permute-start | bytes 202760 | tf_op jit(solution)/shard_map/ppermute | solution.py:267
  93.2 2.5 %collective-permute-start.9 = (bf16[264,128]{1,0:T(8,128)(2,1)}, bf16[264,128]{1,0:T(8,128)(2,1)S(1)}, u32[]{:S(2)}, u32[]{:S(2)}) collective-permute-start(bf16[264,128]{1,0:T(8,128)(2,1)} %get-tuple-element.29), channel_id=1, source_target_pairs={{0,3},{1,0},{2,1},{3,2},{4,7},{5,4},{6,5},{7,6},{8,11},{9,8},{10,9... | collective-permute-start | bytes 202760 | tf_op jit(solution)/shard_map/ppermute | solution.py:267
  95.7 0.0 collective-permute-start.10
  95.7 2.2 %collective-permute-start.11 = (bf16[264,128]{1,0:T(8,128)(2,1)}, bf16[264,128]{1,0:T(8,128)(2,1)S(1)}, u32[]{:S(2)}, u32[]{:S(2)}) collective-permute-start(bf16[264,128]{1,0:T(8,128)(2,1)} %get-tuple-element.32), channel_id=1, source_target_pairs={{0,8},{1,9},{2,10},{3,11},{4,12},{5,13},{6,14},{7,15},{8,0},{9,1},... | collective-permute-start | bytes 202760 | tf_op jit(solution)/shard_map/ppermute | solution.py:267
  97.9 0.0 copy-done
  98.0 0.6 reshape.151.ids_ref
  98.6 0.7 fusion.3
  99.9 5.3 %phi.1.phi_ref = bf16[2,2048,256]{2,1,0:T(8,128)(2,1)} custom-call(s32[32]{0:T(128)} %reshape.151.ids_ref, bf16[16,264,256]{2,1,0:T(8,128)(2,1)} %copy-done, bf16[32,128,128]{2,1,0:T(8,128)(2,1)} %w_ref.2), custom_call_target="tpu_custom_call" | custom-call | tf_op jit(solution)/shard_map/phi/pallas_call | solution.py:290
  105.2 0.6 multiply_reduce_fusion
  105.7 0.0 collective-permute-done.7.refs_1_
  105.7 1.2 collective-permute-start.12
  107.0 0.7 fusion.1.len_ref
  107.7 0.0 collective-permute-done.8.refs_2_
  107.7 1.9 %collective-permute-start = (f32[1,1]{1,0:T(1,128)}, f32[1,1]{1,0:T(1,128)}, u32[]{:S(2)}, u32[]{:S(2)}) collective-permute-start(f32[1,1]{1,0:T(1,128)} %bitcast.1), channel_id=1, source_target_pairs={{0,0},{1,17},{2,34},{3,51},{4,68},{5,85},{6,102},{7,119},{8,136},{... | collective-permute-start | bytes 20 | tf_op jit(solution)/shard_map/ppermute | solution.py:281
  109.6 0.0 collective-permute-done.9.refs_3_
  109.6 0.0 collective-permute-done.10.refs_5_
  109.6 0.0 collective-permute-done.11.refs_6_
  109.6 0.0 copy-start.10
  109.6 0.4 collective-permute-done.12.refs_7_
  110.0 0.0 all-to-all-done.1.part_ref
  110.0 3.7 %collective-permute-done.sq_ref = f32[1,1]{1,0:T(1,128)} collective-permute-done((f32[1,1]{1,0:T(1,128)}, f32[1,1]{1,0:T(1,128)}, u32[]{:S(2)}, u32[]{:S(2)}) %collective-permute-start) | collective-permute-done | bytes 36 | tf_op jit(solution)/shard_map/ppermute | solution.py:281
  113.8 0.0 copy-done.8
  113.8 0.0 copy-done.9
  113.8 0.0 copy-done.10
  113.8 0.0 copy-done.11
  113.8 6.7 %combine.1 = bf16[16,136,256]{2,1,0:T(8,128)(2,1)} custom-call(s32[32]{0:T(128)} %reshape.151.ids_ref, s32[16]{0:T(128)} %fusion.1.len_ref, f32[1,1]{1,0:T(1,128)} %collective-permute-done.sq_ref, bf16[16,264,256]{2,1,0:T(8,128)(2,1)} %all-to-all-done.1.part_ref, bf16[2,2048,256]{2,1,0:T(8,128)(2,1)} %phi.1.phi_ref, ...), custom_call_target="tpu_custom_call" | custom-call | tf_op jit(solution)/shard_map/combine/pallas_call | solution.py:302
  120.5 9.1 %all-to-all-start.2 = ((bf16[16,136,256]{2,1,0:T(8,128)(2,1)}), bf16[16,136,256]{2,1,0:T(8,128)(2,1)S(1)}, u32[]{:S(2)}, u32[]{:S(2)}) async-start(bf16[16,136,256]{2,1,0:T(8,128)(2,1)} %combine.1), calls=%async_computation.2 | async-start | bytes 2228224 | tf_op jit(solution)/shard_map/all_to_all | solution.py:321
  129.6 0.2 select_reduce_fusion.1
  129.8 18.7 %all-to-all-done.2 = bf16[16,136,256]{2,1,0:T(8,128)(2,1)S(1)} async-done(((bf16[16,136,256]{2,1,0:T(8,128)(2,1)}), bf16[16,136,256]{2,1,0:T(8,128)(2,1)S(1)}, u32[]{:S(2)}, u32[]{:S(2)}) %all-to-all-start.2) | async-done | bytes 1114144 | tf_op jit(solution)/shard_map/all_to_all | solution.py:321
  148.4 0.1 slice_bitcast_fusion
  148.5 0.7 copy.15
  149.2 1.3 copy.16
  150.6 0.7 fusion
  151.9 0.1 divide_reduce_fusion
  152.0 0.2 select_reduce_fusion
  152.2 0.1 compare_select_fusion
  152.3 0.6 select_n.47
  (23 shorter events, 0.1 us)
Async XLA Ops:
  4.6 37.2 %all-to-all-start = ((bf16[16,264,256]{2,1,0:T(8,128)(2,1)}), bf16[16,264,256]{2,1,0:T(8,128)(2,1)S(1)}, u32[]{:S(2)}, u32[]{:S(2)}) async-start(bf16[16,264,256]{2,1,0:T(8,128)(2,1)} %spread.1), calls=%async_computation | async-start | bytes 4325376 | tf_op jit(solution)/shard_map/all_to_all | solution.py:232
  41.9 56.1 %copy-start = (bf16[16,264,256]{2,1,0:T(8,128)(2,1)}, bf16[16,264,256]{2,1,0:T(8,128)(2,1)S(1)}, u32[]{:S(2)}) copy-start(bf16[16,264,256]{2,1,0:T(8,128)(2,1)S(1)} %all-to-all-done.q_ref) | copy-start | bytes 6488068
  41.9 68.2 %all-to-all-start.1 = ((bf16[16,264,256]{2,1,0:T(8,128)(2,1)}), bf16[16,264,256]{2,1,0:T(8,128)(2,1)}, u32[]{:S(2)}, u32[]{:S(2)}) async-start(bf16[16,264,256]{2,1,0:T(8,128)(2,1)} %intra.1), calls=%async_computation.1 | async-start | bytes 4325376 | tf_op jit(solution)/shard_map/all_to_all | solution.py:278
  54.3 26.7 %collective-permute-start.1 = (bf16[4,264,128]{2,1,0:T(8,128)(2,1)}, bf16[4,264,128]{2,1,0:T(8,128)(2,1)S(1)}, u32[]{:S(2)}, u32[]{:S(2)}) collective-permute-start(bf16[4,264,128]{2,1,0:T(8,128)(2,1)} %get-tuple-element.19), channel_id=1, source_target_pairs={{0,4},{1,5},{2,6},{3,7},{4,8},{5,9},{6,10},{7,11},{8,12},{9,13},{1... | collective-permute-start | bytes 811016 | tf_op jit(solution)/shard_map/ppermute | solution.py:256
  55.8 28.6 %collective-permute-start.2 = (bf16[4,264,128]{2,1,0:T(8,128)(2,1)}, bf16[4,264,128]{2,1,0:T(8,128)(2,1)S(1)}, u32[]{:S(2)}, u32[]{:S(2)}) collective-permute-start(bf16[4,264,128]{2,1,0:T(8,128)(2,1)} %get-tuple-element.20), channel_id=1, source_target_pairs={{0,8},{1,9},{2,10},{3,11},{4,12},{5,13},{6,14},{7,15},{8,0},{9,1},... | collective-permute-start | bytes 811016 | tf_op jit(solution)/shard_map/ppermute | solution.py:256
  58.5 25.8 %collective-permute-start.3 = (bf16[4,264,128]{2,1,0:T(8,128)(2,1)}, bf16[4,264,128]{2,1,0:T(8,128)(2,1)S(1)}, u32[]{:S(2)}, u32[]{:S(2)}) collective-permute-start(bf16[4,264,128]{2,1,0:T(8,128)(2,1)} %get-tuple-element.21), channel_id=1, source_target_pairs={{0,12},{1,13},{2,14},{3,15},{4,0},{5,1},{6,2},{7,3},{8,4},{9,5},{1... | collective-permute-start | bytes 811016 | tf_op jit(solution)/shard_map/ppermute | solution.py:256
  60.0 24.4 %collective-permute-start.4 = (bf16[4,264,128]{2,1,0:T(8,128)(2,1)}, bf16[4,264,128]{2,1,0:T(8,128)(2,1)S(1)}, u32[]{:S(2)}, u32[]{:S(2)}) collective-permute-start(bf16[4,264,128]{2,1,0:T(8,128)(2,1)} %get-tuple-element.23), channel_id=1, source_target_pairs={{0,1},{1,2},{2,3},{3,0},{4,5},{5,6},{6,7},{7,4},{8,9},{9,10},{10,1... | collective-permute-start | bytes 811016 | tf_op jit(solution)/shard_map/ppermute | solution.py:256
  61.4 23.0 %collective-permute-start.5 = (bf16[4,264,128]{2,1,0:T(8,128)(2,1)}, bf16[4,264,128]{2,1,0:T(8,128)(2,1)S(1)}, u32[]{:S(2)}, u32[]{:S(2)}) collective-permute-start(bf16[4,264,128]{2,1,0:T(8,128)(2,1)} %get-tuple-element.24), channel_id=1, source_target_pairs={{0,2},{1,3},{2,0},{3,1},{4,6},{5,7},{6,4},{7,5},{8,10},{9,11},{10,... | collective-permute-start | bytes 811016 | tf_op jit(solution)/shard_map/ppermute | solution.py:256
  81.0 6.8 %copy-start.1 = (bf16[4,264,128]{2,1,0:T(8,128)(2,1)}, bf16[4,264,128]{2,1,0:T(8,128)(2,1)S(1)}, u32[]{:S(2)}) copy-start(bf16[4,264,128]{2,1,0:T(8,128)(2,1)S(1)} %collective-permute-done.1.refs_1_) | copy-start | bytes 811012
  81.0 6.8 %collective-permute-start.6 = (bf16[4,264,128]{2,1,0:T(8,128)(2,1)}, bf16[4,264,128]{2,1,0:T(8,128)(2,1)}, u32[]{:S(2)}, u32[]{:S(2)}) collective-permute-start(bf16[4,264,128]{2,1,0:T(8,128)(2,1)} %get-tuple-element.25), channel_id=1, source_target_pairs={{0,3},{1,0},{2,1},{3,2},{4,7},{5,4},{6,5},{7,6},{8,11},{9,8},{10,9... | collective-permute-start | bytes 811016 | tf_op jit(solution)/shard_map/ppermute | solution.py:256
  84.4 3.4 %copy-start.2 = (bf16[4,264,128]{2,1,0:T(8,128)(2,1)}, bf16[4,264,128]{2,1,0:T(8,128)(2,1)S(1)}, u32[]{:S(2)}) copy-start(bf16[4,264,128]{2,1,0:T(8,128)(2,1)S(1)} %collective-permute-done.2.refs_2_) | copy-start | bytes 811012
  84.4 3.4 %copy-start.3 = (bf16[4,264,128]{2,1,0:T(8,128)(2,1)}, bf16[4,264,128]{2,1,0:T(8,128)(2,1)S(1)}, u32[]{:S(2)}) copy-start(bf16[4,264,128]{2,1,0:T(8,128)(2,1)S(1)} %collective-permute-done.3.refs_3_) | copy-start | bytes 811012
  84.4 3.4 %copy-start.4 = (bf16[4,264,128]{2,1,0:T(8,128)(2,1)}, bf16[4,264,128]{2,1,0:T(8,128)(2,1)S(1)}, u32[]{:S(2)}) copy-start(bf16[4,264,128]{2,1,0:T(8,128)(2,1)S(1)} %collective-permute-done.4.refs_5_) | copy-start | bytes 811012
  84.4 3.4 %copy-start.5 = (bf16[4,264,128]{2,1,0:T(8,128)(2,1)}, bf16[4,264,128]{2,1,0:T(8,128)(2,1)S(1)}, u32[]{:S(2)}) copy-start(bf16[4,264,128]{2,1,0:T(8,128)(2,1)S(1)} %collective-permute-done.5.refs_6_) | copy-start | bytes 811012
  90.3 15.4 %collective-permute-start.7 = (bf16[264,128]{1,0:T(8,128)(2,1)}, bf16[264,128]{1,0:T(8,128)(2,1)S(1)}, u32[]{:S(2)}, u32[]{:S(2)}) collective-permute-start(bf16[264,128]{1,0:T(8,128)(2,1)} %get-tuple-element.27), channel_id=1, source_target_pairs={{0,1},{1,2},{2,3},{3,0},{4,5},{5,6},{6,7},{7,4},{8,9},{9,10},{10,1... | collective-permute-start | bytes 202760 | tf_op jit(solution)/shard_map/ppermute | solution.py:267
  91.2 16.4 %collective-permute-start.8 = (bf16[264,128]{1,0:T(8,128)(2,1)}, bf16[264,128]{1,0:T(8,128)(2,1)S(1)}, u32[]{:S(2)}, u32[]{:S(2)}) collective-permute-start(bf16[264,128]{1,0:T(8,128)(2,1)} %get-tuple-element.28), channel_id=1, source_target_pairs={{0,2},{1,3},{2,0},{3,1},{4,6},{5,7},{6,4},{7,5},{8,10},{9,11},{10,... | collective-permute-start | bytes 202760 | tf_op jit(solution)/shard_map/ppermute | solution.py:267
  93.2 16.4 %collective-permute-start.9 = (bf16[264,128]{1,0:T(8,128)(2,1)}, bf16[264,128]{1,0:T(8,128)(2,1)S(1)}, u32[]{:S(2)}, u32[]{:S(2)}) collective-permute-start(bf16[264,128]{1,0:T(8,128)(2,1)} %get-tuple-element.29), channel_id=1, source_target_pairs={{0,3},{1,0},{2,1},{3,2},{4,7},{5,4},{6,5},{7,6},{8,11},{9,8},{10,9... | collective-permute-start | bytes 202760 | tf_op jit(solution)/shard_map/ppermute | solution.py:267
  95.7 13.9 %collective-permute-start.10 = (bf16[264,128]{1,0:T(8,128)(2,1)}, bf16[264,128]{1,0:T(8,128)(2,1)S(1)}, u32[]{:S(2)}, u32[]{:S(2)}) collective-permute-start(bf16[264,128]{1,0:T(8,128)(2,1)} %get-tuple-element.31), channel_id=1, source_target_pairs={{0,4},{1,5},{2,6},{3,7},{4,8},{5,9},{6,10},{7,11},{8,12},{9,13},{1... | collective-permute-start | bytes 202760 | tf_op jit(solution)/shard_map/ppermute | solution.py:267
  95.7 13.9 %collective-permute-start.11 = (bf16[264,128]{1,0:T(8,128)(2,1)}, bf16[264,128]{1,0:T(8,128)(2,1)S(1)}, u32[]{:S(2)}, u32[]{:S(2)}) collective-permute-start(bf16[264,128]{1,0:T(8,128)(2,1)} %get-tuple-element.32), channel_id=1, source_target_pairs={{0,8},{1,9},{2,10},{3,11},{4,12},{5,13},{6,14},{7,15},{8,0},{9,1},... | collective-permute-start | bytes 202760 | tf_op jit(solution)/shard_map/ppermute | solution.py:267
  99.9 5.8 %copy-start.14 = (bf16[264,128]{1,0:T(8,128)(2,1)S(1)}, bf16[264,128]{1,0:T(8,128)(2,1)}, u32[]{:S(2)}) copy-start(bf16[264,128]{1,0:T(8,128)(2,1)} %get-tuple-element.33) | copy-start | bytes 202756
  105.7 8.0 %copy-start.6 = (bf16[264,128]{1,0:T(8,128)(2,1)}, bf16[264,128]{1,0:T(8,128)(2,1)S(1)}, u32[]{:S(2)}) copy-start(bf16[264,128]{1,0:T(8,128)(2,1)S(1)} %collective-permute-done.7.refs_1_) | copy-start | bytes 202756
  105.7 4.3 %collective-permute-start.12 = (bf16[264,128]{1,0:T(8,128)(2,1)S(1)}, bf16[264,128]{1,0:T(8,128)(2,1)S(1)}, u32[]{:S(2)}, u32[]{:S(2)}) collective-permute-start(bf16[264,128]{1,0:T(8,128)(2,1)S(1)} %copy-done.14), channel_id=1, source_target_pairs={{0,12},{1,13},{2,14},{3,15},{4,0},{5,1},{6,2},{7,3},{8,4},{9,5},{1... | collective-permute-start | bytes 202760 | tf_op jit(solution)/shard_map/ppermute | solution.py:267
  107.7 6.1 %copy-start.7 = (bf16[264,128]{1,0:T(8,128)(2,1)}, bf16[264,128]{1,0:T(8,128)(2,1)S(1)}, u32[]{:S(2)}) copy-start(bf16[264,128]{1,0:T(8,128)(2,1)S(1)} %collective-permute-done.8.refs_2_) | copy-start | bytes 202756
  107.7 6.1 %collective-permute-start = (f32[1,1]{1,0:T(1,128)}, f32[1,1]{1,0:T(1,128)}, u32[]{:S(2)}, u32[]{:S(2)}) collective-permute-start(f32[1,1]{1,0:T(1,128)} %bitcast.1), channel_id=1, source_target_pairs={{0,0},{1,17},{2,34},{3,51},{4,68},{5,85},{6,102},{7,119},{8,136},{... | collective-permute-start | bytes 20 | tf_op jit(solution)/shard_map/ppermute | solution.py:281
  109.6 4.2 %copy-start.8 = (bf16[264,128]{1,0:T(8,128)(2,1)}, bf16[264,128]{1,0:T(8,128)(2,1)S(1)}, u32[]{:S(2)}) copy-start(bf16[264,128]{1,0:T(8,128)(2,1)S(1)} %collective-permute-done.9.refs_3_) | copy-start | bytes 202756
  109.6 4.2 %copy-start.9 = (bf16[264,128]{1,0:T(8,128)(2,1)}, bf16[264,128]{1,0:T(8,128)(2,1)S(1)}, u32[]{:S(2)}) copy-start(bf16[264,128]{1,0:T(8,128)(2,1)S(1)} %collective-permute-done.10.refs_5_) | copy-start | bytes 202756
  109.6 4.2 %copy-start.10 = (bf16[264,128]{1,0:T(8,128)(2,1)}, bf16[264,128]{1,0:T(8,128)(2,1)S(1)}, u32[]{:S(2)}) copy-start(bf16[264,128]{1,0:T(8,128)(2,1)S(1)} %collective-permute-done.11.refs_6_) | copy-start | bytes 202756
  110.0 3.8 %copy-start.11 = (bf16[264,128]{1,0:T(8,128)(2,1)}, bf16[264,128]{1,0:T(8,128)(2,1)S(1)}, u32[]{:S(2)}) copy-start(bf16[264,128]{1,0:T(8,128)(2,1)S(1)} %collective-permute-done.12.refs_7_) | copy-start | bytes 202756
  120.5 9.1 %copy-start.13 = (s32[1,2]{1,0:T(1,128)S(1)}, s32[1,2]{1,0:T(1,128)}, u32[]{:S(2)}) copy-start(s32[1,2]{1,0:T(1,128)} %own_ref.1) | copy-start | bytes 28
  120.5 9.1 %copy-start.12 = (s32[16]{0:T(128)S(1)}, s32[16]{0:T(128)}, u32[]{:S(2)}) copy-start(s32[16]{0:T(128)} %fusion.1.len_ref) | copy-start | bytes 196
  120.5 27.9 %all-to-all-start.2 = ((bf16[16,136,256]{2,1,0:T(8,128)(2,1)}), bf16[16,136,256]{2,1,0:T(8,128)(2,1)S(1)}, u32[]{:S(2)}, u32[]{:S(2)}) async-start(bf16[16,136,256]{2,1,0:T(8,128)(2,1)} %combine.1), calls=%async_computation.2 | async-start | bytes 2228224 | tf_op jit(solution)/shard_map/all_to_all | solution.py:321

commit v7 on v6

--- a/solution.py
+++ b/solution.py
@@ -268,10 +268,10 @@
 
     inner = pl.pallas_call(
         intra_kernel,
-        grid=(heads // 4,),
-        in_specs=[pl.BlockSpec((length, 4 * width), lambda o: (0, o))] * 3
-        + [pl.BlockSpec((4, width, feat), lambda o: (o, 0, 0))] * 2,
-        out_specs=pl.BlockSpec((2, tall, two), lambda o: (o, 0, 0)),
+        grid=(heads // 8,),
+        in_specs=[pl.BlockSpec((length, 8 * width), lambda o: (0, o))] * 3
+        + [pl.BlockSpec((8, width, feat), lambda o: (o, 0, 0))] * 2,
+        out_specs=pl.BlockSpec((4, tall, two), lambda o: (o, 0, 0)),
         out_shape=jax.ShapeDtypeStruct((dp, tall, two), BF16),
         name="intra",
     )(q, k, v, feat_q, feat_k)

time: 155 us -> 155 us (level)
  transfers between devices with their start and end apart: 16 -> 16, of which waited for: 7 -> 7; matrix products, arithmetic and copies ran while one was open for 2% -> 2% of each run, Pallas kernels for 17% -> 16%
where the time goes in v7:
time: 155 us; the launch traced here: 153 us
  waiting for transfers between devices  66.4 us (43%)
  starting transfers between devices  41.9 us (27%)
  Pallas kernels  33.9 us (22%)
  between operations  4.15 us (3%)
  local copies, waits for them, and re-layouts  3.34 us (2%)
  other arithmetic  3.2 us (2%)
    ppermute x6, waiting for transfers between devices, body(): lax.ppermute(states[i], 'dp', hop(s, 0) if p == 0 else hop(0, s))  24.3 us
    all_to_all x1, waiting for transfers between devices, body(): q_all = lax.all_to_all(q_all, 'dp', 0, 0, tiled=True)  19.3 us
    all_to_all x1, waiting for transfers between devices, body(): out = lax.all_to_all(out, 'dp', 0, 0, tiled=True)  18.7 us
    pallas_call x1, Pallas kernels, body(): pl.pallas_call(intra_kernel, grid=(heads // 8,), in_specs=[pl.BlockSpec((...  10.6 us
    all_to_all x1, starting transfers between devices, body(): out = lax.all_to_all(out, 'dp', 0, 0, tiled=True)  9.05 us
    ppermute x6, starting transfers between devices, body(): lax.ppermute(states[i], 'dp', hop(s, 0) if p == 0 else hop(0, s))  9.05 us
    ppermute x6, starting transfers between devices, body(): lax.ppermute(states[i], 'dp', hop(0, s) if p == 0 else hop(s, 0))  8.83 us
    all_to_all x1, starting transfers between devices, body(): q_all = lax.all_to_all(q_all, 'dp', 0, 0, tiled=True)  7.39 us
  transfers between devices with their start and end apart: 16, of which 7 were waited for; matrix products, arithmetic and copies ran while one was open for 2% of the time, Pallas kernels for 16%

profile of v7, /device:TPU:8, one launch (start us, length us, event | category | flops | bytes accessed | tf_op | source)
XLA Modules:
  0.0 152.9 jit_solution(11188992108330029659)
XLA Ops:
  1.9 2.7 %spread.1 = bf16[16,264,256]{2,1,0:T(8,128)(2,1)} custom-call(s32[1,2]{1,0:T(1,128)} %own_ref.1, s32[1,1]{1,0:T(1,128)S(6)} %copy.24.len_ref, f32[1,1]{1,0:T(1,128)S(6)} %copy.25.rew_ref, bf16[256,4096]{1,0:T(8,128)(2,1)} %bitcast.30), custom_call_target="tpu_custom_call" | custom-call | tf_op jit(solution)/shard_map/spread/pallas_call | solution.py:219
  4.6 7.4 %all-to-all-start = ((bf16[16,264,256]{2,1,0:T(8,128)(2,1)}), bf16[16,264,256]{2,1,0:T(8,128)(2,1)S(1)}, u32[]{:S(2)}, u32[]{:S(2)}) async-start(bf16[16,264,256]{2,1,0:T(8,128)(2,1)} %spread.1), calls=%async_computation | async-start | bytes 4325376 | tf_op jit(solution)/shard_map/all_to_all | solution.py:232
  12.0 10.6 %intra.1 = bf16[16,264,256]{2,1,0:T(8,128)(2,1)} custom-call(bf16[256,4096]{1,0:T(8,128)(2,1)} %bitcast.31, bf16[256,4096]{1,0:T(8,128)(2,1)} %bitcast.33, bf16[256,4096]{1,0:T(8,128)(2,1)} %bitcast.34, bf16[32,128,128]{2,1,0:T(8,128)(2,1)} %w_ref.2, bf16[32,128,128]{2,1,0:T(8,128)(2,1)} %w_ref.3), custom_call_target="tpu_custom_call" | custom-call | tf_op jit(solution)/shard_map/intra/pallas_call | solution.py:269
  22.6 19.3 %all-to-all-done.q_ref = bf16[16,264,256]{2,1,0:T(8,128)(2,1)S(1)} async-done(((bf16[16,264,256]{2,1,0:T(8,128)(2,1)}), bf16[16,264,256]{2,1,0:T(8,128)(2,1)S(1)}, u32[]{:S(2)}, u32[]{:S(2)}) %all-to-all-start) | async-done | bytes 2162720 | tf_op jit(solution)/shard_map/all_to_all | solution.py:232
  41.9 5.6 %all-to-all-start.1 = ((bf16[16,264,256]{2,1,0:T(8,128)(2,1)}), bf16[16,264,256]{2,1,0:T(8,128)(2,1)}, u32[]{:S(2)}, u32[]{:S(2)}) async-start(bf16[16,264,256]{2,1,0:T(8,128)(2,1)} %intra.1), calls=%async_computation.1 | async-start | bytes 4325376 | tf_op jit(solution)/shard_map/all_to_all | solution.py:278
  48.1 6.2 %state.1 = (bf16[4,264,128]{2,1,0:T(8,128)(2,1)}, bf16[4,264,128]{2,1,0:T(8,128)(2,1)}, bf16[4,264,128]{2,1,0:T(8,128)(2,1)}, bf16[4,264,128]{2,1,0:T(8,128)(2,1...) custom-call(s32[1]{0:T(128)S(6)} %copy.23.n_ref, ...), custom_call_target="tpu_custom_call" | custom-call | tf_op jit(solution)/shard_map/state/pallas_call | solution.py:239
  54.3 1.5 collective-permute-start.1
  55.8 2.7 %collective-permute-start.2 = (bf16[4,264,128]{2,1,0:T(8,128)(2,1)}, bf16[4,264,128]{2,1,0:T(8,128)(2,1)S(1)}, u32[]{:S(2)}, u32[]{:S(2)}) collective-permute-start(bf16[4,264,128]{2,1,0:T(8,128)(2,1)} %get-tuple-element.20), channel_id=1, source_target_pairs={{0,8},{1,9},{2,10},{3,11},{4,12},{5,13},{6,14},{7,15},{8,0},{9,1},... | collective-permute-start | bytes 811016 | tf_op jit(solution)/shard_map/ppermute | solution.py:256
  58.5 1.4 collective-permute-start.3
  60.0 1.5 collective-permute-start.4
  61.4 1.2 collective-permute-start.5
  62.6 18.4 %collective-permute-done.1.refs_1_ = bf16[4,264,128]{2,1,0:T(8,128)(2,1)S(1)} collective-permute-done((bf16[4,264,128]{2,1,0:T(8,128)(2,1)}, bf16[4,264,128]{2,1,0:T(8,128)(2,1)S(1)}, u32[]{:S(2)}, u32[]{:S(2)}) %collective-permute-start.1) | collective-permute-done | bytes 270368 | tf_op jit(solution)/shard_map/ppermute | solution.py:256
  81.0 0.8 collective-permute-start.6
  81.7 2.6 %collective-permute-done.2.refs_2_ = bf16[4,264,128]{2,1,0:T(8,128)(2,1)S(1)} collective-permute-done((bf16[4,264,128]{2,1,0:T(8,128)(2,1)}, bf16[4,264,128]{2,1,0:T(8,128)(2,1)S(1)}, u32[]{:S(2)}, u32[]{:S(2)}) %collective-permute-start.2) | collective-permute-done | bytes 270368 | tf_op jit(solution)/shard_map/ppermute | solution.py:256
  84.4 0.0 collective-permute-done.3.refs_3_
  84.4 0.0 collective-permute-done.4.refs_5_
  84.4 0.0 copy-start.4
  84.4 0.0 collective-permute-done.5.refs_6_
  84.4 0.0 copy-start.5
  84.4 3.3 %collective-permute-done.6.refs_7_ = bf16[4,264,128]{2,1,0:T(8,128)(2,1)} collective-permute-done((bf16[4,264,128]{2,1,0:T(8,128)(2,1)}, bf16[4,264,128]{2,1,0:T(8,128)(2,1)}, u32[]{:S(2)}, u32[]{:S(2)}) %collective-permute-start.6) | collective-permute-done | bytes 270368 | tf_op jit(solution)/shard_map/ppermute | solution.py:256
  87.8 0.0 copy-done.1
  87.8 0.0 copy-done.2
  87.8 0.0 copy-done.3
  87.8 0.0 copy-done.4
  87.8 0.0 copy-done.5
  87.8 2.5 %add.93 = (bf16[264,128]{1,0:T(8,128)(2,1)}, bf16[264,128]{1,0:T(8,128)(2,1)}, bf16[264,128]{1,0:T(8,128)(2,1)}, bf16[264,128]{1,0:T(8,128)(2,1)}, bf16[264,128]...) custom-call(bf16[4,264,128]{2,1,0:T(8,128)(2,1)} %get-tuple-element.18.refs_0_, ...), custom_call_target="tpu_custom_call" | custom-call | tf_op jit(solution)/shard_map/add/pallas_call | solution.py:257
  90.3 0.9 collective-permute-start.7
  91.2 2.0 %collective-permute-start.8 = (bf16[264,128]{1,0:T(8,128)(2,1)}, bf16[264,128]{1,0:T(8,128)(2,1)S(1)}, u32[]{:S(2)}, u32[]{:S(2)}) collective-permute-start(bf16[264,128]{1,0:T(8,128)(2,1)} %get-tuple-element.28), channel_id=1, source_target_pairs={{0,2},{1,3},{2,0},{3,1},{4,6},{5,7},{6,4},{7,5},{8,10},{9,11},{10,... | collective-permute-start | bytes 202760 | tf_op jit(solution)/shard_map/ppermute | solution.py:267
  93.2 2.5 %collective-permute-start.9 = (bf16[264,128]{1,0:T(8,128)(2,1)}, bf16[264,128]{1,0:T(8,128)(2,1)S(1)}, u32[]{:S(2)}, u32[]{:S(2)}) collective-permute-start(bf16[264,128]{1,0:T(8,128)(2,1)} %get-tuple-element.29), channel_id=1, source_target_pairs={{0,3},{1,0},{2,1},{3,2},{4,7},{5,4},{6,5},{7,6},{8,11},{9,8},{10,9... | collective-permute-start | bytes 202760 | tf_op jit(solution)/shard_map/ppermute | solution.py:267
  95.7 0.0 collective-permute-start.10
  95.7 2.2 %collective-permute-start.11 = (bf16[264,128]{1,0:T(8,128)(2,1)}, bf16[264,128]{1,0:T(8,128)(2,1)S(1)}, u32[]{:S(2)}, u32[]{:S(2)}) collective-permute-start(bf16[264,128]{1,0:T(8,128)(2,1)} %get-tuple-element.32), channel_id=1, source_target_pairs={{0,8},{1,9},{2,10},{3,11},{4,12},{5,13},{6,14},{7,15},{8,0},{9,1},... | collective-permute-start | bytes 202760 | tf_op jit(solution)/shard_map/ppermute | solution.py:267
  97.9 0.0 copy-done
  98.0 0.6 reshape.151.ids_ref
  98.6 0.7 fusion.3
  99.9 5.3 %phi.1.phi_ref = bf16[2,2048,256]{2,1,0:T(8,128)(2,1)} custom-call(s32[32]{0:T(128)} %reshape.151.ids_ref, bf16[16,264,256]{2,1,0:T(8,128)(2,1)} %copy-done, bf16[32,128,128]{2,1,0:T(8,128)(2,1)} %w_ref.2), custom_call_target="tpu_custom_call" | custom-call | tf_op jit(solution)/shard_map/phi/pallas_call | solution.py:290
  105.2 0.6 multiply_reduce_fusion
  105.7 0.0 collective-permute-done.7.refs_1_
  105.7 1.2 collective-permute-start.12
  107.0 0.7 fusion.1.len_ref
  107.7 0.0 collective-permute-done.8.refs_2_
  107.7 1.9 %collective-permute-start = (f32[1,1]{1,0:T(1,128)}, f32[1,1]{1,0:T(1,128)}, u32[]{:S(2)}, u32[]{:S(2)}) collective-permute-start(f32[1,1]{1,0:T(1,128)} %bitcast.1), channel_id=1, source_target_pairs={{0,0},{1,17},{2,34},{3,51},{4,68},{5,85},{6,102},{7,119},{8,136},{... | collective-permute-start | bytes 20 | tf_op jit(solution)/shard_map/ppermute | solution.py:281
  109.6 0.0 collective-permute-done.9.refs_3_
  109.6 0.0 collective-permute-done.10.refs_5_
  109.6 0.0 collective-permute-done.11.refs_6_
  109.6 0.0 copy-start.10
  109.6 0.4 collective-permute-done.12.refs_7_
  110.0 0.0 all-to-all-done.1.part_ref
  110.0 3.7 %collective-permute-done.sq_ref = f32[1,1]{1,0:T(1,128)} collective-permute-done((f32[1,1]{1,0:T(1,128)}, f32[1,1]{1,0:T(1,128)}, u32[]{:S(2)}, u32[]{:S(2)}) %collective-permute-start) | collective-permute-done | bytes 36 | tf_op jit(solution)/shard_map/ppermute | solution.py:281
  113.8 0.0 copy-done.8
  113.8 0.0 copy-done.9
  113.8 0.0 copy-done.10
  113.8 0.0 copy-done.11
  113.8 6.7 %combine.1 = bf16[16,136,256]{2,1,0:T(8,128)(2,1)} custom-call(s32[32]{0:T(128)} %reshape.151.ids_ref, s32[16]{0:T(128)} %fusion.1.len_ref, f32[1,1]{1,0:T(1,128)} %collective-permute-done.sq_ref, bf16[16,264,256]{2,1,0:T(8,128)(2,1)} %all-to-all-done.1.part_ref, bf16[2,2048,256]{2,1,0:T(8,128)(2,1)} %phi.1.phi_ref, ...), custom_call_target="tpu_custom_call" | custom-call | tf_op jit(solution)/shard_map/combine/pallas_call | solution.py:302
  120.5 9.1 %all-to-all-start.2 = ((bf16[16,136,256]{2,1,0:T(8,128)(2,1)}), bf16[16,136,256]{2,1,0:T(8,128)(2,1)S(1)}, u32[]{:S(2)}, u32[]{:S(2)}) async-start(bf16[16,136,256]{2,1,0:T(8,128)(2,1)} %combine.1), calls=%async_computation.2 | async-start | bytes 2228224 | tf_op jit(solution)/shard_map/all_to_all | solution.py:321
  129.6 0.2 select_reduce_fusion.1
  129.8 18.7 %all-to-all-done.2 = bf16[16,136,256]{2,1,0:T(8,128)(2,1)S(1)} async-done(((bf16[16,136,256]{2,1,0:T(8,128)(2,1)}), bf16[16,136,256]{2,1,0:T(8,128)(2,1)S(1)}, u32[]{:S(2)}, u32[]{:S(2)}) %all-to-all-start.2) | async-done | bytes 1114144 | tf_op jit(solution)/shard_map/all_to_all | solution.py:321
  148.4 0.1 slice_bitcast_fusion
  148.5 0.7 copy.15
  149.2 1.3 copy.16
  150.6 0.7 fusion
  151.9 0.1 divide_reduce_fusion
  152.0 0.2 select_reduce_fusion
  152.2 0.1 compare_select_fusion
  152.3 0.6 select_n.47
  (23 shorter events, 0.1 us)
Async XLA Ops:
  4.6 37.2 %all-to-all-start = ((bf16[16,264,256]{2,1,0:T(8,128)(2,1)}), bf16[16,264,256]{2,1,0:T(8,128)(2,1)S(1)}, u32[]{:S(2)}, u32[]{:S(2)}) async-start(bf16[16,264,256]{2,1,0:T(8,128)(2,1)} %spread.1), calls=%async_computation | async-start | bytes 4325376 | tf_op jit(solution)/shard_map/all_to_all | solution.py:232
  41.9 56.1 %copy-start = (bf16[16,264,256]{2,1,0:T(8,128)(2,1)}, bf16[16,264,256]{2,1,0:T(8,128)(2,1)S(1)}, u32[]{:S(2)}) copy-start(bf16[16,264,256]{2,1,0:T(8,128)(2,1)S(1)} %all-to-all-done.q_ref) | copy-start | bytes 6488068
  41.9 68.2 %all-to-all-start.1 = ((bf16[16,264,256]{2,1,0:T(8,128)(2,1)}), bf16[16,264,256]{2,1,0:T(8,128)(2,1)}, u32[]{:S(2)}, u32[]{:S(2)}) async-start(bf16[16,264,256]{2,1,0:T(8,128)(2,1)} %intra.1), calls=%async_computation.1 | async-start | bytes 4325376 | tf_op jit(solution)/shard_map/all_to_all | solution.py:278
  54.3 26.7 %collective-permute-start.1 = (bf16[4,264,128]{2,1,0:T(8,128)(2,1)}, bf16[4,264,128]{2,1,0:T(8,128)(2,1)S(1)}, u32[]{:S(2)}, u32[]{:S(2)}) collective-permute-start(bf16[4,264,128]{2,1,0:T(8,128)(2,1)} %get-tuple-element.19), channel_id=1, source_target_pairs={{0,4},{1,5},{2,6},{3,7},{4,8},{5,9},{6,10},{7,11},{8,12},{9,13},{1... | collective-permute-start | bytes 811016 | tf_op jit(solution)/shard_map/ppermute | solution.py:256
  55.8 28.6 %collective-permute-start.2 = (bf16[4,264,128]{2,1,0:T(8,128)(2,1)}, bf16[4,264,128]{2,1,0:T(8,128)(2,1)S(1)}, u32[]{:S(2)}, u32[]{:S(2)}) collective-permute-start(bf16[4,264,128]{2,1,0:T(8,128)(2,1)} %get-tuple-element.20), channel_id=1, source_target_pairs={{0,8},{1,9},{2,10},{3,11},{4,12},{5,13},{6,14},{7,15},{8,0},{9,1},... | collective-permute-start | bytes 811016 | tf_op jit(solution)/shard_map/ppermute | solution.py:256
  58.5 25.8 %collective-permute-start.3 = (bf16[4,264,128]{2,1,0:T(8,128)(2,1)}, bf16[4,264,128]{2,1,0:T(8,128)(2,1)S(1)}, u32[]{:S(2)}, u32[]{:S(2)}) collective-permute-start(bf16[4,264,128]{2,1,0:T(8,128)(2,1)} %get-tuple-element.21), channel_id=1, source_target_pairs={{0,12},{1,13},{2,14},{3,15},{4,0},{5,1},{6,2},{7,3},{8,4},{9,5},{1... | collective-permute-start | bytes 811016 | tf_op jit(solution)/shard_map/ppermute | solution.py:256
  60.0 24.4 %collective-permute-start.4 = (bf16[4,264,128]{2,1,0:T(8,128)(2,1)}, bf16[4,264,128]{2,1,0:T(8,128)(2,1)S(1)}, u32[]{:S(2)}, u32[]{:S(2)}) collective-permute-start(bf16[4,264,128]{2,1,0:T(8,128)(2,1)} %get-tuple-element.23), channel_id=1, source_target_pairs={{0,1},{1,2},{2,3},{3,0},{4,5},{5,6},{6,7},{7,4},{8,9},{9,10},{10,1... | collective-permute-start | bytes 811016 | tf_op jit(solution)/shard_map/ppermute | solution.py:256
  61.4 23.0 %collective-permute-start.5 = (bf16[4,264,128]{2,1,0:T(8,128)(2,1)}, bf16[4,264,128]{2,1,0:T(8,128)(2,1)S(1)}, u32[]{:S(2)}, u32[]{:S(2)}) collective-permute-start(bf16[4,264,128]{2,1,0:T(8,128)(2,1)} %get-tuple-element.24), channel_id=1, source_target_pairs={{0,2},{1,3},{2,0},{3,1},{4,6},{5,7},{6,4},{7,5},{8,10},{9,11},{10,... | collective-permute-start | bytes 811016 | tf_op jit(solution)/shard_map/ppermute | solution.py:256
  81.0 6.8 %copy-start.1 = (bf16[4,264,128]{2,1,0:T(8,128)(2,1)}, bf16[4,264,128]{2,1,0:T(8,128)(2,1)S(1)}, u32[]{:S(2)}) copy-start(bf16[4,264,128]{2,1,0:T(8,128)(2,1)S(1)} %collective-permute-done.1.refs_1_) | copy-start | bytes 811012
  81.0 6.8 %collective-permute-start.6 = (bf16[4,264,128]{2,1,0:T(8,128)(2,1)}, bf16[4,264,128]{2,1,0:T(8,128)(2,1)}, u32[]{:S(2)}, u32[]{:S(2)}) collective-permute-start(bf16[4,264,128]{2,1,0:T(8,128)(2,1)} %get-tuple-element.25), channel_id=1, source_target_pairs={{0,3},{1,0},{2,1},{3,2},{4,7},{5,4},{6,5},{7,6},{8,11},{9,8},{10,9... | collective-permute-start | bytes 811016 | tf_op jit(solution)/shard_map/ppermute | solution.py:256
  84.4 3.4 %copy-start.2 = (bf16[4,264,128]{2,1,0:T(8,128)(2,1)}, bf16[4,264,128]{2,1,0:T(8,128)(2,1)S(1)}, u32[]{:S(2)}) copy-start(bf16[4,264,128]{2,1,0:T(8,128)(2,1)S(1)} %collective-permute-done.2.refs_2_) | copy-start | bytes 811012
  84.4 3.4 %copy-start.3 = (bf16[4,264,128]{2,1,0:T(8,128)(2,1)}, bf16[4,264,128]{2,1,0:T(8,128)(2,1)S(1)}, u32[]{:S(2)}) copy-start(bf16[4,264,128]{2,1,0:T(8,128)(2,1)S(1)} %collective-permute-done.3.refs_3_) | copy-start | bytes 811012
  84.4 3.4 %copy-start.4 = (bf16[4,264,128]{2,1,0:T(8,128)(2,1)}, bf16[4,264,128]{2,1,0:T(8,128)(2,1)S(1)}, u32[]{:S(2)}) copy-start(bf16[4,264,128]{2,1,0:T(8,128)(2,1)S(1)} %collective-permute-done.4.refs_5_) | copy-start | bytes 811012
  84.4 3.4 %copy-start.5 = (bf16[4,264,128]{2,1,0:T(8,128)(2,1)}, bf16[4,264,128]{2,1,0:T(8,128)(2,1)S(1)}, u32[]{:S(2)}) copy-start(bf16[4,264,128]{2,1,0:T(8,128)(2,1)S(1)} %collective-permute-done.5.refs_6_) | copy-start | bytes 811012
  90.3 15.4 %collective-permute-start.7 = (bf16[264,128]{1,0:T(8,128)(2,1)}, bf16[264,128]{1,0:T(8,128)(2,1)S(1)}, u32[]{:S(2)}, u32[]{:S(2)}) collective-permute-start(bf16[264,128]{1,0:T(8,128)(2,1)} %get-tuple-element.27), channel_id=1, source_target_pairs={{0,1},{1,2},{2,3},{3,0},{4,5},{5,6},{6,7},{7,4},{8,9},{9,10},{10,1... | collective-permute-start | bytes 202760 | tf_op jit(solution)/shard_map/ppermute | solution.py:267
  91.2 16.4 %collective-permute-start.8 = (bf16[264,128]{1,0:T(8,128)(2,1)}, bf16[264,128]{1,0:T(8,128)(2,1)S(1)}, u32[]{:S(2)}, u32[]{:S(2)}) collective-permute-start(bf16[264,128]{1,0:T(8,128)(2,1)} %get-tuple-element.28), channel_id=1, source_target_pairs={{0,2},{1,3},{2,0},{3,1},{4,6},{5,7},{6,4},{7,5},{8,10},{9,11},{10,... | collective-permute-start | bytes 202760 | tf_op jit(solution)/shard_map/ppermute | solution.py:267
  93.2 16.4 %collective-permute-start.9 = (bf16[264,128]{1,0:T(8,128)(2,1)}, bf16[264,128]{1,0:T(8,128)(2,1)S(1)}, u32[]{:S(2)}, u32[]{:S(2)}) collective-permute-start(bf16[264,128]{1,0:T(8,128)(2,1)} %get-tuple-element.29), channel_id=1, source_target_pairs={{0,3},{1,0},{2,1},{3,2},{4,7},{5,4},{6,5},{7,6},{8,11},{9,8},{10,9... | collective-permute-start | bytes 202760 | tf_op jit(solution)/shard_map/ppermute | solution.py:267
  95.7 13.9 %collective-permute-start.10 = (bf16[264,128]{1,0:T(8,128)(2,1)}, bf16[264,128]{1,0:T(8,128)(2,1)S(1)}, u32[]{:S(2)}, u32[]{:S(2)}) collective-permute-start(bf16[264,128]{1,0:T(8,128)(2,1)} %get-tuple-element.31), channel_id=1, source_target_pairs={{0,4},{1,5},{2,6},{3,7},{4,8},{5,9},{6,10},{7,11},{8,12},{9,13},{1... | collective-permute-start | bytes 202760 | tf_op jit(solution)/shard_map/ppermute | solution.py:267
  95.7 13.9 %collective-permute-start.11 = (bf16[264,128]{1,0:T(8,128)(2,1)}, bf16[264,128]{1,0:T(8,128)(2,1)S(1)}, u32[]{:S(2)}, u32[]{:S(2)}) collective-permute-start(bf16[264,128]{1,0:T(8,128)(2,1)} %get-tuple-element.32), channel_id=1, source_target_pairs={{0,8},{1,9},{2,10},{3,11},{4,12},{5,13},{6,14},{7,15},{8,0},{9,1},... | collective-permute-start | bytes 202760 | tf_op jit(solution)/shard_map/ppermute | solution.py:267
  99.9 5.8 %copy-start.14 = (bf16[264,128]{1,0:T(8,128)(2,1)S(1)}, bf16[264,128]{1,0:T(8,128)(2,1)}, u32[]{:S(2)}) copy-start(bf16[264,128]{1,0:T(8,128)(2,1)} %get-tuple-element.33) | copy-start | bytes 202756
  105.7 8.0 %copy-start.6 = (bf16[264,128]{1,0:T(8,128)(2,1)}, bf16[264,128]{1,0:T(8,128)(2,1)S(1)}, u32[]{:S(2)}) copy-start(bf16[264,128]{1,0:T(8,128)(2,1)S(1)} %collective-permute-done.7.refs_1_) | copy-start | bytes 202756
  105.7 4.3 %collective-permute-start.12 = (bf16[264,128]{1,0:T(8,128)(2,1)S(1)}, bf16[264,128]{1,0:T(8,128)(2,1)S(1)}, u32[]{:S(2)}, u32[]{:S(2)}) collective-permute-start(bf16[264,128]{1,0:T(8,128)(2,1)S(1)} %copy-done.14), channel_id=1, source_target_pairs={{0,12},{1,13},{2,14},{3,15},{4,0},{5,1},{6,2},{7,3},{8,4},{9,5},{1... | collective-permute-start | bytes 202760 | tf_op jit(solution)/shard_map/ppermute | solution.py:267
  107.7 6.1 %copy-start.7 = (bf16[264,128]{1,0:T(8,128)(2,1)}, bf16[264,128]{1,0:T(8,128)(2,1)S(1)}, u32[]{:S(2)}) copy-start(bf16[264,128]{1,0:T(8,128)(2,1)S(1)} %collective-permute-done.8.refs_2_) | copy-start | bytes 202756
  107.7 6.1 %collective-permute-start = (f32[1,1]{1,0:T(1,128)}, f32[1,1]{1,0:T(1,128)}, u32[]{:S(2)}, u32[]{:S(2)}) collective-permute-start(f32[1,1]{1,0:T(1,128)} %bitcast.1), channel_id=1, source_target_pairs={{0,0},{1,17},{2,34},{3,51},{4,68},{5,85},{6,102},{7,119},{8,136},{... | collective-permute-start | bytes 20 | tf_op jit(solution)/shard_map/ppermute | solution.py:281
  109.6 4.2 %copy-start.8 = (bf16[264,128]{1,0:T(8,128)(2,1)}, bf16[264,128]{1,0:T(8,128)(2,1)S(1)}, u32[]{:S(2)}) copy-start(bf16[264,128]{1,0:T(8,128)(2,1)S(1)} %collective-permute-done.9.refs_3_) | copy-start | bytes 202756
  109.6 4.2 %copy-start.9 = (bf16[264,128]{1,0:T(8,128)(2,1)}, bf16[264,128]{1,0:T(8,128)(2,1)S(1)}, u32[]{:S(2)}) copy-start(bf16[264,128]{1,0:T(8,128)(2,1)S(1)} %collective-permute-done.10.refs_5_) | copy-start | bytes 202756
  109.6 4.2 %copy-start.10 = (bf16[264,128]{1,0:T(8,128)(2,1)}, bf16[264,128]{1,0:T(8,128)(2,1)S(1)}, u32[]{:S(2)}) copy-start(bf16[264,128]{1,0:T(8,128)(2,1)S(1)} %collective-permute-done.11.refs_6_) | copy-start | bytes 202756
  110.0 3.8 %copy-start.11 = (bf16[264,128]{1,0:T(8,128)(2,1)}, bf16[264,128]{1,0:T(8,128)(2,1)S(1)}, u32[]{:S(2)}) copy-start(bf16[264,128]{1,0:T(8,128)(2,1)S(1)} %collective-permute-done.12.refs_7_) | copy-start | bytes 202756
  120.5 9.1 %copy-start.13 = (s32[1,2]{1,0:T(1,128)S(1)}, s32[1,2]{1,0:T(1,128)}, u32[]{:S(2)}) copy-start(s32[1,2]{1,0:T(1,128)} %own_ref.1) | copy-start | bytes 28
  120.5 9.1 %copy-start.12 = (s32[16]{0:T(128)S(1)}, s32[16]{0:T(128)}, u32[]{:S(2)}) copy-start(s32[16]{0:T(128)} %fusion.1.len_ref) | copy-start | bytes 196
  120.5 27.9 %all-to-all-start.2 = ((bf16[16,136,256]{2,1,0:T(8,128)(2,1)}), bf16[16,136,256]{2,1,0:T(8,128)(2,1)S(1)}, u32[]{:S(2)}, u32[]{:S(2)}) async-start(bf16[16,136,256]{2,1,0:T(8,128)(2,1)} %combine.1), calls=%async_computation.2 | async-start | bytes 2228224 | tf_op jit(solution)/shard_map/all_to_all | solution.py:321
